TPU v7x, 256 devices: a 4x2x16 block of a 4x16x16 slice. The times are simulated.
256 devices in a mesh: group: 2 (over y), expert: 32 (over z, core), tensor: 4 (over x).
Axes of the slice: x: 4, y: 2, z: 16, core: 2. Of those that a mesh axis runs over, the one named last changes fastest.
The devices are a block of a 4x16x16 slice.
Arguments:
- tokens: bfloat16 [16384, 4096], P(('group', 'expert', 'tensor')), parts along dimension 0, may hold values from -6 to 6
- cotangent: bfloat16 [16384, 4096], P(('group', 'expert', 'tensor')), parts along dimension 0, may hold values from -6 to 6
- expert_ids: int32 [16384, 2], P(('group', 'expert', 'tensor')), parts along dimension 0, may hold values from 0 to 31, all different within a row
- gate_wts: float32 [16384, 2], P(('group', 'expert', 'tensor')), parts along dimension 0, may hold values from 0.2 to 1
- w_gate: bfloat16 [32, 4096, 256], P('expert', 'tensor'), may hold values from -0.09375 to 0.09375
- w_up: bfloat16 [32, 4096, 256], P('expert', 'tensor'), may hold values from -0.09375 to 0.09375
- w_down: bfloat16 [32, 256, 4096], P('expert', 'tensor'), may hold values from -0.375 to 0.375
Outputs:
- input_grad: bfloat16 [16384, 4096], P(('group', 'expert', 'tensor')), parts along dimension 0
- grad_gate: bfloat16 [64, 4096, 256], P(('group', 'expert'), 'tensor'), parts along dimension 0
- grad_up: bfloat16 [64, 4096, 256], P(('group', 'expert'), 'tensor'), parts along dimension 0
- grad_down: bfloat16 [64, 256, 4096], P(('group', 'expert'), 'tensor'), parts along dimension 0
There are 2 independent parts, one for each index of `group`. A program takes and returns all parts, laid end to end along the dimension named above; an argument that names none is the same for every part. Nothing has to cross between parts.
Inputs may be any that keep to these rules, and one draw needn't show every extreme that they name: `expert_ids`: the two ids of a token differ.
All inputs are finite; a program needn't handle non-finite values.
Results may differ from a plain program's by a relative error of at most 0.009.
Values may be sent and summed in bfloat16 or wider, within the bound.
No kernel may reach another device: no remote copies, remote signals or barrier semaphores. Data moves between devices by JAX's collectives and lax.ppermute only.
A program may use at most 64 MiB of HBM per device.

v0:
```python
import jax
import jax.numpy as jnp
from jax import lax
from jax.sharding import PartitionSpec as P


def contract_last(left, right):
    return lax.dot_general(
        left, right, (((1,), (1,)), ((), ())), preferred_element_type=jnp.float32
    )


def contract_first(left, right):
    return lax.dot_general(
        left, right, (((0,), (0,)), ((), ())), preferred_element_type=jnp.float32
    )


def local(tokens, cotangent, expert_ids, gate_wts, w_gate, w_up, w_down):
    tok_rows, model_width = tokens.shape
    experts = lax.axis_size("expert")
    capacity = 2 * tok_rows // experts
    slots_all = experts * capacity
    zero_half = jnp.zeros((), jnp.bfloat16)
    flat_ids = expert_ids.reshape(-1)
    onehot = (flat_ids[:, None] == jnp.arange(experts, dtype=jnp.int32)[None, :]).astype(jnp.int32)
    positions = jnp.sum(onehot * (jnp.cumsum(onehot, axis=0) - 1), axis=1)
    retained = positions < capacity
    target = jnp.where(retained, flat_ids * capacity + positions, slots_all)
    anchor = (
        jnp.full((slots_all,), -1, jnp.int32)
        .at[target]
        .set(jnp.arange(2 * tok_rows, dtype=jnp.int32), mode="drop")
    )
    populated_rows = anchor >= 0
    picked = jnp.maximum(anchor, 0)
    tok_index = picked // 2
    send_rows = jnp.where(populated_rows[:, None], tokens[tok_index], zero_half)
    gate_scale = gate_wts.reshape(-1)[picked]
    scaled = (gate_scale[:, None] * cotangent[tok_index].astype(jnp.float32)).astype(jnp.bfloat16)
    send_cot = jnp.where(populated_rows[:, None], scaled, zero_half)
    recv_rows, recv_cot = (
        lax.all_to_all(
            send_rows.reshape(experts, capacity, model_width),
            "expert",
            split_axis=0,
            concat_axis=0,
            tiled=True,
        ),
        lax.all_to_all(
            send_cot.reshape(experts, capacity, model_width),
            "expert",
            split_axis=0,
            concat_axis=0,
            tiled=True,
        ),
    )
    rows_in = recv_rows.reshape(slots_all, model_width)
    cot_in = recv_cot.reshape(slots_all, model_width)
    gate_shard = w_gate[0]
    up_shard = w_up[0]
    down_shard = w_down[0]
    hidden_width = gate_shard.shape[1]
    full_gate, full_up, complete_down_weight = (
        lax.all_gather(gate_shard, "tensor", axis=0, tiled=True),
        lax.all_gather(up_shard, "tensor", axis=0, tiled=True),
        lax.all_gather(down_shard, "tensor", axis=0, tiled=True),
    )
    pre_gate = jnp.dot(rows_in, full_gate, preferred_element_type=jnp.float32)
    pre_up = jnp.dot(rows_in, full_up, preferred_element_type=jnp.float32)
    grad_hidden = contract_last(cot_in, complete_down_weight)
    sigmoid_gate = jax.nn.sigmoid(pre_gate)
    activated = pre_gate * sigmoid_gate
    hidden = (activated * pre_up).astype(jnp.bfloat16)
    grad_gate_pre = (
        grad_hidden * pre_up * sigmoid_gate * (1.0 + pre_gate * (1.0 - sigmoid_gate))
    ).astype(jnp.bfloat16)
    grad_up_pre = (grad_hidden * activated).astype(jnp.bfloat16)
    joint_grad = jnp.concatenate([grad_gate_pre, grad_up_pre], axis=1)
    columns = rows_in
    summed = lax.psum_scatter(
        contract_first(columns, joint_grad).astype(jnp.bfloat16),
        "tensor",
        scatter_dimension=0,
        tiled=True,
    ).astype(jnp.float32)
    columns = hidden
    summed_down = lax.psum_scatter(
        contract_first(columns, cot_in).astype(jnp.bfloat16),
        "tensor",
        scatter_dimension=0,
        tiled=True,
    )
    rows_out = (
        contract_last(grad_gate_pre, full_gate) + contract_last(grad_up_pre, full_up)
    ).astype(jnp.bfloat16)
    returned = lax.all_to_all(
        rows_out.reshape(experts, capacity, model_width),
        "expert",
        split_axis=0,
        concat_axis=0,
        tiled=True,
    )
    returned = returned.reshape(slots_all, model_width)
    gathered = returned[jnp.minimum(target, slots_all - 1)].astype(jnp.float32)
    gathered = jnp.where(retained[:, None], gathered, jnp.zeros((), jnp.float32))
    input_grad = jnp.sum(gathered.reshape(tok_rows, 2, model_width), axis=1).astype(jnp.bfloat16)
    return (
        input_grad,
        summed[:, :hidden_width].astype(jnp.bfloat16)[None],
        summed[:, hidden_width:].astype(jnp.bfloat16)[None],
        summed_down[None],
    )


def solution(mesh):
    return jax.shard_map(
        local,
        mesh=mesh,
        in_specs=(
            P(("group", "expert", "tensor"), None),
            P(("group", "expert", "tensor"), None),
            P(("group", "expert", "tensor"), None),
            P(("group", "expert", "tensor"), None),
            P("expert", "tensor", None),
            P("expert", "tensor", None),
            P("expert", "tensor", None),
        ),
        out_specs=(
            P(("group", "expert", "tensor"), None),
            P(("group", "expert"), "tensor", None),
            P(("group", "expert"), "tensor", None),
            P(("group", "expert"), "tensor", None),
        ),
        check_vma=False,
    )
```

profile of v0, /device:TPU:33, one launch (start us, length us, event | category | flops | bytes accessed | tf_op | source)
XLA Modules:
  0.0 268.5 jit_solution(17114819456044467848)
XLA Ops:
  7.3 0.7 all-gather.11.cloned.1.call-update
  8.0 0.7 broadcast_multiply_fusion
  8.7 0.8 copy.14
  10.3 1.0 scatter_custom_fusion
  11.3 2.2 gather_fusion.1
  13.5 1.8 reshape.120
  15.5 1.2 gather_fusion
  17.0 2.2 gather_fusion.2
  19.2 2.2 gather.17
  21.4 3.6 %fusion.10 = (bf16[32,4,4096]{2,1,0:T(4,128)(2,1)}, bf16[32,4,4096]{2,1,0:T(4,128)(2,1)}) fusion(f32[32,4,4096]{2,1,0:T(4,128)S(1)} %reshape.120, f32[32,4]{1,0:T(8,128)S(1)} %mul.55, pred[32,4]{1,0:T(8,128)(4,1)S(1)} %broadcast_in_dim.63, bf16[32,4,4096]{2,1,0:T(4,128)(2,1)} %gather.17), kind=kLoop, calls=%fused_computation.20 | loop fusion | flops 2097152 | bytes 5243520 | tf_op jit(solution)/shard_map/jit(_where)/select_n | solution.py:41
  25.0 25.6 %all-to-all-start.1 = ((bf16[32,4,4096]{2,1,0:T(4,128)(2,1)}), bf16[32,4,4096]{2,1,0:T(4,128)(2,1)S(1)}, u32[]{:S(2)}, u32[]{:S(2)}) async-start(bf16[32,4,4096]{2,1,0:T(4,128)(2,1)} %get-tuple-element.9), calls=%async_computation.1 | async-start | bytes 2097152 | tf_op jit(solution)/shard_map/all_to_all | solution.py:43
  50.7 0.7 all-gather.9.cloned.1.call-update
  51.4 54.7 %all-to-all-done.1 = bf16[32,4,4096]{2,1,0:T(4,128)(2,1)S(1)} async-done(((bf16[32,4,4096]{2,1,0:T(4,128)(2,1)}), bf16[32,4,4096]{2,1,0:T(4,128)(2,1)S(1)}, u32[]{:S(2)}, u32[]{:S(2)}) %all-to-all-start.1) | async-done | bytes 1048608 | tf_op jit(solution)/shard_map/all_to_all | solution.py:43
  106.1 5.0 %all-to-all-start = ((bf16[32,4,4096]{2,1,0:T(4,128)(2,1)}), bf16[32,4,4096]{2,1,0:T(4,128)(2,1)}, u32[]{:S(2)}, u32[]{:S(2)}) async-start(bf16[32,4,4096]{2,1,0:T(4,128)(2,1)} %get-tuple-element.8), calls=%async_computation | async-start | bytes 2097152 | tf_op jit(solution)/shard_map/all_to_all | solution.py:50
  111.1 0.7 all-gather.7.cloned.1.call-update
  112.2 54.5 %all-to-all-done = bf16[32,4,4096]{2,1,0:T(4,128)(2,1)} async-done(((bf16[32,4,4096]{2,1,0:T(4,128)(2,1)}), bf16[32,4,4096]{2,1,0:T(4,128)(2,1)}, u32[]{:S(2)}, u32[]{:S(2)}) %all-to-all-start) | async-done | bytes 1048608 | tf_op jit(solution)/shard_map/all_to_all | solution.py:50
  166.8 1.3 reshape.116
  168.1 2.0 fusion.3
  170.2 2.0 fusion.6
  172.3 2.4 multiply_convert_fusion.2
  174.7 3.2 %convolution_convert_fusion = bf16[4096,512]{1,0:T(8,128)(2,1)} fusion(bf16[128,4096]{1,0:T(8,128)(2,1)S(1)} %reshape.117, bf16[128,256]{1,0:T(8,128)(2,1)S(1)} %get-tuple-element.6, bf16[128,256]{1,0:T(8,128)(2,1)S(1)} %get-tuple-element.7), kind=kOutput, calls=%fused_computation.5 | convolution fusion | flops 539230208 | bytes 5373952 | tf_op jit(solution)/shard_map/dot_general | solution.py:14
  178.0 2.5 fusion.1
  180.6 0.8 fusion
  181.4 1.2 reshape.118
  182.6 4.9 %all-to-all-start.2 = ((bf16[32,4,4096]{2,1,0:T(4,128)(2,1)}), bf16[32,4,4096]{2,1,0:T(4,128)(2,1)S(1)}, u32[]{:S(2)}, u32[]{:S(2)}) async-start(bf16[32,4,4096]{2,1,0:T(4,128)(2,1)} %reshape.118), calls=%async_computation.2 | async-start | bytes 2097152 | tf_op jit(solution)/shard_map/all_to_all | solution.py:97
  187.8 2.1 convolution_convert_fusion.1
  190.2 53.0 %all-to-all-done.2 = bf16[32,4,4096]{2,1,0:T(4,128)(2,1)S(1)} async-done(((bf16[32,4,4096]{2,1,0:T(4,128)(2,1)}), bf16[32,4,4096]{2,1,0:T(4,128)(2,1)S(1)}, u32[]{:S(2)}, u32[]{:S(2)}) %all-to-all-start.2) | async-done | bytes 1048608 | tf_op jit(solution)/shard_map/all_to_all | solution.py:97
  243.5 2.2 gather_fusion.3
  245.7 2.4 reshape.121
  248.0 4.8 %select_reduce_fusion = bf16[64,4096]{1,0:T(8,128)(2,1)} fusion(f32[64,2,4096]{2,1,0:T(2,128)S(1)} %reshape.121, pred[64,2]{1,0:T(8,128)(4,1)S(1)} %lt.48), kind=kLoop, calls=%fused_computation.18 | loop fusion | flops 786432 | bytes 2621568 | tf_op jit(solution)/shard_map/reduce_sum | solution.py:107
  252.9 2.3 slice_bitcast_fusion
  255.1 6.8 %reduce-scatter.5.cloned.1.call-done = bf16[64,4096]{1,0:T(8,128)(2,1)} async-done(((bf16[256,4096]{1,0:T(8,128)(2,1)}), bf16[64,4096]{1,0:T(8,128)(2,1)}) %reduce-scatter.5.cloned.1.call-update) | async-done | bytes 524304 | tf_op jit(solution)/shard_map/reduce_scatter | solution.py:88
  (39 shorter events, 2.7 us)
Async XLA Ops:
  7.2 4.1 %copy-start = (bf16[64,4096]{1,0:T(8,128)(2,1)S(1)}, bf16[64,4096]{1,0:T(8,128)(2,1)}, u32[]{:S(2)}) copy-start(bf16[64,4096]{1,0:T(8,128)(2,1)} %param.8) | copy-start | bytes 1572868
  7.2 160.9 %all-gather.11.cloned.1.call-start = ((), (), s32[]{:S(2)}) async-start(), calls=%async_computation.9 | async-start | bytes 2621440 | tf_op jit(solution)/shard_map/all_gather | solution.py:65
  13.5 1.8 copy-start.3
  13.5 3.5 %copy-start.1 = (bf16[64,4096]{1,0:T(8,128)(2,1)S(1)}, bf16[64,4096]{1,0:T(8,128)(2,1)}, u32[]{:S(2)}) copy-start(bf16[64,4096]{1,0:T(8,128)(2,1)} %param.7) | copy-start | bytes 1572868
  25.0 81.1 %all-to-all-start.1 = ((bf16[32,4,4096]{2,1,0:T(4,128)(2,1)}), bf16[32,4,4096]{2,1,0:T(4,128)(2,1)S(1)}, u32[]{:S(2)}, u32[]{:S(2)}) async-start(bf16[32,4,4096]{2,1,0:T(4,128)(2,1)} %get-tuple-element.9), calls=%async_computation.1 | async-start | bytes 2097152 | tf_op jit(solution)/shard_map/all_to_all | solution.py:43
  50.6 119.6 %all-gather.9.cloned.1.call-start = ((), (), s32[]{:S(2)}) async-start(), calls=%async_computation.8 | async-start | bytes 2621440 | tf_op jit(solution)/shard_map/all_gather | solution.py:66
  106.1 60.7 %all-to-all-start = ((bf16[32,4,4096]{2,1,0:T(4,128)(2,1)}), bf16[32,4,4096]{2,1,0:T(4,128)(2,1)}, u32[]{:S(2)}, u32[]{:S(2)}) async-start(bf16[32,4,4096]{2,1,0:T(4,128)(2,1)} %get-tuple-element.8), calls=%async_computation | async-start | bytes 2097152 | tf_op jit(solution)/shard_map/all_to_all | solution.py:50
  111.1 61.2 %all-gather.7.cloned.1.call-start = ((), (), s32[]{:S(2)}) async-start(), calls=%async_computation.7 | async-start | bytes 2621440 | tf_op jit(solution)/shard_map/all_gather | solution.py:67
  111.9 141.0 %reduce-scatter.3.cloned.1.call-start = ((), (), s32[]{:S(2)}) async-start(), calls=%async_computation.5 | async-start | bytes 5242880 | tf_op jit(solution)/shard_map/reduce_scatter | solution.py:81
  178.0 2.6 copy-start.2
  182.6 60.6 %all-to-all-start.2 = ((bf16[32,4,4096]{2,1,0:T(4,128)(2,1)}), bf16[32,4,4096]{2,1,0:T(4,128)(2,1)S(1)}, u32[]{:S(2)}, u32[]{:S(2)}) async-start(bf16[32,4,4096]{2,1,0:T(4,128)(2,1)} %reshape.118), calls=%async_computation.2 | async-start | bytes 2097152 | tf_op jit(solution)/shard_map/all_to_all | solution.py:97
  187.6 74.3 %reduce-scatter.5.cloned.1.call-start = ((), (), s32[]{:S(2)}) async-start(), calls=%async_computation.6 | async-start | bytes 2621440 | tf_op jit(solution)/shard_map/reduce_scatter | solution.py:88
Sparse Core Ops, SparseCore 0:
  9.8 51.2 all-gather.10
  63.0 36.8 all-gather.8
  113.7 38.3 all-gather.6
  178.1 45.2 reduce-scatter.2
  226.4 35.5 reduce-scatter.4
where the time goes:
time: 269 us; the launch traced here: 268 us
  waiting for transfers between devices  171 us (64%)
  starting transfers between devices  36 us (13%)
  local copies, waits for them, and re-layouts  22.3 us (8%)
  matrix products  15.2 us (6%)
  between operations  14.1 us (5%)
  other arithmetic  9.57 us (4%)
    all_to_all x1, waiting for transfers between devices, local(): lax.all_to_all(send_rows.reshape(experts, capacity, model_width), 'expert...  54.7 us
    all_to_all x1, waiting for transfers between devices, local(): lax.all_to_all(send_cot.reshape(experts, capacity, model_width), 'expert'...  54.5 us
    all_to_all x1, waiting for transfers between devices, local(): lax.all_to_all(rows_out.reshape(experts, capacity, model_width), 'expert'...  53 us
    all_to_all x1, starting transfers between devices, local(): lax.all_to_all(send_rows.reshape(experts, capacity, model_width), 'expert...  25.6 us
    reduce_scatter x1, waiting for transfers between devices, local(): lax.psum_scatter(contract_first(columns, cot_in).astype(jnp.bfloat16), 't...  6.78 us
    dot_general x3, matrix products, contract_last(): lax.dot_general(left, right, (((1,), (1,)), ((), ())), preferred_element_...  5.8 us
  transfers between devices with their start and end apart: 8, of which 4 were waited for; matrix products, arithmetic and copies ran while one was open for 15% of the time, Pallas kernels for 0%

commit v1 on v0

v1 whole, which is shorter than its diff:
```python
import functools

import jax
import jax.numpy as jnp
from jax import lax
from jax.experimental import pallas as pl
from jax.experimental.pallas import tpu as pltpu
from jax.sharding import PartitionSpec as P

BF = jnp.bfloat16
F32 = jnp.float32
VMEM = pl.BlockSpec(memory_space=pltpu.VMEM)
SMEM = pl.BlockSpec(memory_space=pltpu.SMEM)
SPLIT = (3, 1)


def cost(flops, bytes_accessed):
    return pl.CostEstimate(flops=int(flops), bytes_accessed=int(bytes_accessed), transcendentals=0)


def nn(a, b):
    return lax.dot_general(a, b, (((1,), (0,)), ((), ())), preferred_element_type=F32)


def nt(a, b):
    return lax.dot_general(a, b, (((1,), (1,)), ((), ())), preferred_element_type=F32)


def tn(a, b):
    return lax.dot_general(a, b, (((0,), (0,)), ((), ())), preferred_element_type=F32)


def dispatch_kernel(split, ids_ref, gate_ref, tok_ref, cot_ref, *refs):
    outs, (pick_ref, scale_ref) = refs[: len(split)], refs[len(split) :]
    n_tok, width = tok_ref.shape
    quarter = width // 4
    experts = outs[0].shape[0]
    rows = experts * 8
    slots = sum(split)

    @pl.when(pl.program_id(0) == 0)
    def _():
        row = lax.broadcasted_iota(jnp.int32, (rows, 2 * n_tok), 0)
        lane = lax.broadcasted_iota(jnp.int32, (rows, 2 * n_tok), 1)
        expert = row // 8
        first = ids_ref[0:1, :] == expert
        second = ids_ref[1:2, :] == expert
        member = jnp.where(first | second, 1.0, 0.0).astype(F32)
        j = lax.broadcasted_iota(jnp.int32, (2 * n_tok, 2 * n_tok), 0)
        c = lax.broadcasted_iota(jnp.int32, (2 * n_tok, 2 * n_tok), 1)
        earlier = jnp.where((j < n_tok) & (j < c % n_tok), 1.0, 0.0).astype(BF)
        before = nn(member.astype(BF), earlier)
        gates = jnp.where(first, gate_ref[0:1, :], gate_ref[1:2, :])
        kind = row % 2
        same_kind = kind == lane // n_tok
        part = (row % 8) // 2
        for p in range(slots):
            chosen = jnp.where(before == float(p), member, 0.0)
            weight = jnp.sum(jnp.where(lane < n_tok, chosen * gates, 0.0), axis=1, keepdims=True)
            scale_ref[p] = jnp.where(kind[:, :1] == 1, weight, 1.0)
            kept = jnp.where(same_kind, chosen, 0.0)
            for q in range(4):
                pick_ref[p, :, q * 2 * n_tok : (q + 1) * 2 * n_tok] = jnp.where(part == q, kept, 0.0).astype(BF)

    stack = []
    for q in range(4):
        cols = slice(q * quarter, (q + 1) * quarter)
        stack += [tok_ref[:, cols], cot_ref[:, cols]]
    source = jnp.concatenate(stack, axis=0)
    p = 0
    for out, count in zip(outs, split):
        for k in range(count):
            picked = nn(pick_ref[p], source) * scale_ref[p]
            out[:, 0, :, k * quarter : (k + 1) * quarter] = picked.reshape(experts, 8, quarter).astype(BF)
            p += 1


def dispatch(ids2, gates2, tokens, cotangent, experts, parts, split):
    n_tok, d = tokens.shape
    width = d // parts
    rows = experts * 8
    slots = sum(split)
    return pl.pallas_call(
        functools.partial(dispatch_kernel, split),
        grid=(parts,),
        in_specs=[
            pl.BlockSpec((2, 2 * n_tok), lambda i: (0, 0)),
            pl.BlockSpec((2, 2 * n_tok), lambda i: (0, 0)),
            pl.BlockSpec((n_tok, width), lambda i: (0, i)),
            pl.BlockSpec((n_tok, width), lambda i: (0, i)),
        ],
        out_specs=[pl.BlockSpec((experts, 1, 8, c * width // 4), lambda i: (0, i, 0, 0)) for c in split],
        out_shape=[jax.ShapeDtypeStruct((experts, parts, 8, c * width // 4), BF) for c in split],
        scratch_shapes=[pltpu.VMEM((slots, rows, 8 * n_tok), BF), pltpu.VMEM((slots, rows, 1), F32)],
        cost_estimate=cost(2 * slots * rows * 8 * n_tok * d // 4, 4 * n_tok * d * 2 + 2 * slots * experts * d * 2),
        name="dispatch",
    )(ids2, gates2, tokens, cotangent)


def project_kernel(count, t_ref, recv_ref, wg_ref, wu_ref, *refs):
    parts = 4
    wd_refs, refs = refs[:parts], refs[parts:]
    x_ref, c_ref = refs[0], refs[1]
    z_refs, (flat, wd, z) = refs[2 : 2 + parts], refs[2 + parts :]
    t = t_ref[0]
    ff_part, width = wd_refs[0].shape
    sources = recv_ref.shape[0]
    quarter = width // 4
    group = sources // parts
    for d in range(parts):
        at = pl.multiple_of(lax.rem(t - d + parts, parts) * ff_part, ff_part)
        wd[pl.ds(at, ff_part), :] = wd_refs[d][...]
    for b in range(flat.shape[0]):
        flat[b] = recv_ref[:, :, b * 128 : (b + 1) * 128].astype(F32).reshape(flat.shape[1:])
    lanes = quarter // 128
    for p in range(count):
        for kind, dst in ((0, x_ref), (1, c_ref)):
            for q in range(4):
                for b in range(lanes):
                    v = flat[p * lanes + b, pl.ds(2 * q + kind, sources, stride=8), :].astype(BF)
                    for g in range(parts):
                        r = (g * count + p) * group
                        dst[r : r + group, q * quarter + b * 128 : q * quarter + (b + 1) * 128] = v[
                            g * group : (g + 1) * group
                        ]
    ff = wg_ref.shape[1]
    per = count * group
    x = x_ref[...]
    z[:, :, 0:ff] = nn(x, wg_ref[...]).astype(BF).reshape(parts, per, ff)
    z[:, :, ff : 2 * ff] = nn(x, wu_ref[...]).astype(BF).reshape(parts, per, ff)
    z[:, :, 2 * ff :] = nt(c_ref[...], wd[...]).astype(BF).reshape(parts, per, ff)
    for d in range(parts):
        z_refs[d][...] = z[lax.rem(t + d, parts)]


def project(t, recv, wg, wu, wd_pieces, count):
    sources = recv.shape[0]
    width, ff = wg.shape
    rows = sources * count
    parts = len(wd_pieces)
    out = [jax.ShapeDtypeStruct((rows, width), BF)] * 2 + [jax.ShapeDtypeStruct((rows // parts, 3 * ff), BF)] * parts
    return pl.pallas_call(
        functools.partial(project_kernel, count),
        in_specs=[SMEM] + [VMEM] * (3 + parts),
        out_specs=[VMEM] * len(out),
        out_shape=out,
        scratch_shapes=[
            pltpu.VMEM((count * width // 4 // 128, sources * 8, 128), F32),
            pltpu.VMEM((ff, width), BF),
            pltpu.VMEM((parts, rows // parts, 3 * ff), BF),
        ],
        cost_estimate=cost(2 * rows * width * 3 * ff, 4 * rows * width * 2 + 3 * ff * width * 2),
        name="project",
    )(t, recv, wg, wu, *wd_pieces)


def middle_kernel(a_ref, b_ref, c_ref, d_ref, h_ref):
    ff = h_ref.shape[1] // 3
    total = (a_ref[...].astype(F32) + b_ref[...].astype(F32)) + (c_ref[...].astype(F32) + d_ref[...].astype(F32))
    pre_gate, pre_up, grad_hidden = total[:, :ff], total[:, ff : 2 * ff], total[:, 2 * ff :]
    sig = jax.nn.sigmoid(pre_gate)
    activated = pre_gate * sig
    h_ref[:, :ff] = (activated * pre_up).astype(BF)
    h_ref[:, ff : 2 * ff] = (grad_hidden * pre_up * sig * (1.0 + pre_gate * (1.0 - sig))).astype(BF)
    h_ref[:, 2 * ff :] = (grad_hidden * activated).astype(BF)


def middle(z):
    return pl.pallas_call(
        middle_kernel,
        in_specs=[VMEM] * 4,
        out_specs=VMEM,
        out_shape=jax.ShapeDtypeStruct(z[0].shape, BF),
        cost_estimate=cost(40 * z[0].size, 10 * z[0].size),
        name="middle",
    )(*z)


def back_kernel(count, t_ref, wg_ref, wu_ref, *refs):
    parts = 4
    h_refs, (msg_ref, all_ref, h, flat) = refs[:parts], refs[parts:]
    t = t_ref[0]
    width, ff = wg_ref.shape
    sources = msg_ref.shape[0]
    group = sources // parts
    for d in range(parts):
        h[lax.rem(t - d + parts, parts)] = h_refs[d][...]
    joint = h[...].reshape(sources * count, 3 * ff)
    all_ref[...] = joint
    eighth = width // 8
    for half in range(2):
        cols = slice(half * width // 2, (half + 1) * width // 2)
        rows = nt(joint[:, ff : 2 * ff], wg_ref[cols, :]) + nt(joint[:, 2 * ff :], wu_ref[cols, :])
        for g in range(parts):
            for p in range(count):
                r = (g * count + p) * group
                for o in range(4):
                    flat[p, pl.ds(g * group * 8 + half * 4 + o, group, stride=8), :] = rows[
                        r : r + group, o * eighth : (o + 1) * eighth
                    ]
    for p in range(count):
        msg_ref[:, :, p * eighth : (p + 1) * eighth] = flat[p].reshape(sources, 8, eighth).astype(BF)


def back(t, wg, wu, h, count):
    width, ff = wg.shape
    parts = len(h)
    rows = h[0].shape[0] * parts
    sources = rows // count
    return pl.pallas_call(
        functools.partial(back_kernel, count),
        in_specs=[SMEM] + [VMEM] * (2 + parts),
        out_specs=[VMEM] * 2,
        out_shape=[
            jax.ShapeDtypeStruct((sources, 8, count * width // 8), BF),
            jax.ShapeDtypeStruct((rows, 3 * ff), BF),
        ],
        scratch_shapes=[
            pltpu.VMEM((parts, rows // parts, 3 * ff), BF),
            pltpu.VMEM((count, sources * 8, width // 8), F32),
        ],
        cost_estimate=cost(4 * rows * width * ff, rows * width * 2 + 2 * width * ff * 2),
        name="back",
    )(t, wg, wu, *h)


def combine_kernel(split, parts, ids_ref, *refs):
    rets, refs = refs[: len(split)], refs[len(split) :]
    out_ref, flats, rhs = refs[0], refs[1 : 1 + len(split)], refs[1 + len(split)]
    n_tok, d = out_ref.shape
    slots = sum(split)
    experts = rets[0].shape[0] // parts
    eighth = d // parts // 8
    lane = lax.broadcasted_iota(jnp.int32, (n_tok, slots * experts), 1)
    expert = lane % experts
    member = jnp.where((ids_ref[:, 0:1] == expert) | (ids_ref[:, 1:2] == expert), 1.0, 0.0).astype(F32)
    i = lax.broadcasted_iota(jnp.int32, (n_tok, n_tok), 0)
    j = lax.broadcasted_iota(jnp.int32, (n_tok, n_tok), 1)
    before = nn(jnp.where(j < i, 1.0, 0.0).astype(BF), member.astype(BF))
    pick = jnp.where(before == (lane // experts).astype(F32), member, 0.0).astype(BF)
    for ret, flat in zip(rets, flats):
        for k in range(flat.shape[0]):
            flat[k] = ret[:, :, k * eighth : (k + 1) * eighth].astype(F32).reshape(flat.shape[1:])
    for u in range(parts * 8):
        p = 0
        for flat, count in zip(flats, split):
            for k in range(count):
                v = flat[k, pl.ds(u, experts, stride=parts * 8), :]
                rhs[p * experts : (p + 1) * experts, u * eighth : (u + 1) * eighth] = v.astype(BF)
                p += 1
    out_ref[...] = nn(pick, rhs[...]).astype(BF)


def combine(ids, rets, split, parts, d):
    n_tok = ids.shape[0]
    slots = sum(split)
    experts = rets[0].shape[0] // parts
    return pl.pallas_call(
        functools.partial(combine_kernel, split, parts),
        in_specs=[VMEM] * (1 + len(split)),
        out_specs=VMEM,
        out_shape=jax.ShapeDtypeStruct((n_tok, d), BF),
        scratch_shapes=[pltpu.VMEM((c, r.shape[0] * 8, d // parts // 8), F32) for c, r in zip(split, rets)]
        + [pltpu.VMEM((slots * experts, d), BF)],
        cost_estimate=cost(2 * n_tok * slots * experts * d, 4 * n_tok * d * 2),
        name="combine",
    )(ids, *rets)


def place_kernel(t_ref, *refs):
    parts = len(refs) - 1
    out = refs[-1]
    width = refs[0].shape[1]
    for d in range(parts):
        at = pl.multiple_of(lax.rem(t_ref[0] - d + parts, parts) * width, width)
        out[:, pl.ds(at, width)] = refs[d][...]


def place(t, pieces):
    rows, width = pieces[0].shape
    return pl.pallas_call(
        place_kernel,
        in_specs=[SMEM] + [VMEM] * len(pieces),
        out_specs=VMEM,
        out_shape=jax.ShapeDtypeStruct((rows, width * len(pieces)), BF),
        cost_estimate=cost(rows * width, 4 * rows * width * 4),
        name="place",
    )(t, *pieces)


def local(tokens, cotangent, expert_ids, gate_wts, w_gate, w_up, w_down):
    n_tok, d = tokens.shape
    experts = lax.axis_size("expert")
    parts = lax.axis_size("tensor")
    slots = 2 * n_tok // experts
    split = SPLIT if sum(SPLIT) == slots else (slots,)
    t = lax.axis_index("tensor").astype(jnp.int32)
    t1 = t.reshape(1)
    wg, wu, wd = w_gate[0], w_up[0], w_down[0]
    width, ff = wg.shape
    ff_part = wd.shape[0]

    def shift(x, k):
        return lax.ppermute(x, "tensor", [(s, (s + k) % parts) for s in range(parts)])

    ids2 = jnp.tile(expert_ids.T, (1, 2))
    gates2 = jnp.tile(gate_wts.T, (1, 2))
    sends = dispatch(ids2, gates2, tokens, cotangent, experts, parts, split)
    sources = experts * parts

    wd_pieces = [lax.dynamic_slice_in_dim(wd, lax.rem(t + k, parts) * width, width, 1) for k in range(parts)]
    wd_pieces = [wd_pieces[0]] + [shift(wd_pieces[k], k) for k in range(1, parts)]

    axes = ("expert", "tensor")
    x_all, c_all, h_all, rets = [], [], [], []
    for send, count in zip(sends, split):
        recv = lax.all_to_all(send.reshape(sources, 8, -1), axes, 0, 0, tiled=True)
        x, c, *z = project(t1, recv, wg, wu, wd_pieces, count)
        h = middle([z[0]] + [shift(z[k], k) for k in range(1, parts)])
        msg, joint = back(t1, wg, wu, [h] + [shift(h, k) for k in range(1, parts)], count)
        rets.append(lax.all_to_all(msg, axes, 0, 0, tiled=True))
        x_all.append(x)
        c_all.append(c)
        h_all.append(joint)

    def total(pairs):
        return functools.reduce(lambda a, b: a + b, [tn(a, b) for a, b in pairs]).astype(BF)

    grad_gate = total([(x, h[:, ff : 2 * ff]) for x, h in zip(x_all, h_all)])
    grad_up = total([(x, h[:, 2 * ff :]) for x, h in zip(x_all, h_all)])
    grad_down = total([(h[:, :ff], c) for c, h in zip(c_all, h_all)])
    pieces = [lax.dynamic_slice_in_dim(grad_down, lax.rem(t + k, parts) * ff_part, ff_part, 0) for k in range(parts)]
    grad_down = place(t1, [pieces[0]] + [shift(pieces[k], k) for k in range(1, parts)])
    input_grad = combine(expert_ids, rets, split, parts, d)
    return input_grad, grad_gate[None], grad_up[None], grad_down[None]


def solution(mesh):
    tok = P(("group", "expert", "tensor"), None)
    wts = P("expert", "tensor", None)
    out = P(("group", "expert"), "tensor", None)
    return jax.shard_map(
        local,
        mesh=mesh,
        in_specs=(tok, tok, tok, tok, wts, wts, wts),
        out_specs=(tok, out, out, out),
        check_vma=False,
    )
```

time: 269 us -> 266 us (0.989)
  waiting for transfers between devices: 171 us -> 95.7 us
  blocking collectives: 0 us -> 63.5 us
  starting transfers between devices: 36 us -> 64.1 us
  Pallas kernels: 0 us -> 26.6 us
  between operations: 14.1 us -> 0.83 us
  local copies, waits for them, and re-layouts: 22.3 us -> 10.3 us
  matrix products: 15.2 us -> 3.96 us
  other arithmetic: 9.57 us -> 0 us
    all_to_all x3, waiting for transfers between devices: 162 us -> 67.2 us  [the longest x1 41.4 us: local(): recv = lax.all_to_all(send.reshape(sources, 8, -1), axes, 0, 0, tiled=True)]
    all_to_all x0 -> x1, blocking collectives: none -> 63.5 us  [local(): recv = lax.all_to_all(send.reshape(sources, 8, -1), axes, 0, 0, tiled=True)]
    ppermute x0 -> x18, waiting for transfers between devices: none -> 28.5 us  [shift(): lax.ppermute(x, 'tensor', [(s, (s + k) % parts) for s in range(parts)])]
    ppermute x0 -> x18, starting transfers between devices: none -> 26.7 us  [shift(): lax.ppermute(x, 'tensor', [(s, (s + k) % parts) for s in range(parts)])]
    pallas_call x0 -> x9, Pallas kernels: none -> 26.6 us  [the longest x2 6.91 us: project(): pl.pallas_call(functools.partial(project_kernel, count), in_specs=[SMEM]...]
    dot_general x7 -> x6, matrix products: 15.2 us -> 3.96 us  [tn(): lax.dot_general(a, b, (((0,), (0,)), ((), ())), preferred_element_type=F32)]
    gather x5 -> x0, local copies, waits for them, and re-layouts: 10 us -> none  [the longest x2 4.42 us: local(): send_rows = jnp.where(populated_rows[:, None], tokens[tok_index], zero_half)]
    reduce_scatter x2 -> x0, waiting for transfers between devices: 6.79 us -> none  [the longest x1 6.78 us: local(): lax.psum_scatter(contract_first(columns, cot_in).astype(jnp.bfloat16), 't...]
  transfers between devices with their start and end apart: 8 -> 21, of which waited for: 4 -> 16; matrix products, arithmetic and copies ran while one was open for 15% -> 2% of each run, Pallas kernels for 0% -> 7%
where the time goes in v1:
time: 266 us; the launch traced here: 265 us
  waiting for transfers between devices  95.7 us (36%)
  starting transfers between devices  64.1 us (24%)
  blocking collectives  63.5 us (24%)
  Pallas kernels  26.6 us (10%)
  local copies, waits for them, and re-layouts  10.3 us (4%)
  matrix products  3.96 us (1%)
    all_to_all x1, blocking collectives, local(): recv = lax.all_to_all(send.reshape(sources, 8, -1), axes, 0, 0, tiled=True)  63.5 us
    all_to_all x1, waiting for transfers between devices, local(): recv = lax.all_to_all(send.reshape(sources, 8, -1), axes, 0, 0, tiled=True)  41.4 us
    all_to_all x2, starting transfers between devices, local(): rets.append(lax.all_to_all(msg, axes, 0, 0, tiled=True))  29.1 us
    ppermute x18, waiting for transfers between devices, shift(): lax.ppermute(x, 'tensor', [(s, (s + k) % parts) for s in range(parts)])  28.5 us
    ppermute x18, starting transfers between devices, shift(): lax.ppermute(x, 'tensor', [(s, (s + k) % parts) for s in range(parts)])  26.7 us
    all_to_all x2, waiting for transfers between devices, local(): rets.append(lax.all_to_all(msg, axes, 0, 0, tiled=True))  25.8 us
    all_to_all x1, starting transfers between devices, local(): recv = lax.all_to_all(send.reshape(sources, 8, -1), axes, 0, 0, tiled=True)  8.3 us
    pallas_call x2, Pallas kernels, project(): pl.pallas_call(functools.partial(project_kernel, count), in_specs=[SMEM]...  6.91 us
  transfers between devices with their start and end apart: 21, of which 16 were waited for; matrix products, arithmetic and copies ran while one was open for 2% of the time, Pallas kernels for 7%

profile of v1, /device:TPU:33, one launch (start us, length us, event | category | flops | bytes accessed | tf_op | source)
XLA Modules:
  0.0 265.1 jit_solution(12910170733460831377)
XLA Ops:
  3.3 5.0 %dispatch.1 = (bf16[32,4,8,768]{3,2,1,0:T(8,128)(2,1)}, bf16[32,4,8,256]{3,2,1,0:T(8,128)(2,1)}) custom-call(s32[2,128]{1,0:T(2,128)} %tile.9.ids_ref, f32[2,128]{1,0:T(2,128)} %tile.21.gate_ref, bf16[64,4096]{1,0:T(8,128)(2,1)} %tok_ref.1, bf16[64,4096]{1,0:T(8,128)(2,1)} %cot_ref.1), custom_call_target="tpu_custom_call" | custom-call | flops 1073741824 | bytes 4194304 | tf_op jit(solution)/shard_map/dispatch/pallas_call | solution.py:83
  8.3 63.5 %all_to_all.20.recv_ref = bf16[128,8,256]{2,1,0:T(8,128)(2,1)} all-to-all(bf16[128,8,256]{2,1,0:T(8,128)(2,1)} %bitcast.35), channel_id=1, replica_groups=mesh['group'=2,'expert'=32,'tensor'=4] {'expert','tensor'}, dimensions={0} | all-to-all | bytes 1048576 | tf_op jit(solution)/shard_map/all_to_all | solution.py:317
  71.8 8.3 %all-to-all-start = ((bf16[128,8,768]{2,1,0:T(8,128)(2,1)}), bf16[128,8,768]{2,1,0:T(8,128)(2,1)S(1)}, u32[]{:S(2)}, u32[]{:S(2)}) async-start(bf16[128,8,768]{2,1,0:T(8,128)(2,1)} %bitcast.34), calls=%async_computation | async-start | bytes 3145728 | tf_op jit(solution)/shard_map/all_to_all | solution.py:317
  80.8 1.4 collective-permute-start
  82.2 2.4 collective-permute-start.1
  86.4 6.0 %collective-permute-done.1.refs_2_ = bf16[64,1024]{1,0:T(8,128)(2,1)S(1)} collective-permute-done((bf16[64,1024]{1,0:T(8,128)(2,1)S(1)}, bf16[64,1024]{1,0:T(8,128)(2,1)S(1)}, u32[]{:S(2)}, u32[]{:S(2)}) %collective-permute-start.1) | collective-permute-done | bytes 131104 | tf_op jit(solution)/shard_map/ppermute | solution.py:304
  93.1 2.8 %project.3 = (bf16[128,1024]{1,0:T(8,128)(2,1)}, bf16[128,1024]{1,0:T(8,128)(2,1)}, bf16[32,768]{1,0:T(8,128)(2,1)}, bf16[32,768]{1,0:T(8,128)(2,1)}, bf16[32,768]{1,0:T(8,128)(2,1)}, /*index=5*/bf16[32,768]{1,0:T(8,128)(2,1)}) custom-call(s32[1]{0:T(128)} %bitcast.t_ref, bf16[128,8,256]{2,1,0:T(8,128)(2,1)} %all_to_all.20.recv_ref, ...), custom_call_target="tpu_custom_call" | custom-call | flops 201326592 | bytes 2621440 | tf_op jit(solution)/shard_map/project/pallas_call | solution.py:142
  96.2 2.0 collective-permute-start.10
  98.1 1.4 collective-permute-start.11
  102.6 1.5 middle.3.refs_0_
  105.1 2.7 %collective-permute-start.13 = (bf16[32,768]{1,0:T(8,128)(2,1)}, bf16[32,768]{1,0:T(8,128)(2,1)S(1)}, u32[]{:S(2)}, u32[]{:S(2)}) collective-permute-start(bf16[32,768]{1,0:T(8,128)(2,1)} %middle.3.refs_0_), channel_id=1, source_target_pairs={{0,2},{1,3},{2,0},{3,1},{4,6},{5,7},{6,4},{7,5},{8,10},{9,11},{10,... | collective-permute-start | bytes 147464 | tf_op jit(solution)/shard_map/ppermute | solution.py:304
  108.9 1.8 collective-permute-done.13.refs_2_
  112.1 2.4 back.3
  114.6 41.4 %all-to-all-done.recv_ref = bf16[128,8,768]{2,1,0:T(8,128)(2,1)S(1)} async-done(((bf16[128,8,768]{2,1,0:T(8,128)(2,1)}), bf16[128,8,768]{2,1,0:T(8,128)(2,1)S(1)}, u32[]{:S(2)}, u32[]{:S(2)}) %all-to-all-start) | async-done | bytes 1572896 | tf_op jit(solution)/shard_map/all_to_all | solution.py:317
  156.0 9.3 %all-to-all-start.3 = ((bf16[128,8,128]{2,1,0:T(8,128)(2,1)}), bf16[128,8,128]{2,1,0:T(8,128)(2,1)S(1)}, u32[]{:S(2)}, u32[]{:S(2)}) async-start(bf16[128,8,128]{2,1,0:T(8,128)(2,1)} %get-tuple-element.33), calls=%async_computation.3 | async-start | bytes 524288 | tf_op jit(solution)/shard_map/all_to_all | solution.py:321
  165.4 4.1 %project.2 = (bf16[384,1024]{1,0:T(8,128)(2,1)}, bf16[384,1024]{1,0:T(8,128)(2,1)}, bf16[96,768]{1,0:T(8,128)(2,1)}, bf16[96,768]{1,0:T(8,128)(2,1)}, bf16[96,768]{1,0:T(8,128)(2,1)}, /*index=5*/bf16[96,768]{1,0:T(8,128)(2,1)}) custom-call(s32[1]{0:T(128)} %bitcast.t_ref, bf16[128,8,768]{2,1,0:T(8,128)(2,1)} %copy-done, bf16[1024,256]{1,0:T(8,128)(2,1)} %bitcast.28, ...), custom_call_target="tpu_custom_call" | custom-call | flops 603979776 | bytes 4718592 | tf_op jit(solution)/shard_map/project/pallas_call | solution.py:142
  169.5 1.4 collective-permute-start.3
  170.8 2.4 collective-permute-start.4
  175.6 6.0 %collective-permute-done.4.c_ref = bf16[96,768]{1,0:T(8,128)(2,1)S(1)} collective-permute-done((bf16[96,768]{1,0:T(8,128)(2,1)}, bf16[96,768]{1,0:T(8,128)(2,1)S(1)}, u32[]{:S(2)}, u32[]{:S(2)}) %collective-permute-start.4) | collective-permute-done | bytes 147488 | tf_op jit(solution)/shard_map/ppermute | solution.py:304
  182.3 1.9 middle.2.refs_0_
  185.1 1.8 collective-permute-start.7
  187.0 1.3 collective-permute-start.8
  188.3 1.4 collective-permute-done.6.refs_1_
  189.8 2.8 %collective-permute-done.7.refs_2_ = bf16[96,768]{1,0:T(8,128)(2,1)S(1)} collective-permute-done((bf16[96,768]{1,0:T(8,128)(2,1)}, bf16[96,768]{1,0:T(8,128)(2,1)S(1)}, u32[]{:S(2)}, u32[]{:S(2)}) %collective-permute-start.7) | collective-permute-done | bytes 147488 | tf_op jit(solution)/shard_map/ppermute | solution.py:304
  194.1 3.2 %back.2 = (bf16[128,8,384]{2,1,0:T(8,128)(2,1)}, bf16[384,768]{1,0:T(8,128)(2,1)}) custom-call(s32[1]{0:T(128)} %bitcast.t_ref, bf16[1024,256]{1,0:T(8,128)(2,1)} %bitcast.29, bf16[1024,256]{1,0:T(8,128)(2,1)} %bitcast.33, bf16[96,768]{1,0:T(8,128)(2,1)} %middle.2.refs_0_, bf16[96,768]{1,0:T(8,128)(2,1)} %copy-done.13, bf16[96,768]{1,0:T(8,128)(2,1)} %copy-done.14, ...), custom_call_target="tpu_custom_call" | custom-call | flops 402653184 | bytes 1835008 | tf_op jit(solution)/shard_map/back/pallas_call | solution.py:210
  197.3 19.8 %all-to-all-start.1 = ((bf16[128,8,384]{2,1,0:T(8,128)(2,1)}), bf16[128,8,384]{2,1,0:T(8,128)(2,1)S(1)}, u32[]{:S(2)}, u32[]{:S(2)}) async-start(bf16[128,8,384]{2,1,0:T(8,128)(2,1)} %get-tuple-element.27), calls=%async_computation.1 | async-start | bytes 1572864 | tf_op jit(solution)/shard_map/all_to_all | solution.py:321
  220.6 1.4 collective-permute-start.15
  222.0 2.4 collective-permute-start.16
  228.1 3.9 %collective-permute-done.16.refs_2_ = bf16[64,1024]{1,0:T(8,128)(2,1)S(1)} collective-permute-done((bf16[64,1024]{1,0:T(8,128)(2,1)S(1)}, bf16[64,1024]{1,0:T(8,128)(2,1)S(1)}, u32[]{:S(2)}, u32[]{:S(2)}) %collective-permute-start.16) | collective-permute-done | bytes 131104 | tf_op jit(solution)/shard_map/ppermute | solution.py:304
  232.7 1.9 place.1
  234.6 25.8 %all-to-all-done.1.refs_0_ = bf16[128,8,384]{2,1,0:T(8,128)(2,1)S(1)} async-done(((bf16[128,8,384]{2,1,0:T(8,128)(2,1)}), bf16[128,8,384]{2,1,0:T(8,128)(2,1)S(1)}, u32[]{:S(2)}, u32[]{:S(2)}) %all-to-all-start.1) | async-done | bytes 786464 | tf_op jit(solution)/shard_map/all_to_all | solution.py:321
  261.3 3.8 %combine.1 = bf16[64,4096]{1,0:T(8,128)(2,1)} custom-call(s32[64,2]{1,0:T(8,128)} %copy.11.ids_ref, bf16[128,8,384]{2,1,0:T(8,128)(2,1)} %copy-done.1, bf16[128,8,128]{2,1,0:T(8,128)(2,1)} %copy-done.3), custom_call_target="tpu_custom_call" | custom-call | flops 67108864 | bytes 2097152 | tf_op jit(solution)/shard_map/combine/pallas_call | solution.py:258
  (91 shorter events, 27.1 us)
Async XLA Ops:
  71.8 8.3 %copy-start.7 = (bf16[1,64,4096]{2,1,0:T(8,128)(2,1)S(1)}, bf16[1,64,4096]{2,1,0:T(8,128)(2,1)}, u32[]{:S(2)}) copy-start(bf16[1,64,4096]{2,1,0:T(8,128)(2,1)} %param.13) | copy-start | bytes 1572868
  71.8 84.2 %all-to-all-start = ((bf16[128,8,768]{2,1,0:T(8,128)(2,1)}), bf16[128,8,768]{2,1,0:T(8,128)(2,1)S(1)}, u32[]{:S(2)}, u32[]{:S(2)}) async-start(bf16[128,8,768]{2,1,0:T(8,128)(2,1)} %bitcast.34), calls=%async_computation | async-start | bytes 3145728 | tf_op jit(solution)/shard_map/all_to_all | solution.py:317
  80.8 5.5 %collective-permute-start = (bf16[64,1024]{1,0:T(8,128)(2,1)S(1)}, bf16[64,1024]{1,0:T(8,128)(2,1)S(1)}, u32[]{:S(2)}, u32[]{:S(2)}) collective-permute-start(bf16[64,1024]{1,0:T(8,128)(2,1)S(1)} %get-tuple-element.45), channel_id=1, source_target_pairs={{0,1},{1,2},{2,3},{3,0},{4,5},{5,6},{6,7},{7,4},{8,9},{9,10},{10,1... | collective-permute-start | bytes 393224 | tf_op jit(solution)/shard_map/ppermute | solution.py:304
  82.2 10.2 %collective-permute-start.1 = (bf16[64,1024]{1,0:T(8,128)(2,1)S(1)}, bf16[64,1024]{1,0:T(8,128)(2,1)S(1)}, u32[]{:S(2)}, u32[]{:S(2)}) collective-permute-start(bf16[64,1024]{1,0:T(8,128)(2,1)S(1)} %get-tuple-element.47), channel_id=1, source_target_pairs={{0,2},{1,3},{2,0},{3,1},{4,6},{5,7},{6,4},{7,5},{8,10},{9,11},{10,... | collective-permute-start | bytes 393224 | tf_op jit(solution)/shard_map/ppermute | solution.py:304
  84.6 7.8 %collective-permute-start.2 = (bf16[64,1024]{1,0:T(8,128)(2,1)S(1)}, bf16[64,1024]{1,0:T(8,128)(2,1)S(1)}, u32[]{:S(2)}, u32[]{:S(2)}) collective-permute-start(bf16[64,1024]{1,0:T(8,128)(2,1)S(1)} %get-tuple-element.44), channel_id=1, source_target_pairs={{0,3},{1,0},{2,1},{3,2},{4,7},{5,4},{6,5},{7,6},{8,11},{9,8},{10,9... | collective-permute-start | bytes 393224 | tf_op jit(solution)/shard_map/ppermute | solution.py:304
  86.4 6.0 %copy-start.8 = (bf16[64,1024]{1,0:T(8,128)(2,1)}, bf16[64,1024]{1,0:T(8,128)(2,1)S(1)}, u32[]{:S(2)}) copy-start(bf16[64,1024]{1,0:T(8,128)(2,1)S(1)} %collective-permute-done.refs_1_) | copy-start | bytes 393220
  95.9 4.7 %collective-permute-start.9 = (bf16[32,768]{1,0:T(8,128)(2,1)}, bf16[32,768]{1,0:T(8,128)(2,1)S(1)}, u32[]{:S(2)}, u32[]{:S(2)}) collective-permute-start(bf16[32,768]{1,0:T(8,128)(2,1)} %get-tuple-element.30), channel_id=1, source_target_pairs={{0,1},{1,2},{2,3},{3,0},{4,5},{5,6},{6,7},{7,4},{8,9},{9,10},{10,1... | collective-permute-start | bytes 147464 | tf_op jit(solution)/shard_map/ppermute | solution.py:304
  96.2 5.0 %collective-permute-start.10 = (bf16[32,768]{1,0:T(8,128)(2,1)}, bf16[32,768]{1,0:T(8,128)(2,1)S(1)}, u32[]{:S(2)}, u32[]{:S(2)}) collective-permute-start(bf16[32,768]{1,0:T(8,128)(2,1)} %get-tuple-element.31), channel_id=1, source_target_pairs={{0,2},{1,3},{2,0},{3,1},{4,6},{5,7},{6,4},{7,5},{8,10},{9,11},{10,... | collective-permute-start | bytes 147464 | tf_op jit(solution)/shard_map/ppermute | solution.py:304
  98.1 3.9 %collective-permute-start.11 = (bf16[32,768]{1,0:T(8,128)(2,1)}, bf16[32,768]{1,0:T(8,128)(2,1)S(1)}, u32[]{:S(2)}, u32[]{:S(2)}) collective-permute-start(bf16[32,768]{1,0:T(8,128)(2,1)} %get-tuple-element.32), channel_id=1, source_target_pairs={{0,3},{1,0},{2,1},{3,2},{4,7},{5,4},{6,5},{7,6},{8,11},{9,8},{10,9... | collective-permute-start | bytes 147464 | tf_op jit(solution)/shard_map/ppermute | solution.py:304
  104.1 4.8 %collective-permute-start.12 = (bf16[32,768]{1,0:T(8,128)(2,1)}, bf16[32,768]{1,0:T(8,128)(2,1)S(1)}, u32[]{:S(2)}, u32[]{:S(2)}) collective-permute-start(bf16[32,768]{1,0:T(8,128)(2,1)} %middle.3.refs_0_), channel_id=1, source_target_pairs={{0,1},{1,2},{2,3},{3,0},{4,5},{5,6},{6,7},{7,4},{8,9},{9,10},{10,1... | collective-permute-start | bytes 147464 | tf_op jit(solution)/shard_map/ppermute | solution.py:304
  105.1 5.6 %collective-permute-start.13 = (bf16[32,768]{1,0:T(8,128)(2,1)}, bf16[32,768]{1,0:T(8,128)(2,1)S(1)}, u32[]{:S(2)}, u32[]{:S(2)}) collective-permute-start(bf16[32,768]{1,0:T(8,128)(2,1)} %middle.3.refs_0_), channel_id=1, source_target_pairs={{0,2},{1,3},{2,0},{3,1},{4,6},{5,7},{6,4},{7,5},{8,10},{9,11},{10,... | collective-permute-start | bytes 147464 | tf_op jit(solution)/shard_map/ppermute | solution.py:304
  107.7 3.8 %collective-permute-start.14 = (bf16[32,768]{1,0:T(8,128)(2,1)}, bf16[32,768]{1,0:T(8,128)(2,1)S(1)}, u32[]{:S(2)}, u32[]{:S(2)}) collective-permute-start(bf16[32,768]{1,0:T(8,128)(2,1)} %middle.3.refs_0_), channel_id=1, source_target_pairs={{0,3},{1,0},{2,1},{3,2},{4,7},{5,4},{6,5},{7,6},{8,11},{9,8},{10,9... | collective-permute-start | bytes 147464 | tf_op jit(solution)/shard_map/ppermute | solution.py:304
  156.0 9.3 %copy-start = (bf16[128,8,768]{2,1,0:T(8,128)(2,1)}, bf16[128,8,768]{2,1,0:T(8,128)(2,1)S(1)}, u32[]{:S(2)}) copy-start(bf16[128,8,768]{2,1,0:T(8,128)(2,1)S(1)} %all-to-all-done.recv_ref) | copy-start | bytes 4718596
  156.0 41.3 %all-to-all-start.3 = ((bf16[128,8,128]{2,1,0:T(8,128)(2,1)}), bf16[128,8,128]{2,1,0:T(8,128)(2,1)S(1)}, u32[]{:S(2)}, u32[]{:S(2)}) async-start(bf16[128,8,128]{2,1,0:T(8,128)(2,1)} %get-tuple-element.33), calls=%async_computation.3 | async-start | bytes 524288 | tf_op jit(solution)/shard_map/all_to_all | solution.py:321
  169.5 6.1 %collective-permute-start.3 = (bf16[96,768]{1,0:T(8,128)(2,1)}, bf16[96,768]{1,0:T(8,128)(2,1)S(1)}, u32[]{:S(2)}, u32[]{:S(2)}) collective-permute-start(bf16[96,768]{1,0:T(8,128)(2,1)} %get-tuple-element.24), channel_id=1, source_target_pairs={{0,1},{1,2},{2,3},{3,0},{4,5},{5,6},{6,7},{7,4},{8,9},{9,10},{10,1... | collective-permute-start | bytes 442376 | tf_op jit(solution)/shard_map/ppermute | solution.py:304
  170.8 10.8 %collective-permute-start.4 = (bf16[96,768]{1,0:T(8,128)(2,1)}, bf16[96,768]{1,0:T(8,128)(2,1)S(1)}, u32[]{:S(2)}, u32[]{:S(2)}) collective-permute-start(bf16[96,768]{1,0:T(8,128)(2,1)} %get-tuple-element.25), channel_id=1, source_target_pairs={{0,2},{1,3},{2,0},{3,1},{4,6},{5,7},{6,4},{7,5},{8,10},{9,11},{10,... | collective-permute-start | bytes 442376 | tf_op jit(solution)/shard_map/ppermute | solution.py:304
  173.2 8.4 %collective-permute-start.5 = (bf16[96,768]{1,0:T(8,128)(2,1)}, bf16[96,768]{1,0:T(8,128)(2,1)S(1)}, u32[]{:S(2)}, u32[]{:S(2)}) collective-permute-start(bf16[96,768]{1,0:T(8,128)(2,1)} %get-tuple-element.26), channel_id=1, source_target_pairs={{0,3},{1,0},{2,1},{3,2},{4,7},{5,4},{6,5},{7,6},{8,11},{9,8},{10,9... | collective-permute-start | bytes 442376 | tf_op jit(solution)/shard_map/ppermute | solution.py:304
  175.6 6.0 %copy-start.16 = (bf16[96,768]{1,0:T(8,128)(2,1)}, bf16[96,768]{1,0:T(8,128)(2,1)S(1)}, u32[]{:S(2)}) copy-start(bf16[96,768]{1,0:T(8,128)(2,1)S(1)} %collective-permute-done.3.b_ref) | copy-start | bytes 442372
  184.2 32.9 %copy-start.28 = (s32[64,2]{0,1:T(2,128)S(1)}, s32[64,2]{0,1:T(2,128)}, u32[]{:S(2)}) copy-start(s32[64,2]{0,1:T(2,128)} %param.9) | copy-start | bytes 1540
  184.2 33.6 %copy-start.4 = (bf16[128,1024]{1,0:T(8,128)(2,1)S(1)}, bf16[128,1024]{1,0:T(8,128)(2,1)}, u32[]{:S(2)}) copy-start(bf16[128,1024]{1,0:T(8,128)(2,1)} %get-tuple-element.36) | copy-start | bytes 786436
  184.2 33.6 %copy-start.12 = (bf16[128,768]{1,0:T(8,128)(2,1)S(1)}, bf16[128,768]{1,0:T(8,128)(2,1)}, u32[]{:S(2)}) copy-start(bf16[128,768]{1,0:T(8,128)(2,1)} %get-tuple-element.37) | copy-start | bytes 589828
  184.2 5.5 %collective-permute-start.6 = (bf16[96,768]{1,0:T(8,128)(2,1)}, bf16[96,768]{1,0:T(8,128)(2,1)S(1)}, u32[]{:S(2)}, u32[]{:S(2)}) collective-permute-start(bf16[96,768]{1,0:T(8,128)(2,1)} %middle.2.refs_0_), channel_id=1, source_target_pairs={{0,1},{1,2},{2,3},{3,0},{4,5},{5,6},{6,7},{7,4},{8,9},{9,10},{10,1... | collective-permute-start | bytes 442376 | tf_op jit(solution)/shard_map/ppermute | solution.py:304
  185.1 7.4 %collective-permute-start.7 = (bf16[96,768]{1,0:T(8,128)(2,1)}, bf16[96,768]{1,0:T(8,128)(2,1)S(1)}, u32[]{:S(2)}, u32[]{:S(2)}) collective-permute-start(bf16[96,768]{1,0:T(8,128)(2,1)} %middle.2.refs_0_), channel_id=1, source_target_pairs={{0,2},{1,3},{2,0},{3,1},{4,6},{5,7},{6,4},{7,5},{8,10},{9,11},{10,... | collective-permute-start | bytes 442376 | tf_op jit(solution)/shard_map/ppermute | solution.py:304
  187.0 6.5 %collective-permute-start.8 = (bf16[96,768]{1,0:T(8,128)(2,1)}, bf16[96,768]{1,0:T(8,128)(2,1)S(1)}, u32[]{:S(2)}, u32[]{:S(2)}) collective-permute-start(bf16[96,768]{1,0:T(8,128)(2,1)} %middle.2.refs_0_), channel_id=1, source_target_pairs={{0,3},{1,0},{2,1},{3,2},{4,7},{5,4},{6,5},{7,6},{8,11},{9,8},{10,9... | collective-permute-start | bytes 442376 | tf_op jit(solution)/shard_map/ppermute | solution.py:304
  189.7 3.7 %copy-start.13 = (bf16[96,768]{1,0:T(8,128)(2,1)}, bf16[96,768]{1,0:T(8,128)(2,1)S(1)}, u32[]{:S(2)}) copy-start(bf16[96,768]{1,0:T(8,128)(2,1)S(1)} %collective-permute-done.6.refs_1_) | copy-start | bytes 442372
  197.3 21.2 %copy-start.3 = (bf16[128,8,128]{2,1,0:T(8,128)(2,1)}, bf16[128,8,128]{2,1,0:T(8,128)(2,1)S(1)}, u32[]{:S(2)}) copy-start(bf16[128,8,128]{2,1,0:T(8,128)(2,1)S(1)} %all-to-all-done.3.refs_1_) | copy-start | bytes 786436
  197.3 63.1 %all-to-all-start.1 = ((bf16[128,8,384]{2,1,0:T(8,128)(2,1)}), bf16[128,8,384]{2,1,0:T(8,128)(2,1)S(1)}, u32[]{:S(2)}, u32[]{:S(2)}) async-start(bf16[128,8,384]{2,1,0:T(8,128)(2,1)} %get-tuple-element.27), calls=%async_computation.1 | async-start | bytes 1572864 | tf_op jit(solution)/shard_map/all_to_all | solution.py:321
  219.4 6.1 %copy-start.2 = (bf16[384,1024]{1,0:T(8,128)(2,1)S(1)}, bf16[384,1024]{1,0:T(8,128)(2,1)}, u32[]{:S(2)}) copy-start(bf16[384,1024]{1,0:T(8,128)(2,1)} %get-tuple-element.34) | copy-start | bytes 2359300
  220.6 7.5 %collective-permute-start.15 = (bf16[64,1024]{1,0:T(8,128)(2,1)S(1)}, bf16[64,1024]{1,0:T(8,128)(2,1)S(1)}, u32[]{:S(2)}, u32[]{:S(2)}) collective-permute-start(bf16[64,1024]{1,0:T(8,128)(2,1)S(1)} %get-tuple-element.42), channel_id=1, source_target_pairs={{0,1},{1,2},{2,3},{3,0},{4,5},{5,6},{6,7},{7,4},{8,9},{9,10},{10,1... | collective-permute-start | bytes 393224 | tf_op jit(solution)/shard_map/ppermute | solution.py:304
  222.0 10.0 %collective-permute-start.16 = (bf16[64,1024]{1,0:T(8,128)(2,1)S(1)}, bf16[64,1024]{1,0:T(8,128)(2,1)S(1)}, u32[]{:S(2)}, u32[]{:S(2)}) collective-permute-start(bf16[64,1024]{1,0:T(8,128)(2,1)S(1)} %get-tuple-element.41), channel_id=1, source_target_pairs={{0,2},{1,3},{2,0},{3,1},{4,6},{5,7},{6,4},{7,5},{8,10},{9,11},{10,... | collective-permute-start | bytes 393224 | tf_op jit(solution)/shard_map/ppermute | solution.py:304
  224.4 7.6 %collective-permute-start.17 = (bf16[64,1024]{1,0:T(8,128)(2,1)S(1)}, bf16[64,1024]{1,0:T(8,128)(2,1)S(1)}, u32[]{:S(2)}, u32[]{:S(2)}) collective-permute-start(bf16[64,1024]{1,0:T(8,128)(2,1)S(1)} %get-tuple-element.40), channel_id=1, source_target_pairs={{0,3},{1,0},{2,1},{3,2},{4,7},{5,4},{6,5},{7,6},{8,11},{9,8},{10,9... | collective-permute-start | bytes 393224 | tf_op jit(solution)/shard_map/ppermute | solution.py:304
  228.1 3.9 %copy-start.19 = (bf16[64,1024]{1,0:T(8,128)(2,1)}, bf16[64,1024]{1,0:T(8,128)(2,1)S(1)}, u32[]{:S(2)}) copy-start(bf16[64,1024]{1,0:T(8,128)(2,1)S(1)} %collective-permute-done.15.refs_1_) | copy-start | bytes 393220
  (18 other events, 17.3 us)

commit v2 on v1

v2 whole, which is shorter than its diff:
```python
import functools

import jax
import jax.numpy as jnp
from jax import lax
from jax.experimental import pallas as pl
from jax.experimental.pallas import tpu as pltpu
from jax.sharding import PartitionSpec as P

BF = jnp.bfloat16
F32 = jnp.float32
VMEM = pl.BlockSpec(memory_space=pltpu.VMEM)
SMEM = pl.BlockSpec(memory_space=pltpu.SMEM)
SPLIT = (2, 2)
PARTS = 4
STEPS = 4


def cost(flops, bytes_accessed):
    return pl.CostEstimate(flops=int(flops), bytes_accessed=int(bytes_accessed), transcendentals=0)


def nn(a, b):
    return lax.dot_general(a, b, (((1,), (0,)), ((), ())), preferred_element_type=F32)


def nt(a, b):
    return lax.dot_general(a, b, (((1,), (1,)), ((), ())), preferred_element_type=F32)


def tn(a, b):
    return lax.dot_general(a, b, (((0,), (0,)), ((), ())), preferred_element_type=F32)


def dispatch_kernel(split, ids_ref, gate_ref, *refs):
    sources, refs = refs[:8], refs[8:]
    outs, (pick_ref, scale_ref) = refs[: len(split)], refs[len(split) :]
    n_tok, lanes = sources[0].shape
    experts = outs[0].shape[0]
    rows = experts * 8
    slots = sum(split)

    @pl.when(pl.program_id(0) == 0)
    def _():
        row = lax.broadcasted_iota(jnp.int32, (rows, n_tok), 0)
        expert = row // 8
        first = ids_ref[0:1, :] == expert
        second = ids_ref[1:2, :] == expert
        member = jnp.where(first | second, 1.0, 0.0).astype(F32)
        j = lax.broadcasted_iota(jnp.int32, (n_tok, n_tok), 0)
        i = lax.broadcasted_iota(jnp.int32, (n_tok, n_tok), 1)
        before = nn(member.astype(BF), jnp.where(j < i, 1.0, 0.0).astype(BF))
        gates = jnp.where(first, gate_ref[0:1, :], gate_ref[1:2, :])
        is_cot = row % 2 == 1
        wide = lax.broadcasted_iota(jnp.int32, (rows, 2 * n_tok), 0)
        part = (wide % 8) // 2
        for p in range(slots):
            chosen = jnp.where(before == float(p), member, 0.0)
            weight = jnp.sum(chosen * gates, axis=1, keepdims=True)
            scale_ref[p] = jnp.where(is_cot[:, :1], weight, 1.0)
            kept = jnp.concatenate([jnp.where(is_cot, 0.0, chosen), jnp.where(is_cot, chosen, 0.0)], axis=1)
            for q in range(4):
                pick_ref[p, :, q * 2 * n_tok : (q + 1) * 2 * n_tok] = jnp.where(part == q, kept, 0.0).astype(BF)

    source = jnp.concatenate([s[...] for s in sources], axis=0)
    p = 0
    for out, count in zip(outs, split):
        for k in range(count):
            picked = nn(pick_ref[p], source) * scale_ref[p]
            out[:, :, k * lanes : (k + 1) * lanes] = picked.reshape(experts, 8, lanes).astype(BF)
            p += 1


def dispatch(ids2, gates2, tokens, cotangent, experts, split):
    n_tok, d = tokens.shape
    lanes = d // 4 // STEPS
    rows = experts * 8
    slots = sum(split)
    columns = []
    for q in range(4):
        columns += [pl.BlockSpec((n_tok, lanes), lambda i, q=q: (0, q * STEPS + i))] * 2
    return pl.pallas_call(
        functools.partial(dispatch_kernel, split),
        grid=(STEPS,),
        in_specs=[pl.BlockSpec((2, n_tok), lambda i: (0, 0))] * 2 + columns,
        out_specs=[pl.BlockSpec((experts, 8, c * lanes), lambda i: (0, 0, i)) for c in split],
        out_shape=[jax.ShapeDtypeStruct((experts, 8, c * d // 4), BF) for c in split],
        scratch_shapes=[pltpu.VMEM((slots, rows, 8 * n_tok), BF), pltpu.VMEM((slots, rows, 1), F32)],
        cost_estimate=cost(2 * slots * rows * 8 * n_tok * d // 4, 4 * n_tok * d * 2 + 2 * slots * experts * d * 2),
        name="dispatch",
    )(ids2, gates2, *([tokens, cotangent] * 4))


def expert_kernel(count, t_ref, recv_ref, *refs):
    wg, wu, wds, refs = refs[:PARTS], refs[PARTS : 2 * PARTS], refs[2 * PARTS : 3 * PARTS], refs[3 * PARTS :]
    msg_ref, exchange, (flat, x, c, wd, back, ret) = refs[0], refs[1 : 1 + PARTS], refs[1 + PARTS :]
    t = t_ref[0]
    width, ff = wg[0].shape
    ff_part, d_model = wds[0].shape
    sources = recv_ref.shape[0]
    rows = count * sources
    lanes = d_model // 4 // STEPS
    blocks = lanes // 128
    part = [lax.rem(t - k + PARTS, PARTS) for k in range(PARTS)]
    for k in range(PARTS):
        wd[pl.ds(pl.multiple_of(part[k] * ff_part, ff_part), ff_part), :] = wds[k][...]
    for b in range(flat.shape[0]):
        flat[b] = recv_ref[:, :, b * 128 : (b + 1) * 128].astype(F32).reshape(flat.shape[1:])
    for step in range(STEPS):
        for p in range(count):
            for b in range(blocks):
                for q in range(4):
                    col = q * (d_model // 4) + step * lanes + b * 128
                    for kind, dst in ((0, x), (1, c)):
                        v = flat[(step * count + p) * blocks + b, pl.ds(2 * q + kind, sources, stride=8), :]
                        dst[p * sources : (p + 1) * sources, col : col + 128] = v.astype(BF)
    cols = [pl.ds(pl.multiple_of(part[k] * width, width), width) for k in range(PARTS)]
    pre_gate = functools.reduce(lambda a, b: a + b, [nn(x[:, cols[k]], wg[k][...]) for k in range(PARTS)])
    pre_up = functools.reduce(lambda a, b: a + b, [nn(x[:, cols[k]], wu[k][...]) for k in range(PARTS)])
    grad_hidden = nt(c[...], wd[...])
    sig = jax.nn.sigmoid(pre_gate)
    activated = pre_gate * sig
    hidden = (activated * pre_up).astype(BF)
    grad_gate_pre = (grad_hidden * pre_up * sig * (1.0 + pre_gate * (1.0 - sig))).astype(BF)
    grad_up_pre = (grad_hidden * activated).astype(BF)
    for k in range(PARTS):
        to = lax.rem(t + k, PARTS)
        there = pl.ds(pl.multiple_of(to * width, width), width)
        exchange[k][0:rows, :] = x[:, there]
        exchange[k][rows : 2 * rows, :] = c[:, there]
        exchange[k][2 * rows :, 0:ff] = hidden
        exchange[k][2 * rows :, ff : 2 * ff] = grad_gate_pre
        exchange[k][2 * rows :, 2 * ff : 3 * ff] = grad_up_pre
        exchange[k][2 * rows :, 3 * ff :] = jnp.zeros((rows, width - 3 * ff), BF)
    for k in range(PARTS):
        back[:, cols[k]] = nt(grad_gate_pre, wg[k][...]) + nt(grad_up_pre, wu[k][...])
    eighth = d_model // 8
    for p in range(count):
        for b in range(eighth // 128):
            for o in range(8):
                col = o * eighth + b * 128
                ret[p * (eighth // 128) + b, pl.ds(o, sources, stride=8), :] = back[
                    p * sources : (p + 1) * sources, col : col + 128
                ]
    for b in range(ret.shape[0]):
        msg_ref[:, :, b * 128 : (b + 1) * 128] = ret[b].reshape(sources, 8, 128).astype(BF)


def expert_round(t, recv, wg, wu, wd, count):
    sources = recv.shape[0]
    width, ff = wg[0].shape
    ff_part, d = wd[0].shape
    rows = sources * count
    return pl.pallas_call(
        functools.partial(expert_kernel, count),
        in_specs=[SMEM] + [VMEM] * (1 + 3 * PARTS),
        out_specs=[VMEM] * (1 + PARTS),
        out_shape=[jax.ShapeDtypeStruct((sources, 8, count * d // 8), BF)]
        + [jax.ShapeDtypeStruct((3 * rows, width), BF)] * PARTS,
        scratch_shapes=[
            pltpu.VMEM((count * d // 4 // 128, sources * 8, 128), F32),
            pltpu.VMEM((rows, d), BF),
            pltpu.VMEM((rows, d), BF),
            pltpu.VMEM((ff, d), BF),
            pltpu.VMEM((rows, d), F32),
            pltpu.VMEM((count * d // 8 // 128, sources * 8, 128), F32),
        ],
        cost_estimate=cost(2 * rows * d * 5 * ff, 3 * ff * d * 2 + 5 * rows * d * 2),
        name="expert_round",
    )(t, recv, *wg, *wu, *wd)


def grads_kernel(ff, t_ref, *refs):
    n = len(refs) - (2 + PARTS) - 3
    boxes, (gg_ref, gu_ref), downs, (x, c, h) = refs[:n], refs[n : n + 2], refs[n + 2 : n + 2 + PARTS], refs[-3:]
    at = 0
    for box in boxes:
        rows = box.shape[0] // 3
        x[at : at + rows, :] = box[0:rows, :]
        c[at : at + rows, :] = box[rows : 2 * rows, :]
        h[at : at + rows, :] = box[2 * rows :, 0 : 3 * ff]
        at += rows
    gg_ref[...] = tn(x[...], h[:, ff : 2 * ff]).astype(BF)
    gu_ref[...] = tn(x[...], h[:, 2 * ff :]).astype(BF)
    hidden = h[:, 0:ff]
    down = tn(hidden, c[...]).astype(BF)
    x[0:ff, :] = down
    part = ff // PARTS
    for k in range(PARTS):
        downs[k][...] = x[pl.ds(pl.multiple_of(lax.rem(t_ref[0] + k, PARTS) * part, part), part), :]


def grads(t, boxes, ff):
    width = boxes[0].shape[1]
    rows = sum(b.shape[0] for b in boxes) // 3
    return pl.pallas_call(
        functools.partial(grads_kernel, ff),
        in_specs=[SMEM] + [VMEM] * len(boxes),
        out_specs=[VMEM] * (2 + PARTS),
        out_shape=[jax.ShapeDtypeStruct((width, ff), BF)] * 2
        + [jax.ShapeDtypeStruct((ff // PARTS, width), BF)] * PARTS,
        scratch_shapes=[
            pltpu.VMEM((rows, width), BF),
            pltpu.VMEM((rows, width), BF),
            pltpu.VMEM((rows, 3 * ff), BF),
        ],
        cost_estimate=cost(2 * rows * width * 3 * ff, 3 * rows * width * 2 + 3 * width * ff * 2),
        name="grads",
    )(t, *boxes)


def combine_kernel(split, ids_ref, *refs):
    rets, refs = refs[: len(split)], refs[len(split) :]
    out_ref, flats, rhs = refs[0], refs[1 : 1 + len(split)], refs[1 + len(split)]
    n_tok, d = out_ref.shape
    slots = sum(split)
    experts = rets[0].shape[0]
    eighth = d // 8
    blocks = eighth // 128
    lane = lax.broadcasted_iota(jnp.int32, (n_tok, slots * experts), 1)
    expert = lane % experts
    member = jnp.where((ids_ref[:, 0:1] == expert) | (ids_ref[:, 1:2] == expert), 1.0, 0.0).astype(F32)
    i = lax.broadcasted_iota(jnp.int32, (n_tok, n_tok), 0)
    j = lax.broadcasted_iota(jnp.int32, (n_tok, n_tok), 1)
    before = nn(jnp.where(j < i, 1.0, 0.0).astype(BF), member.astype(BF))
    pick = jnp.where(before == (lane // experts).astype(F32), member, 0.0).astype(BF)
    for ret, flat in zip(rets, flats):
        for b in range(flat.shape[0]):
            flat[b] = ret[:, :, b * 128 : (b + 1) * 128].astype(F32).reshape(flat.shape[1:])
    for o in range(8):
        for b in range(blocks):
            col = o * eighth + b * 128
            p = 0
            for flat, count in zip(flats, split):
                for k in range(count):
                    v = flat[k * blocks + b, pl.ds(o, experts, stride=8), :]
                    rhs[p * experts : (p + 1) * experts, col : col + 128] = v.astype(BF)
                    p += 1
    out_ref[...] = nn(pick, rhs[...]).astype(BF)


def combine(ids, rets, split, d):
    n_tok = ids.shape[0]
    slots = sum(split)
    experts = rets[0].shape[0]
    return pl.pallas_call(
        functools.partial(combine_kernel, split),
        in_specs=[VMEM] * (1 + len(split)),
        out_specs=VMEM,
        out_shape=jax.ShapeDtypeStruct((n_tok, d), BF),
        scratch_shapes=[pltpu.VMEM((c * d // 8 // 128, r.shape[0] * 8, 128), F32) for c, r in zip(split, rets)]
        + [pltpu.VMEM((slots * experts, d), BF)],
        cost_estimate=cost(2 * n_tok * slots * experts * d, 4 * n_tok * d * 2),
        name="combine",
    )(ids, *rets)


def place_kernel(t_ref, *refs):
    out = refs[-1]
    width = refs[0].shape[1]
    for k in range(PARTS):
        at = pl.multiple_of(lax.rem(t_ref[0] - k + PARTS, PARTS) * width, width)
        out[:, pl.ds(at, width)] = refs[k][...]


def place(t, pieces):
    rows, width = pieces[0].shape
    return pl.pallas_call(
        place_kernel,
        in_specs=[SMEM] + [VMEM] * len(pieces),
        out_specs=VMEM,
        out_shape=jax.ShapeDtypeStruct((rows, width * len(pieces)), BF),
        cost_estimate=cost(rows * width, 4 * rows * width * 4),
        name="place",
    )(t, *pieces)


def local(tokens, cotangent, expert_ids, gate_wts, w_gate, w_up, w_down):
    n_tok, d = tokens.shape
    experts = lax.axis_size("expert")
    slots = 2 * n_tok // experts
    split = SPLIT if sum(SPLIT) == slots else (slots,)
    t = lax.axis_index("tensor").astype(jnp.int32).reshape(1)
    ff = w_gate.shape[2]

    def shift(x, k):
        return lax.ppermute(x, "tensor", [(s, (s + k) % PARTS) for s in range(PARTS)])

    def everyone(x):
        return [x] + [shift(x, k) for k in range(1, PARTS)]

    sends = dispatch(expert_ids.T, gate_wts.T, tokens, cotangent, experts, split)
    recvs = []
    for r, send in enumerate(sends):
        with jax.named_scope(f"inbound{r}"):
            recvs.append(lax.all_to_all(send, "expert", 0, 0, tiled=True))
    wg, wu, wd = everyone(w_gate[0]), everyone(w_up[0]), everyone(w_down[0])
    boxes, rets = [], []
    for r, (recv, count) in enumerate(zip(recvs, split)):
        with jax.named_scope(f"round{r}"):
            msg, *box = expert_round(t, recv, wg, wu, wd, count)
        with jax.named_scope(f"outbound{r}"):
            rets.append(lax.all_to_all(msg, "expert", 0, 0, tiled=True))
        with jax.named_scope(f"exchange{r}"):
            boxes += [box[0]] + [shift(box[k], k) for k in range(1, PARTS)]
    grad_gate, grad_up, *down = grads(t, boxes, ff)
    grad_down = place(t, [down[0]] + [shift(down[k], k) for k in range(1, PARTS)])
    input_grad = combine(expert_ids, rets, split, d)
    return input_grad, grad_gate[None], grad_up[None], grad_down[None]


def solution(mesh):
    tok = P(("group", "expert", "tensor"), None)
    wts = P("expert", "tensor", None)
    out = P(("group", "expert"), "tensor", None)

    return jax.shard_map(
        local,
        mesh=mesh,
        in_specs=(tok, tok, tok, tok, wts, wts, wts),
        out_specs=(tok, out, out, out),
        check_vma=False,
    )
```

time: 266 us -> 284 us (1.068)
  waiting for transfers between devices: 95.7 us -> 123 us
  starting transfers between devices: 64.1 us -> 42.7 us
  blocking collectives: 63.5 us -> 81.1 us
  local copies, waits for them, and re-layouts: 10.3 us -> 4.55 us
  Pallas kernels: 26.6 us -> 30.9 us
  matrix products: 3.96 us -> 0 us
    ppermute x18, waiting for transfers between devices: 28.5 us -> 98 us  [shift(): lax.ppermute(x, 'tensor', [(s, (s + k) % PARTS) for s in range(PARTS)])]
    all_to_all x3, waiting for transfers between devices: 67.2 us -> 24.5 us  [the longest x2 24.5 us: local(): rets.append(lax.all_to_all(msg, 'expert', 0, 0, tiled=True))]
    all_to_all x1, blocking collectives: 63.5 us -> 81.1 us  [local(): recvs.append(lax.all_to_all(send, 'expert', 0, 0, tiled=True))]
    all_to_all x3, starting transfers between devices: 37.4 us -> 23 us  [the longest x2 18.5 us: local(): rets.append(lax.all_to_all(msg, 'expert', 0, 0, tiled=True))]
    ppermute x18, starting transfers between devices: 26.7 us -> 19.7 us  [shift(): lax.ppermute(x, 'tensor', [(s, (s + k) % PARTS) for s in range(PARTS)])]
    pallas_call x8 -> x5, Pallas kernels: 24.7 us -> 29 us  [the longest x2 17.4 us: expert_round(): pl.pallas_call(functools.partial(expert_kernel, count), in_specs=[SMEM] +...]
    dot_general x6 -> x0, matrix products: 3.96 us -> none  [tn(): lax.dot_general(a, b, (((0,), (0,)), ((), ())), preferred_element_type=F32)]
    unnamed x59 -> x47, local copies, waits for them, and re-layouts: 6.29 us -> 4.55 us
  transfers between devices with their start and end apart: 21 -> 21, of which waited for: 16 -> 18; matrix products, arithmetic and copies ran while one was open for 2% -> 0% of each run, Pallas kernels for 7% -> 8%
where the time goes in v2:
time: 284 us; the launch traced here: 282 us
  waiting for transfers between devices  123 us (43%)
  blocking collectives  81.1 us (29%)
  starting transfers between devices  42.7 us (15%)
  Pallas kernels  30.9 us (11%)
  local copies, waits for them, and re-layouts  4.55 us (2%)
    ppermute x18, waiting for transfers between devices, shift(): lax.ppermute(x, 'tensor', [(s, (s + k) % PARTS) for s in range(PARTS)])  98 us
    all_to_all x1, blocking collectives, local(): recvs.append(lax.all_to_all(send, 'expert', 0, 0, tiled=True))  81.1 us
    all_to_all x2, waiting for transfers between devices, local(): rets.append(lax.all_to_all(msg, 'expert', 0, 0, tiled=True))  24.5 us
    ppermute x18, starting transfers between devices, shift(): lax.ppermute(x, 'tensor', [(s, (s + k) % PARTS) for s in range(PARTS)])  19.7 us
    all_to_all x2, starting transfers between devices, local(): rets.append(lax.all_to_all(msg, 'expert', 0, 0, tiled=True))  18.5 us
    pallas_call x2, Pallas kernels, expert_round(): pl.pallas_call(functools.partial(expert_kernel, count), in_specs=[SMEM] +...  17.4 us
  transfers between devices with their start and end apart: 21, of which 18 were waited for; matrix products, arithmetic and copies ran while one was open for 0% of the time, Pallas kernels for 8%

profile of v2, /device:TPU:33, one launch (start us, length us, event | category | flops | bytes accessed | tf_op | source)
XLA Modules:
  0.0 282.5 jit_solution(2857411516965229776)
XLA Ops:
  0.6 4.9 %dispatch.1 = (bf16[32,8,2048]{2,1,0:T(8,128)(2,1)}, bf16[32,8,2048]{2,1,0:T(8,128)(2,1)}) custom-call(s32[2,64]{1,0:T(2,128)} %bitcast.25, f32[2,64]{1,0:T(2,128)} %bitcast.26, bf16[64,4096]{1,0:T(8,128)(2,1)} %refs_6_.1, bf16[64,4096]{1,0:T(8,128)(2,1)} %refs_7_.1, bf16[64,4096]{1,0:T(8,128)(2,1)} %refs_6_.1, bf16[64,4096]{1,0:T(8,128)(2,1)} %refs_7_.1, ...), custom_call_target="tpu_custom_call" | custom-call | flops 1073741824 | bytes 4194304 | tf_op jit(solution)/shard_map/dispatch/pallas_call | solution.py:82
  5.5 81.1 %all_to_all.20.recv_ref = bf16[32,8,2048]{2,1,0:T(8,128)(2,1)} all-to-all(bf16[32,8,2048]{2,1,0:T(8,128)(2,1)} %get-tuple-element.22), channel_id=1, replica_groups=mesh['group'=2,'expert'=32,'tensor'=4] {'expert'}, dimensions={0} | all-to-all | bytes 2097152 | tf_op jit(solution)/shard_map/inbound0/all_to_all | solution.py:296
  86.6 4.5 %all-to-all-start.2 = ((bf16[32,8,2048]{2,1,0:T(8,128)(2,1)}), bf16[32,8,2048]{2,1,0:T(8,128)(2,1)S(1)}, u32[]{:S(2)}, u32[]{:S(2)}) async-start(bf16[32,8,2048]{2,1,0:T(8,128)(2,1)} %get-tuple-element.24), calls=%async_computation.2 | async-start | bytes 2097152 | tf_op jit(solution)/shard_map/inbound1/all_to_all | solution.py:296
  91.1 1.5 collective-permute-start
  92.5 2.7 collective-permute-start.1
  97.5 7.8 %collective-permute-done.refs_1_ = bf16[1024,256]{1,0:T(8,128)(2,1)S(1)} collective-permute-done((bf16[1024,256]{1,0:T(8,128)(2,1)S(1)}, bf16[1024,256]{1,0:T(8,128)(2,1)S(1)}, u32[]{:S(2)}, u32[]{:S(2)}) %collective-permute-start) | collective-permute-done | bytes 524320 | tf_op jit(solution)/shard_map/ppermute | solution.py:287
  106.5 11.0 %collective-permute-done.1.refs_2_ = bf16[1024,256]{1,0:T(8,128)(2,1)S(1)} collective-permute-done((bf16[1024,256]{1,0:T(8,128)(2,1)S(1)}, bf16[1024,256]{1,0:T(8,128)(2,1)S(1)}, u32[]{:S(2)}, u32[]{:S(2)}) %collective-permute-start.1) | collective-permute-done | bytes 524320 | tf_op jit(solution)/shard_map/ppermute | solution.py:287
  118.2 1.3 collective-permute-start.7
  119.5 8.3 %collective-permute-done.3.refs_5_ = bf16[1024,256]{1,0:T(8,128)(2,1)S(1)} collective-permute-done((bf16[1024,256]{1,0:T(8,128)(2,1)S(1)}, bf16[1024,256]{1,0:T(8,128)(2,1)S(1)}, u32[]{:S(2)}, u32[]{:S(2)}) %collective-permute-start.3) | collective-permute-done | bytes 524320 | tf_op jit(solution)/shard_map/ppermute | solution.py:287
  127.8 1.4 collective-permute-start.8
  129.2 11.0 %collective-permute-done.4.refs_6_ = bf16[1024,256]{1,0:T(8,128)(2,1)} collective-permute-done((bf16[1024,256]{1,0:T(8,128)(2,1)S(1)}, bf16[1024,256]{1,0:T(8,128)(2,1)}, u32[]{:S(2)}, u32[]{:S(2)}) %collective-permute-start.4) | collective-permute-done | bytes 524320 | tf_op jit(solution)/shard_map/ppermute | solution.py:287
  140.7 9.7 %collective-permute-done.6.refs_9_ = bf16[64,4096]{1,0:T(8,128)(2,1)} collective-permute-done((bf16[64,4096]{1,0:T(8,128)(2,1)S(1)}, bf16[64,4096]{1,0:T(8,128)(2,1)}, u32[]{:S(2)}, u32[]{:S(2)}) %collective-permute-start.6) | collective-permute-done | bytes 524320 | tf_op jit(solution)/shard_map/ppermute | solution.py:287
  150.4 12.2 %collective-permute-done.7.refs_10_ = bf16[64,4096]{1,0:T(8,128)(2,1)S(1)} collective-permute-done((bf16[64,4096]{1,0:T(8,128)(2,1)S(1)}, bf16[64,4096]{1,0:T(8,128)(2,1)S(1)}, u32[]{:S(2)}, u32[]{:S(2)}) %collective-permute-start.7) | collective-permute-done | bytes 524320 | tf_op jit(solution)/shard_map/ppermute | solution.py:287
  163.3 8.6 %expert_round.2 = (bf16[32,8,1024]{2,1,0:T(8,128)(2,1)}, bf16[192,1024]{1,0:T(8,128)(2,1)}, bf16[192,1024]{1,0:T(8,128)(2,1)}, bf16[192,1024]{1,0:T(8,128)(2,1)}, bf16[192,1024]{1,0:T(8,128)(2,1)}) custom-call(s32[1]{0:T(128)} %bitcast.t_ref, bf16[32,8,2048]{2,1,0:T(8,128)(2,1)} %all_to_all.20.recv_ref, bf16[1024,256]{1,0:T(8,128)(2,1)} %bitcast.9, ...), custom_call_target="tpu_custom_call" | custom-call | flops 671088640 | bytes 8912896 | tf_op jit(solution)/shard_map/round0/expert_round/pallas_call | solution.py:154
  172.0 14.2 %all-to-all-start.1 = ((bf16[32,8,1024]{2,1,0:T(8,128)(2,1)}), bf16[32,8,1024]{2,1,0:T(8,128)(2,1)S(1)}, u32[]{:S(2)}, u32[]{:S(2)}) async-start(bf16[32,8,1024]{2,1,0:T(8,128)(2,1)} %get-tuple-element.23), calls=%async_computation.1 | async-start | bytes 1048576 | tf_op jit(solution)/shard_map/outbound0/all_to_all | solution.py:303
  186.2 8.8 %expert_round.3 = (bf16[32,8,1024]{2,1,0:T(8,128)(2,1)}, bf16[192,1024]{1,0:T(8,128)(2,1)}, bf16[192,1024]{1,0:T(8,128)(2,1)}, bf16[192,1024]{1,0:T(8,128)(2,1)}, bf16[192,1024]{1,0:T(8,128)(2,1)}) custom-call(s32[1]{0:T(128)} %bitcast.t_ref, bf16[32,8,2048]{2,1,0:T(8,128)(2,1)} %copy-done, bf16[1024,256]{1,0:T(8,128)(2,1)} %bitcast.10, ...), custom_call_target="tpu_custom_call" | custom-call | flops 671088640 | bytes 8912896 | tf_op jit(solution)/shard_map/round1/expert_round/pallas_call | solution.py:154
  195.0 24.5 %all-to-all-done.1.refs_0_ = bf16[32,8,1024]{2,1,0:T(8,128)(2,1)S(1)} async-done(((bf16[32,8,1024]{2,1,0:T(8,128)(2,1)}), bf16[32,8,1024]{2,1,0:T(8,128)(2,1)S(1)}, u32[]{:S(2)}, u32[]{:S(2)}) %all-to-all-start.1) | async-done | bytes 524320 | tf_op jit(solution)/shard_map/outbound0/all_to_all | solution.py:303
  220.3 4.3 %all-to-all-start.3 = ((bf16[32,8,1024]{2,1,0:T(8,128)(2,1)}), bf16[32,8,1024]{2,1,0:T(8,128)(2,1)S(1)}, u32[]{:S(2)}, u32[]{:S(2)}) async-start(bf16[32,8,1024]{2,1,0:T(8,128)(2,1)} %get-tuple-element.25), calls=%async_computation.3 | async-start | bytes 1048576 | tf_op jit(solution)/shard_map/outbound1/all_to_all | solution.py:303
  224.6 1.6 collective-permute-start.10
  227.7 1.5 collective-permute-start.13
  230.3 5.6 %collective-permute-done.10.refs_2_ = bf16[192,1024]{1,0:T(8,128)(2,1)S(1)} collective-permute-done((bf16[192,1024]{1,0:T(8,128)(2,1)S(1)}, bf16[192,1024]{1,0:T(8,128)(2,1)S(1)}, u32[]{:S(2)}, u32[]{:S(2)}) %collective-permute-start.10) | collective-permute-done | bytes 393248 | tf_op jit(solution)/shard_map/exchange0/ppermute | solution.py:287
  236.1 8.2 %collective-permute-done.11.refs_3_ = bf16[192,1024]{1,0:T(8,128)(2,1)S(1)} collective-permute-done((bf16[192,1024]{1,0:T(8,128)(2,1)}, bf16[192,1024]{1,0:T(8,128)(2,1)S(1)}, u32[]{:S(2)}, u32[]{:S(2)}) %collective-permute-start.11) | collective-permute-done | bytes 393248 | tf_op jit(solution)/shard_map/exchange0/ppermute | solution.py:287
  244.4 2.7 collective-permute-done.12.refs_5_
  247.1 5.8 %collective-permute-done.13.refs_6_ = bf16[192,1024]{1,0:T(8,128)(2,1)S(1)} collective-permute-done((bf16[192,1024]{1,0:T(8,128)(2,1)}, bf16[192,1024]{1,0:T(8,128)(2,1)S(1)}, u32[]{:S(2)}, u32[]{:S(2)}) %collective-permute-start.13) | collective-permute-done | bytes 393248 | tf_op jit(solution)/shard_map/exchange1/ppermute | solution.py:287
  252.8 7.5 %collective-permute-done.14.refs_7_ = bf16[192,1024]{1,0:T(8,128)(2,1)S(1)} collective-permute-done((bf16[192,1024]{1,0:T(8,128)(2,1)}, bf16[192,1024]{1,0:T(8,128)(2,1)S(1)}, u32[]{:S(2)}, u32[]{:S(2)}) %collective-permute-start.14) | collective-permute-done | bytes 393248 | tf_op jit(solution)/shard_map/exchange1/ppermute | solution.py:287
  260.4 2.2 collective-permute-done.9.refs_1_
  263.3 3.7 %grads.1 = (bf16[1024,256]{1,0:T(8,128)(2,1)}, bf16[1024,256]{1,0:T(8,128)(2,1)}, bf16[64,1024]{1,0:T(8,128)(2,1)}, bf16[64,1024]{1,0:T(8,128)(2,1)}, bf16[64,10...) custom-call(s32[1]{0:T(128)} %bitcast.t_ref, bf16[192,1024]{1,0:T(8,128)(2,1)} %get-tuple-element.26.refs_0_, ...), custom_call_target="tpu_custom_call" | custom-call | flops 805306368 | bytes 4718592 | tf_op jit(solution)/shard_map/grads/pallas_call | solution.py:196
  267.3 2.1 collective-permute-start.16
  271.3 1.9 collective-permute-done.15.refs_1_
  273.3 2.3 collective-permute-done.16.refs_2_
  276.8 1.9 place.1
  279.5 3.0 %combine.1 = bf16[64,4096]{1,0:T(8,128)(2,1)} custom-call(s32[64,2]{1,0:T(8,128)} %copy.11.ids_ref, bf16[32,8,1024]{2,1,0:T(8,128)(2,1)} %copy-done.1, bf16[32,8,1024]{2,1,0:T(8,128)(2,1)} %copy-done.2), custom_call_target="tpu_custom_call" | custom-call | flops 67108864 | bytes 2097152 | tf_op jit(solution)/shard_map/combine/pallas_call | solution.py:246
  (64 shorter events, 14.0 us)
Async XLA Ops:
  86.6 9.7 %copy-start.4 = (bf16[1,1024,256]{2,1,0:T(8,128)(2,1)S(1)}, bf16[1,1024,256]{2,1,0:T(8,128)(2,1)}, u32[]{:S(2)}) copy-start(bf16[1,1024,256]{2,1,0:T(8,128)(2,1)} %param.12) | copy-start | bytes 1572868
  86.6 30.9 %copy-start.5 = (bf16[1,64,4096]{2,1,0:T(8,128)(2,1)S(1)}, bf16[1,64,4096]{2,1,0:T(8,128)(2,1)}, u32[]{:S(2)}) copy-start(bf16[1,64,4096]{2,1,0:T(8,128)(2,1)} %param.13) | copy-start | bytes 1572868
  86.6 85.4 %all-to-all-start.2 = ((bf16[32,8,2048]{2,1,0:T(8,128)(2,1)}), bf16[32,8,2048]{2,1,0:T(8,128)(2,1)S(1)}, u32[]{:S(2)}, u32[]{:S(2)}) async-start(bf16[32,8,2048]{2,1,0:T(8,128)(2,1)} %get-tuple-element.24), calls=%async_computation.2 | async-start | bytes 2097152 | tf_op jit(solution)/shard_map/inbound1/all_to_all | solution.py:296
  91.1 14.2 %collective-permute-start = (bf16[1024,256]{1,0:T(8,128)(2,1)S(1)}, bf16[1024,256]{1,0:T(8,128)(2,1)S(1)}, u32[]{:S(2)}, u32[]{:S(2)}) collective-permute-start(bf16[1024,256]{1,0:T(8,128)(2,1)S(1)} %bitcast.11), channel_id=1, source_target_pairs={{0,1},{1,2},{2,3},{3,0},{4,5},{5,6},{6,7},{7,4},{8,9},{9,10},{10,1... | collective-permute-start | bytes 1572872 | tf_op jit(solution)/shard_map/ppermute | solution.py:287
  92.5 25.0 %collective-permute-start.1 = (bf16[1024,256]{1,0:T(8,128)(2,1)S(1)}, bf16[1024,256]{1,0:T(8,128)(2,1)S(1)}, u32[]{:S(2)}, u32[]{:S(2)}) collective-permute-start(bf16[1024,256]{1,0:T(8,128)(2,1)S(1)} %bitcast.12), channel_id=1, source_target_pairs={{0,2},{1,3},{2,0},{3,1},{4,6},{5,7},{6,4},{7,5},{8,10},{9,11},{10,... | collective-permute-start | bytes 1572872 | tf_op jit(solution)/shard_map/ppermute | solution.py:287
  95.3 23.0 %collective-permute-start.2 = (bf16[1024,256]{1,0:T(8,128)(2,1)S(1)}, bf16[1024,256]{1,0:T(8,128)(2,1)S(1)}, u32[]{:S(2)}, u32[]{:S(2)}) collective-permute-start(bf16[1024,256]{1,0:T(8,128)(2,1)S(1)} %bitcast.13), channel_id=1, source_target_pairs={{0,3},{1,0},{2,1},{3,2},{4,7},{5,4},{6,5},{7,6},{8,11},{9,8},{10,9... | collective-permute-start | bytes 1572872 | tf_op jit(solution)/shard_map/ppermute | solution.py:287
  96.3 31.5 %collective-permute-start.3 = (bf16[1024,256]{1,0:T(8,128)(2,1)S(1)}, bf16[1024,256]{1,0:T(8,128)(2,1)S(1)}, u32[]{:S(2)}, u32[]{:S(2)}) collective-permute-start(bf16[1024,256]{1,0:T(8,128)(2,1)S(1)} %bitcast.16), channel_id=1, source_target_pairs={{0,1},{1,2},{2,3},{3,0},{4,5},{5,6},{6,7},{7,4},{8,9},{9,10},{10,1... | collective-permute-start | bytes 1572872 | tf_op jit(solution)/shard_map/ppermute | solution.py:287
  96.7 43.4 %collective-permute-start.4 = (bf16[1024,256]{1,0:T(8,128)(2,1)S(1)}, bf16[1024,256]{1,0:T(8,128)(2,1)}, u32[]{:S(2)}, u32[]{:S(2)}) collective-permute-start(bf16[1024,256]{1,0:T(8,128)(2,1)S(1)} %bitcast.17), channel_id=1, source_target_pairs={{0,2},{1,3},{2,0},{3,1},{4,6},{5,7},{6,4},{7,5},{8,10},{9,11},{10,... | collective-permute-start | bytes 1572872 | tf_op jit(solution)/shard_map/ppermute | solution.py:287
  105.3 57.2 %copy-start.6 = (bf16[1024,256]{1,0:T(8,128)(2,1)}, bf16[1024,256]{1,0:T(8,128)(2,1)S(1)}, u32[]{:S(2)}) copy-start(bf16[1024,256]{1,0:T(8,128)(2,1)S(1)} %collective-permute-done.refs_1_) | copy-start | bytes 1572868
  105.3 35.4 %collective-permute-start.5 = (bf16[1024,256]{1,0:T(8,128)(2,1)S(1)}, bf16[1024,256]{1,0:T(8,128)(2,1)}, u32[]{:S(2)}, u32[]{:S(2)}) collective-permute-start(bf16[1024,256]{1,0:T(8,128)(2,1)S(1)} %bitcast.18), channel_id=1, source_target_pairs={{0,3},{1,0},{2,1},{3,2},{4,7},{5,4},{6,5},{7,6},{8,11},{9,8},{10,9... | collective-permute-start | bytes 1572872 | tf_op jit(solution)/shard_map/ppermute | solution.py:287
  117.5 11.6 %copy-start.7 = (bf16[1024,256]{1,0:T(8,128)(2,1)}, bf16[1024,256]{1,0:T(8,128)(2,1)S(1)}, u32[]{:S(2)}) copy-start(bf16[1024,256]{1,0:T(8,128)(2,1)S(1)} %collective-permute-done.1.refs_2_) | copy-start | bytes 1572868
  117.5 32.8 %collective-permute-start.6 = (bf16[64,4096]{1,0:T(8,128)(2,1)S(1)}, bf16[64,4096]{1,0:T(8,128)(2,1)}, u32[]{:S(2)}, u32[]{:S(2)}) collective-permute-start(bf16[64,4096]{1,0:T(8,128)(2,1)S(1)} %bitcast.21), channel_id=1, source_target_pairs={{0,1},{1,2},{2,3},{3,0},{4,5},{5,6},{6,7},{7,4},{8,9},{9,10},{10,1... | collective-permute-start | bytes 1572872 | tf_op jit(solution)/shard_map/ppermute | solution.py:287
  118.2 10.9 %copy-start.8 = (bf16[1024,256]{1,0:T(8,128)(2,1)}, bf16[1024,256]{1,0:T(8,128)(2,1)S(1)}, u32[]{:S(2)}) copy-start(bf16[1024,256]{1,0:T(8,128)(2,1)S(1)} %collective-permute-done.2.refs_3_) | copy-start | bytes 1572868
  118.2 44.3 %collective-permute-start.7 = (bf16[64,4096]{1,0:T(8,128)(2,1)S(1)}, bf16[64,4096]{1,0:T(8,128)(2,1)S(1)}, u32[]{:S(2)}, u32[]{:S(2)}) collective-permute-start(bf16[64,4096]{1,0:T(8,128)(2,1)S(1)} %bitcast.22), channel_id=1, source_target_pairs={{0,2},{1,3},{2,0},{3,1},{4,6},{5,7},{6,4},{7,5},{8,10},{9,11},{10,... | collective-permute-start | bytes 1572872 | tf_op jit(solution)/shard_map/ppermute | solution.py:287
  127.8 34.7 %collective-permute-start.8 = (bf16[64,4096]{1,0:T(8,128)(2,1)S(1)}, bf16[64,4096]{1,0:T(8,128)(2,1)}, u32[]{:S(2)}, u32[]{:S(2)}) collective-permute-start(bf16[64,4096]{1,0:T(8,128)(2,1)S(1)} %bitcast.23), channel_id=1, source_target_pairs={{0,3},{1,0},{2,1},{3,2},{4,7},{5,4},{6,5},{7,6},{8,11},{9,8},{10,9... | collective-permute-start | bytes 1572872 | tf_op jit(solution)/shard_map/ppermute | solution.py:287
  172.0 14.2 %copy-start = (bf16[32,8,2048]{2,1,0:T(8,128)(2,1)}, bf16[32,8,2048]{2,1,0:T(8,128)(2,1)S(1)}, u32[]{:S(2)}) copy-start(bf16[32,8,2048]{2,1,0:T(8,128)(2,1)S(1)} %all-to-all-done.2.recv_ref) | copy-start | bytes 3145732
  172.0 47.5 %all-to-all-start.1 = ((bf16[32,8,1024]{2,1,0:T(8,128)(2,1)}), bf16[32,8,1024]{2,1,0:T(8,128)(2,1)S(1)}, u32[]{:S(2)}, u32[]{:S(2)}) async-start(bf16[32,8,1024]{2,1,0:T(8,128)(2,1)} %get-tuple-element.23), calls=%async_computation.1 | async-start | bytes 1048576 | tf_op jit(solution)/shard_map/outbound0/all_to_all | solution.py:303
  219.5 16.4 %copy-start.21 = (bf16[192,1024]{1,0:T(8,128)(2,1)S(1)}, bf16[192,1024]{1,0:T(8,128)(2,1)}, u32[]{:S(2)}) copy-start(bf16[192,1024]{1,0:T(8,128)(2,1)} %get-tuple-element.27) | copy-start | bytes 1179652
  220.3 58.4 %all-to-all-start.3 = ((bf16[32,8,1024]{2,1,0:T(8,128)(2,1)}), bf16[32,8,1024]{2,1,0:T(8,128)(2,1)S(1)}, u32[]{:S(2)}, u32[]{:S(2)}) async-start(bf16[32,8,1024]{2,1,0:T(8,128)(2,1)} %get-tuple-element.25), calls=%async_computation.3 | async-start | bytes 1048576 | tf_op jit(solution)/shard_map/outbound1/all_to_all | solution.py:303
  224.6 11.3 %collective-permute-start.10 = (bf16[192,1024]{1,0:T(8,128)(2,1)S(1)}, bf16[192,1024]{1,0:T(8,128)(2,1)S(1)}, u32[]{:S(2)}, u32[]{:S(2)}) collective-permute-start(bf16[192,1024]{1,0:T(8,128)(2,1)S(1)} %copy-done.22), channel_id=1, source_target_pairs={{0,2},{1,3},{2,0},{3,1},{4,6},{5,7},{6,4},{7,5},{8,10},{9,11},{10,... | collective-permute-start | bytes 1179656 | tf_op jit(solution)/shard_map/exchange0/ppermute | solution.py:287
  226.3 18.1 %collective-permute-start.11 = (bf16[192,1024]{1,0:T(8,128)(2,1)}, bf16[192,1024]{1,0:T(8,128)(2,1)S(1)}, u32[]{:S(2)}, u32[]{:S(2)}) collective-permute-start(bf16[192,1024]{1,0:T(8,128)(2,1)} %get-tuple-element.29), channel_id=1, source_target_pairs={{0,3},{1,0},{2,1},{3,2},{4,7},{5,4},{6,5},{7,6},{8,11},{9,8},{10,9... | collective-permute-start | bytes 1179656 | tf_op jit(solution)/shard_map/exchange0/ppermute | solution.py:287
  227.3 19.7 %collective-permute-start.12 = (bf16[192,1024]{1,0:T(8,128)(2,1)}, bf16[192,1024]{1,0:T(8,128)(2,1)S(1)}, u32[]{:S(2)}, u32[]{:S(2)}) collective-permute-start(bf16[192,1024]{1,0:T(8,128)(2,1)} %get-tuple-element.31), channel_id=1, source_target_pairs={{0,1},{1,2},{2,3},{3,0},{4,5},{5,6},{6,7},{7,4},{8,9},{9,10},{10,1... | collective-permute-start | bytes 1179656 | tf_op jit(solution)/shard_map/exchange1/ppermute | solution.py:287
  227.7 25.1 %collective-permute-start.13 = (bf16[192,1024]{1,0:T(8,128)(2,1)}, bf16[192,1024]{1,0:T(8,128)(2,1)S(1)}, u32[]{:S(2)}, u32[]{:S(2)}) collective-permute-start(bf16[192,1024]{1,0:T(8,128)(2,1)} %get-tuple-element.32), channel_id=1, source_target_pairs={{0,2},{1,3},{2,0},{3,1},{4,6},{5,7},{6,4},{7,5},{8,10},{9,11},{10,... | collective-permute-start | bytes 1179656 | tf_op jit(solution)/shard_map/exchange1/ppermute | solution.py:287
  229.2 31.2 %collective-permute-start.14 = (bf16[192,1024]{1,0:T(8,128)(2,1)}, bf16[192,1024]{1,0:T(8,128)(2,1)S(1)}, u32[]{:S(2)}, u32[]{:S(2)}) collective-permute-start(bf16[192,1024]{1,0:T(8,128)(2,1)} %get-tuple-element.33), channel_id=1, source_target_pairs={{0,3},{1,0},{2,1},{3,2},{4,7},{5,4},{6,5},{7,6},{8,11},{9,8},{10,9... | collective-permute-start | bytes 1179656 | tf_op jit(solution)/shard_map/exchange1/ppermute | solution.py:287
  235.9 26.6 %copy-start.11 = (bf16[192,1024]{1,0:T(8,128)(2,1)}, bf16[192,1024]{1,0:T(8,128)(2,1)S(1)}, u32[]{:S(2)}) copy-start(bf16[192,1024]{1,0:T(8,128)(2,1)S(1)} %collective-permute-done.10.refs_2_) | copy-start | bytes 1179652
  235.9 26.6 %collective-permute-start.9 = (bf16[192,1024]{1,0:T(8,128)(2,1)S(1)}, bf16[192,1024]{1,0:T(8,128)(2,1)S(1)}, u32[]{:S(2)}, u32[]{:S(2)}) collective-permute-start(bf16[192,1024]{1,0:T(8,128)(2,1)S(1)} %copy-done.21), channel_id=1, source_target_pairs={{0,1},{1,2},{2,3},{3,0},{4,5},{5,6},{6,7},{7,4},{8,9},{9,10},{10,1... | collective-permute-start | bytes 1179656 | tf_op jit(solution)/shard_map/exchange0/ppermute | solution.py:287
  244.4 18.2 %copy-start.12 = (bf16[192,1024]{1,0:T(8,128)(2,1)}, bf16[192,1024]{1,0:T(8,128)(2,1)S(1)}, u32[]{:S(2)}) copy-start(bf16[192,1024]{1,0:T(8,128)(2,1)S(1)} %collective-permute-done.11.refs_3_) | copy-start | bytes 1179652
  247.1 15.5 %copy-start.13 = (bf16[192,1024]{1,0:T(8,128)(2,1)}, bf16[192,1024]{1,0:T(8,128)(2,1)S(1)}, u32[]{:S(2)}) copy-start(bf16[192,1024]{1,0:T(8,128)(2,1)S(1)} %collective-permute-done.12.refs_5_) | copy-start | bytes 1179652
  252.8 9.7 %copy-start.14 = (bf16[192,1024]{1,0:T(8,128)(2,1)}, bf16[192,1024]{1,0:T(8,128)(2,1)S(1)}, u32[]{:S(2)}) copy-start(bf16[192,1024]{1,0:T(8,128)(2,1)S(1)} %collective-permute-done.13.refs_6_) | copy-start | bytes 1179652
  267.0 6.2 %collective-permute-start.15 = (bf16[64,1024]{1,0:T(8,128)(2,1)}, bf16[64,1024]{1,0:T(8,128)(2,1)S(1)}, u32[]{:S(2)}, u32[]{:S(2)}) collective-permute-start(bf16[64,1024]{1,0:T(8,128)(2,1)} %get-tuple-element.37), channel_id=1, source_target_pairs={{0,1},{1,2},{2,3},{3,0},{4,5},{5,6},{6,7},{7,4},{8,9},{9,10},{10,1... | collective-permute-start | bytes 393224 | tf_op jit(solution)/shard_map/ppermute | solution.py:287
  267.3 8.2 %collective-permute-start.16 = (bf16[64,1024]{1,0:T(8,128)(2,1)}, bf16[64,1024]{1,0:T(8,128)(2,1)S(1)}, u32[]{:S(2)}, u32[]{:S(2)}) collective-permute-start(bf16[64,1024]{1,0:T(8,128)(2,1)} %get-tuple-element.38), channel_id=1, source_target_pairs={{0,2},{1,3},{2,0},{3,1},{4,6},{5,7},{6,4},{7,5},{8,10},{9,11},{10,... | collective-permute-start | bytes 393224 | tf_op jit(solution)/shard_map/ppermute | solution.py:287
  269.5 6.7 %collective-permute-start.17 = (bf16[64,1024]{1,0:T(8,128)(2,1)}, bf16[64,1024]{1,0:T(8,128)(2,1)S(1)}, u32[]{:S(2)}, u32[]{:S(2)}) collective-permute-start(bf16[64,1024]{1,0:T(8,128)(2,1)} %get-tuple-element.39), channel_id=1, source_target_pairs={{0,3},{1,0},{2,1},{3,2},{4,7},{5,4},{6,5},{7,6},{8,11},{9,8},{10,9... | collective-permute-start | bytes 393224 | tf_op jit(solution)/shard_map/ppermute | solution.py:287
  (12 other events, 23.8 us)

commit v3 on v2

--- a/solution.py
+++ b/solution.py
@@ -7,11 +7,12 @@
 from jax.experimental.pallas import tpu as pltpu
 from jax.sharding import PartitionSpec as P
 
+
 BF = jnp.bfloat16
 F32 = jnp.float32
 VMEM = pl.BlockSpec(memory_space=pltpu.VMEM)
 SMEM = pl.BlockSpec(memory_space=pltpu.SMEM)
-SPLIT = (2, 2)
+SPLIT = (4,)
 PARTS = 4
 STEPS = 4
 
@@ -91,19 +92,37 @@
     )(ids2, gates2, *([tokens, cotangent] * 4))
 
 
+def stack_kernel(t_ref, *refs):
+    out = refs[-1]
+    part = refs[0].shape[0]
+    for k in range(PARTS):
+        at = pl.multiple_of(lax.rem(t_ref[0] - k + PARTS, PARTS) * part, part)
+        out[pl.ds(at, part), :] = refs[k][...]
+
+
+def stack_down(t, pieces):
+    part, d = pieces[0].shape
+    return pl.pallas_call(
+        stack_kernel,
+        in_specs=[SMEM] + [VMEM] * PARTS,
+        out_specs=VMEM,
+        out_shape=jax.ShapeDtypeStruct((part * PARTS, d), BF),
+        cost_estimate=cost(part * d, 4 * part * d * 4),
+        name="stack_down",
+    )(t, *pieces)
+
+
 def expert_kernel(count, t_ref, recv_ref, *refs):
-    wg, wu, wds, refs = refs[:PARTS], refs[PARTS : 2 * PARTS], refs[2 * PARTS : 3 * PARTS], refs[3 * PARTS :]
-    msg_ref, exchange, (flat, x, c, wd, back, ret) = refs[0], refs[1 : 1 + PARTS], refs[1 + PARTS :]
+    wg, wu, wd, refs = refs[:PARTS], refs[PARTS : 2 * PARTS], refs[2 * PARTS], refs[2 * PARTS + 1 :]
+    msg_ref, exchange, (flat, x, c, back, ret) = refs[0], refs[1 : 1 + PARTS], refs[1 + PARTS :]
     t = t_ref[0]
     width, ff = wg[0].shape
-    ff_part, d_model = wds[0].shape
+    d_model = wd.shape[1]
     sources = recv_ref.shape[0]
     rows = count * sources
     lanes = d_model // 4 // STEPS
     blocks = lanes // 128
     part = [lax.rem(t - k + PARTS, PARTS) for k in range(PARTS)]
-    for k in range(PARTS):
-        wd[pl.ds(pl.multiple_of(part[k] * ff_part, ff_part), ff_part), :] = wds[k][...]
     for b in range(flat.shape[0]):
         flat[b] = recv_ref[:, :, b * 128 : (b + 1) * 128].astype(F32).reshape(flat.shape[1:])
     for step in range(STEPS):
@@ -149,11 +168,11 @@
 def expert_round(t, recv, wg, wu, wd, count):
     sources = recv.shape[0]
     width, ff = wg[0].shape
-    ff_part, d = wd[0].shape
+    d = wd.shape[1]
     rows = sources * count
     return pl.pallas_call(
         functools.partial(expert_kernel, count),
-        in_specs=[SMEM] + [VMEM] * (1 + 3 * PARTS),
+        in_specs=[SMEM] + [VMEM] * (2 + 2 * PARTS),
         out_specs=[VMEM] * (1 + PARTS),
         out_shape=[jax.ShapeDtypeStruct((sources, 8, count * d // 8), BF)]
         + [jax.ShapeDtypeStruct((3 * rows, width), BF)] * PARTS,
@@ -161,13 +180,12 @@
             pltpu.VMEM((count * d // 4 // 128, sources * 8, 128), F32),
             pltpu.VMEM((rows, d), BF),
             pltpu.VMEM((rows, d), BF),
-            pltpu.VMEM((ff, d), BF),
             pltpu.VMEM((rows, d), F32),
             pltpu.VMEM((count * d // 8 // 128, sources * 8, 128), F32),
         ],
         cost_estimate=cost(2 * rows * d * 5 * ff, 3 * ff * d * 2 + 5 * rows * d * 2),
         name="expert_round",
-    )(t, recv, *wg, *wu, *wd)
+    )(t, recv, *wg, *wu, wd)
 
 
 def grads_kernel(ff, t_ref, *refs):
@@ -291,18 +309,15 @@
 
     sends = dispatch(expert_ids.T, gate_wts.T, tokens, cotangent, experts, split)
     recvs = []
-    for r, send in enumerate(sends):
-        with jax.named_scope(f"inbound{r}"):
-            recvs.append(lax.all_to_all(send, "expert", 0, 0, tiled=True))
+    for send in sends:
+        recvs.append(lax.all_to_all(send, "expert", 0, 0, tiled=True))
     wg, wu, wd = everyone(w_gate[0]), everyone(w_up[0]), everyone(w_down[0])
+    wd = stack_down(t, wd)
     boxes, rets = [], []
-    for r, (recv, count) in enumerate(zip(recvs, split)):
-        with jax.named_scope(f"round{r}"):
-            msg, *box = expert_round(t, recv, wg, wu, wd, count)
-        with jax.named_scope(f"outbound{r}"):
-            rets.append(lax.all_to_all(msg, "expert", 0, 0, tiled=True))
-        with jax.named_scope(f"exchange{r}"):
-            boxes += [box[0]] + [shift(box[k], k) for k in range(1, PARTS)]
+    for recv, count in zip(recvs, split):
+        msg, *box = expert_round(t, recv, wg, wu, wd, count)
+        rets.append(lax.all_to_all(msg, "expert", 0, 0, tiled=True))
+        boxes += [box[0]] + [shift(box[k], k) for k in range(1, PARTS)]
     grad_gate, grad_up, *down = grads(t, boxes, ff)
     grad_down = place(t, [down[0]] + [shift(down[k], k) for k in range(1, PARTS)])
     input_grad = combine(expert_ids, rets, split, d)

time: 284 us -> 208 us (0.73)
  blocking collectives: 81.1 us -> 0 us
  starting transfers between devices: 42.7 us -> 51.4 us
  Pallas kernels: 30.9 us -> 27.3 us
    all_to_all x1 -> x0, blocking collectives: 81.1 us -> none  [local(): recvs.append(lax.all_to_all(send, 'expert', 0, 0, tiled=True))]
    all_to_all x1, waiting for transfers between devices: 0.01 us -> 26.8 us  [local(): recvs.append(lax.all_to_all(send, 'expert', 0, 0, tiled=True))]
    all_to_all x2 -> x1, waiting for transfers between devices: 24.5 us -> 0.01 us  [local(): rets.append(lax.all_to_all(msg, 'expert', 0, 0, tiled=True))]
    all_to_all x1, starting transfers between devices: 4.47 us -> 25.6 us  [local(): recvs.append(lax.all_to_all(send, 'expert', 0, 0, tiled=True))]
    all_to_all x2 -> x1, starting transfers between devices: 18.5 us -> 5.25 us  [local(): rets.append(lax.all_to_all(msg, 'expert', 0, 0, tiled=True))]
    pallas_call x2 -> x1, Pallas kernels: 17.4 us -> 10.5 us  [expert_round(): pl.pallas_call(functools.partial(expert_kernel, count), in_specs=[SMEM] +...]
    pallas_call x0 -> x1, Pallas kernels: none -> 3 us  [stack_down(): pl.pallas_call(stack_kernel, in_specs=[SMEM] + [VMEM] * PARTS, out_specs=...]
    ppermute x18 -> x15, waiting for transfers between devices: 98 us -> 95.3 us  [shift(): lax.ppermute(x, 'tensor', [(s, (s + k) % PARTS) for s in range(PARTS)])]
  transfers between devices with their start and end apart: 21 -> 17, of which waited for: 18 -> 13; matrix products, arithmetic and copies ran while one was open for 0% -> 0% of each run, Pallas kernels for 8% -> 4%
where the time goes in v3:
time: 208 us; the launch traced here: 207 us
  waiting for transfers between devices  122 us (59%)
  starting transfers between devices  51.4 us (25%)
  Pallas kernels  27.3 us (13%)
  local copies, waits for them, and re-layouts  5.43 us (3%)
    ppermute x15, waiting for transfers between devices, shift(): lax.ppermute(x, 'tensor', [(s, (s + k) % PARTS) for s in range(PARTS)])  95.3 us
    all_to_all x1, waiting for transfers between devices, local(): recvs.append(lax.all_to_all(send, 'expert', 0, 0, tiled=True))  26.8 us
    all_to_all x1, starting transfers between devices, local(): recvs.append(lax.all_to_all(send, 'expert', 0, 0, tiled=True))  25.6 us
    ppermute x15, starting transfers between devices, shift(): lax.ppermute(x, 'tensor', [(s, (s + k) % PARTS) for s in range(PARTS)])  20.5 us
    pallas_call x1, Pallas kernels, expert_round(): pl.pallas_call(functools.partial(expert_kernel, count), in_specs=[SMEM] +...  10.5 us
    unnamed x33, local copies, waits for them, and re-layouts  5.43 us
    all_to_all x1, starting transfers between devices, local(): rets.append(lax.all_to_all(msg, 'expert', 0, 0, tiled=True))  5.25 us
    pallas_call x1, Pallas kernels, dispatch(): pl.pallas_call(functools.partial(dispatch_kernel, split), grid=(STEPS,),...  5.13 us
  transfers between devices with their start and end apart: 17, of which 13 were waited for; matrix products, arithmetic and copies ran while one was open for 0% of the time, Pallas kernels for 4%

profile of v3, /device:TPU:33, one launch (start us, length us, event | category | flops | bytes accessed | tf_op | source)
XLA Modules:
  0.0 206.9 jit_solution(2719689107373355095)
XLA Ops:
  0.6 5.1 %dispatch.1 = bf16[32,8,4096]{2,1,0:T(8,128)(2,1)} custom-call(s32[2,64]{1,0:T(2,128)} %bitcast.22, f32[2,64]{1,0:T(2,128)} %bitcast.23, bf16[64,4096]{1,0:T(8,128)(2,1)} %refs_6_.1, bf16[64,4096]{1,0:T(8,128)(2,1)} %refs_7_.1, bf16[64,4096]{1,0:T(8,128)(2,1)} %refs_6_.1, bf16[64,4096]{1,0:T(8,128)(2,1)} %refs_7_.1, bf16[64,4096]{1,0:T(8,128)(2,1)} %refs_6_.1, ...), custom_call_target="tpu_custom_call" | custom-call | flops 1073741824 | bytes 4194304 | tf_op jit(solution)/shard_map/dispatch/pallas_call | solution.py:83
  5.8 25.6 %all-to-all-start = ((bf16[32,8,4096]{2,1,0:T(8,128)(2,1)}), bf16[32,8,4096]{2,1,0:T(8,128)(2,1)S(1)}, u32[]{:S(2)}, u32[]{:S(2)}) async-start(bf16[32,8,4096]{2,1,0:T(8,128)(2,1)} %dispatch.1), calls=%async_computation | async-start | bytes 4194304 | tf_op jit(solution)/shard_map/all_to_all | solution.py:313
  31.4 1.5 collective-permute-start.6
  32.9 2.7 %collective-permute-start.7 = (bf16[64,4096]{1,0:T(8,128)(2,1)S(1)}, bf16[64,4096]{1,0:T(8,128)(2,1)S(1)}, u32[]{:S(2)}, u32[]{:S(2)}) collective-permute-start(bf16[64,4096]{1,0:T(8,128)(2,1)S(1)} %bitcast.11), channel_id=1, source_target_pairs={{0,2},{1,3},{2,0},{3,1},{4,6},{5,7},{6,4},{7,5},{8,10},{9,11},{10,... | collective-permute-start | bytes 1572872 | tf_op jit(solution)/shard_map/ppermute | solution.py:305
  35.6 1.0 collective-permute-start.8
  37.8 8.2 %collective-permute-done.6.refs_1_ = bf16[64,4096]{1,0:T(8,128)(2,1)S(1)} collective-permute-done((bf16[64,4096]{1,0:T(8,128)(2,1)S(1)}, bf16[64,4096]{1,0:T(8,128)(2,1)S(1)}, u32[]{:S(2)}, u32[]{:S(2)}) %collective-permute-start.6) | collective-permute-done | bytes 524320 | tf_op jit(solution)/shard_map/ppermute | solution.py:305
  46.0 1.2 collective-permute-start.2
  47.2 11.0 %collective-permute-done.7.refs_2_ = bf16[64,4096]{1,0:T(8,128)(2,1)S(1)} collective-permute-done((bf16[64,4096]{1,0:T(8,128)(2,1)S(1)}, bf16[64,4096]{1,0:T(8,128)(2,1)S(1)}, u32[]{:S(2)}, u32[]{:S(2)}) %collective-permute-start.7) | collective-permute-done | bytes 524320 | tf_op jit(solution)/shard_map/ppermute | solution.py:305
  58.3 1.9 collective-permute-start.4
  60.2 8.3 %collective-permute-done.refs_1_ = bf16[1024,256]{1,0:T(8,128)(2,1)S(1)} collective-permute-done((bf16[1024,256]{1,0:T(8,128)(2,1)S(1)}, bf16[1024,256]{1,0:T(8,128)(2,1)S(1)}, u32[]{:S(2)}, u32[]{:S(2)}) %collective-permute-start) | collective-permute-done | bytes 524320 | tf_op jit(solution)/shard_map/ppermute | solution.py:305
  68.4 0.8 copy-done.7
  69.2 1.4 collective-permute-start.5
  70.6 3.0 %stack_down.1.refs_8_ = bf16[256,4096]{1,0:T(8,128)(2,1)} custom-call(s32[1]{0:T(128)} %bitcast.t_ref, bf16[64,4096]{1,0:T(8,128)(2,1)} %bitcast.9, bf16[64,4096]{1,0:T(8,128)(2,1)} %copy-done.8, bf16[64,4096]{1,0:T(8,128)(2,1)} %copy-done.9, bf16[64,4096]{1,0:T(8,128)(2,1)} %copy-done.11), custom_call_target="tpu_custom_call" | custom-call | flops 262144 | bytes 4194304 | tf_op jit(solution)/shard_map/stack_down/pallas_call | solution.py:105
  73.6 7.2 %collective-permute-done.1.refs_2_ = bf16[1024,256]{1,0:T(8,128)(2,1)} collective-permute-done((bf16[1024,256]{1,0:T(8,128)(2,1)S(1)}, bf16[1024,256]{1,0:T(8,128)(2,1)}, u32[]{:S(2)}, u32[]{:S(2)}) %collective-permute-start.1) | collective-permute-done | bytes 524320 | tf_op jit(solution)/shard_map/ppermute | solution.py:305
  80.8 10.2 %collective-permute-done.3.refs_5_ = bf16[1024,256]{1,0:T(8,128)(2,1)} collective-permute-done((bf16[1024,256]{1,0:T(8,128)(2,1)}, bf16[1024,256]{1,0:T(8,128)(2,1)}, u32[]{:S(2)}, u32[]{:S(2)}) %collective-permute-start.3) | collective-permute-done | bytes 524320 | tf_op jit(solution)/shard_map/ppermute | solution.py:305
  91.0 12.2 %collective-permute-done.4.refs_6_ = bf16[1024,256]{1,0:T(8,128)(2,1)S(1)} collective-permute-done((bf16[1024,256]{1,0:T(8,128)(2,1)}, bf16[1024,256]{1,0:T(8,128)(2,1)S(1)}, u32[]{:S(2)}, u32[]{:S(2)}) %collective-permute-start.4) | collective-permute-done | bytes 524320 | tf_op jit(solution)/shard_map/ppermute | solution.py:305
  103.2 26.8 %all-to-all-done.recv_ref = bf16[32,8,4096]{2,1,0:T(8,128)(2,1)S(1)} async-done(((bf16[32,8,4096]{2,1,0:T(8,128)(2,1)}), bf16[32,8,4096]{2,1,0:T(8,128)(2,1)S(1)}, u32[]{:S(2)}, u32[]{:S(2)}) %all-to-all-start) | async-done | bytes 2097184 | tf_op jit(solution)/shard_map/all_to_all | solution.py:313
  130.0 1.3 copy-done
  131.3 10.5 %expert_round.1 = (bf16[32,8,2048]{2,1,0:T(8,128)(2,1)}, bf16[384,1024]{1,0:T(8,128)(2,1)}, bf16[384,1024]{1,0:T(8,128)(2,1)}, bf16[384,1024]{1,0:T(8,128)(2,1)}, bf16[384,1024]{1,0:T(8,128)(2,1)}) custom-call(s32[1]{0:T(128)} %bitcast.t_ref, bf16[32,8,4096]{2,1,0:T(8,128)(2,1)} %copy-done, bf16[1024,256]{1,0:T(8,128)(2,1)} %bitcast.13, ...), custom_call_target="tpu_custom_call" | custom-call | flops 1342177280 | bytes 11534336 | tf_op jit(solution)/shard_map/expert_round/pallas_call | solution.py:173
  141.8 5.2 %all-to-all-start.1 = ((bf16[32,8,2048]{2,1,0:T(8,128)(2,1)}), bf16[32,8,2048]{2,1,0:T(8,128)(2,1)S(1)}, u32[]{:S(2)}, u32[]{:S(2)}) async-start(bf16[32,8,2048]{2,1,0:T(8,128)(2,1)} %get-tuple-element.15), calls=%async_computation.1 | async-start | bytes 2097152 | tf_op jit(solution)/shard_map/all_to_all | solution.py:319
  147.1 3.1 %collective-permute-start.10 = (bf16[384,1024]{1,0:T(8,128)(2,1)}, bf16[384,1024]{1,0:T(8,128)(2,1)S(1)}, u32[]{:S(2)}, u32[]{:S(2)}) collective-permute-start(bf16[384,1024]{1,0:T(8,128)(2,1)} %get-tuple-element.18), channel_id=1, source_target_pairs={{0,2},{1,3},{2,0},{3,1},{4,6},{5,7},{6,4},{7,5},{8,10},{9,11},{10,... | collective-permute-start | bytes 2359304 | tf_op jit(solution)/shard_map/ppermute | solution.py:305
  150.9 0.8 collective-permute-start.9
  151.7 15.7 %collective-permute-done.10.refs_2_ = bf16[384,1024]{1,0:T(8,128)(2,1)S(1)} collective-permute-done((bf16[384,1024]{1,0:T(8,128)(2,1)}, bf16[384,1024]{1,0:T(8,128)(2,1)S(1)}, u32[]{:S(2)}, u32[]{:S(2)}) %collective-permute-start.10) | collective-permute-done | bytes 786464 | tf_op jit(solution)/shard_map/ppermute | solution.py:305
  167.4 17.4 %collective-permute-done.11.refs_3_ = bf16[384,1024]{1,0:T(8,128)(2,1)S(1)} collective-permute-done((bf16[384,1024]{1,0:T(8,128)(2,1)}, bf16[384,1024]{1,0:T(8,128)(2,1)S(1)}, u32[]{:S(2)}, u32[]{:S(2)}) %collective-permute-start.11) | collective-permute-done | bytes 786464 | tf_op jit(solution)/shard_map/ppermute | solution.py:305
  186.2 3.7 %grads.1 = (bf16[1024,256]{1,0:T(8,128)(2,1)}, bf16[1024,256]{1,0:T(8,128)(2,1)}, bf16[64,1024]{1,0:T(8,128)(2,1)}, bf16[64,1024]{1,0:T(8,128)(2,1)}, bf16[64,10...) custom-call(s32[1]{0:T(128)} %bitcast.t_ref, bf16[384,1024]{1,0:T(8,128)(2,1)} %get-tuple-element.16.refs_0_, ...), custom_call_target="tpu_custom_call" | custom-call | flops 805306368 | bytes 4718592 | tf_op jit(solution)/shard_map/grads/pallas_call | solution.py:214
  189.9 1.5 collective-permute-start.12
  191.4 2.7 %collective-permute-start.13 = (bf16[64,1024]{1,0:T(8,128)(2,1)}, bf16[64,1024]{1,0:T(8,128)(2,1)S(1)}, u32[]{:S(2)}, u32[]{:S(2)}) collective-permute-start(bf16[64,1024]{1,0:T(8,128)(2,1)} %get-tuple-element.24), channel_id=1, source_target_pairs={{0,2},{1,3},{2,0},{3,1},{4,6},{5,7},{6,4},{7,5},{8,10},{9,11},{10,... | collective-permute-start | bytes 393224 | tf_op jit(solution)/shard_map/ppermute | solution.py:305
  194.2 0.8 collective-permute-start.14
  196.0 4.3 %collective-permute-done.13.refs_2_ = bf16[64,1024]{1,0:T(8,128)(2,1)S(1)} collective-permute-done((bf16[64,1024]{1,0:T(8,128)(2,1)}, bf16[64,1024]{1,0:T(8,128)(2,1)S(1)}, u32[]{:S(2)}, u32[]{:S(2)}) %collective-permute-start.13) | collective-permute-done | bytes 131104 | tf_op jit(solution)/shard_map/ppermute | solution.py:305
  201.0 1.9 place.1
  202.9 1.0 copy-done.1
  203.9 3.0 %combine.1 = bf16[64,4096]{1,0:T(8,128)(2,1)} custom-call(s32[64,2]{1,0:T(8,128)} %copy.11.ids_ref, bf16[32,8,2048]{2,1,0:T(8,128)(2,1)} %copy-done.1), custom_call_target="tpu_custom_call" | custom-call | flops 67108864 | bytes 2097152 | tf_op jit(solution)/shard_map/combine/pallas_call | solution.py:264
  (41 shorter events, 5.1 us)
Async XLA Ops:
  5.8 25.6 %copy-start.5 = (bf16[1,64,4096]{2,1,0:T(8,128)(2,1)S(1)}, bf16[1,64,4096]{2,1,0:T(8,128)(2,1)}, u32[]{:S(2)}) copy-start(bf16[1,64,4096]{2,1,0:T(8,128)(2,1)} %param.13) | copy-start | bytes 1572868
  5.8 30.8 %copy-start.6 = (bf16[1,1024,256]{2,1,0:T(8,128)(2,1)S(1)}, bf16[1,1024,256]{2,1,0:T(8,128)(2,1)}, u32[]{:S(2)}) copy-start(bf16[1,1024,256]{2,1,0:T(8,128)(2,1)} %param.11) | copy-start | bytes 1572868
  5.8 124.2 %all-to-all-start = ((bf16[32,8,4096]{2,1,0:T(8,128)(2,1)}), bf16[32,8,4096]{2,1,0:T(8,128)(2,1)S(1)}, u32[]{:S(2)}, u32[]{:S(2)}) async-start(bf16[32,8,4096]{2,1,0:T(8,128)(2,1)} %dispatch.1), calls=%async_computation | async-start | bytes 4194304 | tf_op jit(solution)/shard_map/all_to_all | solution.py:313
  31.4 14.6 %collective-permute-start.6 = (bf16[64,4096]{1,0:T(8,128)(2,1)S(1)}, bf16[64,4096]{1,0:T(8,128)(2,1)S(1)}, u32[]{:S(2)}, u32[]{:S(2)}) collective-permute-start(bf16[64,4096]{1,0:T(8,128)(2,1)S(1)} %bitcast.10), channel_id=1, source_target_pairs={{0,1},{1,2},{2,3},{3,0},{4,5},{5,6},{6,7},{7,4},{8,9},{9,10},{10,1... | collective-permute-start | bytes 1572872 | tf_op jit(solution)/shard_map/ppermute | solution.py:305
  32.9 25.3 %collective-permute-start.7 = (bf16[64,4096]{1,0:T(8,128)(2,1)S(1)}, bf16[64,4096]{1,0:T(8,128)(2,1)S(1)}, u32[]{:S(2)}, u32[]{:S(2)}) collective-permute-start(bf16[64,4096]{1,0:T(8,128)(2,1)S(1)} %bitcast.11), channel_id=1, source_target_pairs={{0,2},{1,3},{2,0},{3,1},{4,6},{5,7},{6,4},{7,5},{8,10},{9,11},{10,... | collective-permute-start | bytes 1572872 | tf_op jit(solution)/shard_map/ppermute | solution.py:305
  35.6 22.7 %collective-permute-start.8 = (bf16[64,4096]{1,0:T(8,128)(2,1)S(1)}, bf16[64,4096]{1,0:T(8,128)(2,1)S(1)}, u32[]{:S(2)}, u32[]{:S(2)}) collective-permute-start(bf16[64,4096]{1,0:T(8,128)(2,1)S(1)} %bitcast.12), channel_id=1, source_target_pairs={{0,3},{1,0},{2,1},{3,2},{4,7},{5,4},{6,5},{7,6},{8,11},{9,8},{10,9... | collective-permute-start | bytes 1572872 | tf_op jit(solution)/shard_map/ppermute | solution.py:305
  36.6 31.8 %collective-permute-start = (bf16[1024,256]{1,0:T(8,128)(2,1)S(1)}, bf16[1024,256]{1,0:T(8,128)(2,1)S(1)}, u32[]{:S(2)}, u32[]{:S(2)}) collective-permute-start(bf16[1024,256]{1,0:T(8,128)(2,1)S(1)} %bitcast.14), channel_id=1, source_target_pairs={{0,1},{1,2},{2,3},{3,0},{4,5},{5,6},{6,7},{7,4},{8,9},{9,10},{10,1... | collective-permute-start | bytes 1572872 | tf_op jit(solution)/shard_map/ppermute | solution.py:305
  37.1 43.7 %collective-permute-start.1 = (bf16[1024,256]{1,0:T(8,128)(2,1)S(1)}, bf16[1024,256]{1,0:T(8,128)(2,1)}, u32[]{:S(2)}, u32[]{:S(2)}) collective-permute-start(bf16[1024,256]{1,0:T(8,128)(2,1)S(1)} %bitcast.15), channel_id=1, source_target_pairs={{0,2},{1,3},{2,0},{3,1},{4,6},{5,7},{6,4},{7,5},{8,10},{9,11},{10,... | collective-permute-start | bytes 1572872 | tf_op jit(solution)/shard_map/ppermute | solution.py:305
  46.0 24.6 %copy-start.8 = (bf16[64,4096]{1,0:T(8,128)(2,1)}, bf16[64,4096]{1,0:T(8,128)(2,1)S(1)}, u32[]{:S(2)}) copy-start(bf16[64,4096]{1,0:T(8,128)(2,1)S(1)} %collective-permute-done.6.refs_1_) | copy-start | bytes 1572868
  46.0 34.8 %collective-permute-start.2 = (bf16[1024,256]{1,0:T(8,128)(2,1)S(1)}, bf16[1024,256]{1,0:T(8,128)(2,1)}, u32[]{:S(2)}, u32[]{:S(2)}) collective-permute-start(bf16[1024,256]{1,0:T(8,128)(2,1)S(1)} %bitcast.16), channel_id=1, source_target_pairs={{0,3},{1,0},{2,1},{3,2},{4,7},{5,4},{6,5},{7,6},{8,11},{9,8},{10,9... | collective-permute-start | bytes 1572872 | tf_op jit(solution)/shard_map/ppermute | solution.py:305
  58.2 12.4 %copy-start.9 = (bf16[64,4096]{1,0:T(8,128)(2,1)}, bf16[64,4096]{1,0:T(8,128)(2,1)S(1)}, u32[]{:S(2)}) copy-start(bf16[64,4096]{1,0:T(8,128)(2,1)S(1)} %collective-permute-done.7.refs_2_) | copy-start | bytes 1572868
  58.2 32.8 %collective-permute-start.3 = (bf16[1024,256]{1,0:T(8,128)(2,1)}, bf16[1024,256]{1,0:T(8,128)(2,1)}, u32[]{:S(2)}, u32[]{:S(2)}) collective-permute-start(bf16[1024,256]{1,0:T(8,128)(2,1)} %bitcast.17), channel_id=1, source_target_pairs={{0,1},{1,2},{2,3},{3,0},{4,5},{5,6},{6,7},{7,4},{8,9},{9,10},{10,1... | collective-permute-start | bytes 1572872 | tf_op jit(solution)/shard_map/ppermute | solution.py:305
  58.3 12.4 %copy-start.11 = (bf16[64,4096]{1,0:T(8,128)(2,1)}, bf16[64,4096]{1,0:T(8,128)(2,1)S(1)}, u32[]{:S(2)}) copy-start(bf16[64,4096]{1,0:T(8,128)(2,1)S(1)} %collective-permute-done.8.refs_3_) | copy-start | bytes 1572868
  58.3 44.9 %collective-permute-start.4 = (bf16[1024,256]{1,0:T(8,128)(2,1)}, bf16[1024,256]{1,0:T(8,128)(2,1)S(1)}, u32[]{:S(2)}, u32[]{:S(2)}) collective-permute-start(bf16[1024,256]{1,0:T(8,128)(2,1)} %bitcast.18), channel_id=1, source_target_pairs={{0,2},{1,3},{2,0},{3,1},{4,6},{5,7},{6,4},{7,5},{8,10},{9,11},{10,... | collective-permute-start | bytes 1572872 | tf_op jit(solution)/shard_map/ppermute | solution.py:305
  68.4 0.8 copy-start.7
  69.2 33.9 %collective-permute-start.5 = (bf16[1024,256]{1,0:T(8,128)(2,1)}, bf16[1024,256]{1,0:T(8,128)(2,1)}, u32[]{:S(2)}, u32[]{:S(2)}) collective-permute-start(bf16[1024,256]{1,0:T(8,128)(2,1)} %bitcast.19), channel_id=1, source_target_pairs={{0,3},{1,0},{2,1},{3,2},{4,7},{5,4},{6,5},{7,6},{8,11},{9,8},{10,9... | collective-permute-start | bytes 1572872 | tf_op jit(solution)/shard_map/ppermute | solution.py:305
  103.2 26.8 %copy-start.10 = (bf16[1024,256]{1,0:T(8,128)(2,1)}, bf16[1024,256]{1,0:T(8,128)(2,1)S(1)}, u32[]{:S(2)}) copy-start(bf16[1024,256]{1,0:T(8,128)(2,1)S(1)} %collective-permute-done.4.refs_6_) | copy-start | bytes 1572868
  130.0 1.3 copy-start
  141.8 61.1 %all-to-all-start.1 = ((bf16[32,8,2048]{2,1,0:T(8,128)(2,1)}), bf16[32,8,2048]{2,1,0:T(8,128)(2,1)S(1)}, u32[]{:S(2)}, u32[]{:S(2)}) async-start(bf16[32,8,2048]{2,1,0:T(8,128)(2,1)} %get-tuple-element.15), calls=%async_computation.1 | async-start | bytes 2097152 | tf_op jit(solution)/shard_map/all_to_all | solution.py:319
  147.1 47.9 %copy-start.15 = (s32[64,2]{0,1:T(2,128)S(1)}, s32[64,2]{0,1:T(2,128)}, u32[]{:S(2)}) copy-start(s32[64,2]{0,1:T(2,128)} %param.9) | copy-start | bytes 1540
  147.1 20.3 %collective-permute-start.10 = (bf16[384,1024]{1,0:T(8,128)(2,1)}, bf16[384,1024]{1,0:T(8,128)(2,1)S(1)}, u32[]{:S(2)}, u32[]{:S(2)}) collective-permute-start(bf16[384,1024]{1,0:T(8,128)(2,1)} %get-tuple-element.18), channel_id=1, source_target_pairs={{0,2},{1,3},{2,0},{3,1},{4,6},{5,7},{6,4},{7,5},{8,10},{9,11},{10,... | collective-permute-start | bytes 2359304 | tf_op jit(solution)/shard_map/ppermute | solution.py:305
  150.2 34.6 %collective-permute-start.11 = (bf16[384,1024]{1,0:T(8,128)(2,1)}, bf16[384,1024]{1,0:T(8,128)(2,1)S(1)}, u32[]{:S(2)}, u32[]{:S(2)}) collective-permute-start(bf16[384,1024]{1,0:T(8,128)(2,1)} %get-tuple-element.19), channel_id=1, source_target_pairs={{0,3},{1,0},{2,1},{3,2},{4,7},{5,4},{6,5},{7,6},{8,11},{9,8},{10,9... | collective-permute-start | bytes 2359304 | tf_op jit(solution)/shard_map/ppermute | solution.py:305
  150.9 34.4 %collective-permute-start.9 = (bf16[384,1024]{1,0:T(8,128)(2,1)}, bf16[384,1024]{1,0:T(8,128)(2,1)S(1)}, u32[]{:S(2)}, u32[]{:S(2)}) collective-permute-start(bf16[384,1024]{1,0:T(8,128)(2,1)} %get-tuple-element.17), channel_id=1, source_target_pairs={{0,1},{1,2},{2,3},{3,0},{4,5},{5,6},{6,7},{7,4},{8,9},{9,10},{10,1... | collective-permute-start | bytes 2359304 | tf_op jit(solution)/shard_map/ppermute | solution.py:305
  167.4 17.9 %copy-start.2 = (bf16[384,1024]{1,0:T(8,128)(2,1)}, bf16[384,1024]{1,0:T(8,128)(2,1)S(1)}, u32[]{:S(2)}) copy-start(bf16[384,1024]{1,0:T(8,128)(2,1)S(1)} %collective-permute-done.10.refs_2_) | copy-start | bytes 2359300
  184.8 0.9 copy-start.3
  185.3 0.9 copy-start.4
  189.9 6.1 %collective-permute-start.12 = (bf16[64,1024]{1,0:T(8,128)(2,1)}, bf16[64,1024]{1,0:T(8,128)(2,1)S(1)}, u32[]{:S(2)}, u32[]{:S(2)}) collective-permute-start(bf16[64,1024]{1,0:T(8,128)(2,1)} %get-tuple-element.23), channel_id=1, source_target_pairs={{0,1},{1,2},{2,3},{3,0},{4,5},{5,6},{6,7},{7,4},{8,9},{9,10},{10,1... | collective-permute-start | bytes 393224 | tf_op jit(solution)/shard_map/ppermute | solution.py:305
  191.4 8.9 %collective-permute-start.13 = (bf16[64,1024]{1,0:T(8,128)(2,1)}, bf16[64,1024]{1,0:T(8,128)(2,1)S(1)}, u32[]{:S(2)}, u32[]{:S(2)}) collective-permute-start(bf16[64,1024]{1,0:T(8,128)(2,1)} %get-tuple-element.24), channel_id=1, source_target_pairs={{0,2},{1,3},{2,0},{3,1},{4,6},{5,7},{6,4},{7,5},{8,10},{9,11},{10,... | collective-permute-start | bytes 393224 | tf_op jit(solution)/shard_map/ppermute | solution.py:305
  194.2 6.1 %collective-permute-start.14 = (bf16[64,1024]{1,0:T(8,128)(2,1)}, bf16[64,1024]{1,0:T(8,128)(2,1)S(1)}, u32[]{:S(2)}, u32[]{:S(2)}) collective-permute-start(bf16[64,1024]{1,0:T(8,128)(2,1)} %get-tuple-element.25), channel_id=1, source_target_pairs={{0,3},{1,0},{2,1},{3,2},{4,7},{5,4},{6,5},{7,6},{8,11},{9,8},{10,9... | collective-permute-start | bytes 393224 | tf_op jit(solution)/shard_map/ppermute | solution.py:305
  196.0 4.3 %copy-start.12 = (bf16[64,1024]{1,0:T(8,128)(2,1)}, bf16[64,1024]{1,0:T(8,128)(2,1)S(1)}, u32[]{:S(2)}) copy-start(bf16[64,1024]{1,0:T(8,128)(2,1)S(1)} %collective-permute-done.12.refs_1_) | copy-start | bytes 393220
  200.3 0.7 copy-start.14
  202.9 1.0 copy-start.1
  (1 other events, 0.7 us)

commit v4 on v3

--- a/solution.py
+++ b/solution.py
@@ -12,13 +12,16 @@
 F32 = jnp.float32
 VMEM = pl.BlockSpec(memory_space=pltpu.VMEM)
 SMEM = pl.BlockSpec(memory_space=pltpu.SMEM)
-SPLIT = (4,)
 PARTS = 4
 STEPS = 4
 
 
 def cost(flops, bytes_accessed):
     return pl.CostEstimate(flops=int(flops), bytes_accessed=int(bytes_accessed), transcendentals=0)
+
+
+def struct(*shape):
+    return jax.ShapeDtypeStruct(shape, BF)
 
 
 def nn(a, b):
@@ -108,52 +111,59 @@
         out_specs=VMEM,
         out_shape=jax.ShapeDtypeStruct((part * PARTS, d), BF),
         cost_estimate=cost(part * d, 4 * part * d * 4),
+        compiler_params=pltpu.CompilerParams(vmem_limit_bytes=10 << 20),
         name="stack_down",
     )(t, *pieces)
 
 
-def expert_kernel(count, t_ref, recv_ref, *refs):
-    wg, wu, wd, refs = refs[:PARTS], refs[PARTS : 2 * PARTS], refs[2 * PARTS], refs[2 * PARTS + 1 :]
-    msg_ref, exchange, (flat, x, c, back, ret) = refs[0], refs[1 : 1 + PARTS], refs[1 + PARTS :]
-    t = t_ref[0]
-    width, ff = wg[0].shape
-    d_model = wd.shape[1]
+def unpack(recv_ref, flat, kinds):
     sources = recv_ref.shape[0]
-    rows = count * sources
-    lanes = d_model // 4 // STEPS
+    d = kinds[0][1].shape[1]
+    count = kinds[0][1].shape[0] // sources
+    lanes = d // 4 // STEPS
     blocks = lanes // 128
-    part = [lax.rem(t - k + PARTS, PARTS) for k in range(PARTS)]
     for b in range(flat.shape[0]):
         flat[b] = recv_ref[:, :, b * 128 : (b + 1) * 128].astype(F32).reshape(flat.shape[1:])
     for step in range(STEPS):
         for p in range(count):
             for b in range(blocks):
                 for q in range(4):
-                    col = q * (d_model // 4) + step * lanes + b * 128
-                    for kind, dst in ((0, x), (1, c)):
+                    col = q * (d // 4) + step * lanes + b * 128
+                    for kind, dst in kinds:
                         v = flat[(step * count + p) * blocks + b, pl.ds(2 * q + kind, sources, stride=8), :]
                         dst[p * sources : (p + 1) * sources, col : col + 128] = v.astype(BF)
-    cols = [pl.ds(pl.multiple_of(part[k] * width, width), width) for k in range(PARTS)]
+
+
+def flat_scratch(recv):
+    return pltpu.VMEM((recv.shape[2] // 128, recv.shape[0] * 8, 128), F32)
+
+
+def expert_kernel(count, t_ref, recv_ref, *refs):
+    wg, wu, wd, (msg_ref, h_ref, flat, x, c, back, ret) = (
+        refs[:PARTS],
+        refs[PARTS : 2 * PARTS],
+        refs[2 * PARTS],
+        refs[2 * PARTS + 1 :],
+    )
+    t = t_ref[0]
+    width, ff = wg[0].shape
+    d = wd.shape[1]
+    sources = recv_ref.shape[0]
+    unpack(recv_ref, flat, [(0, x), (1, c)])
+    cols = [pl.ds(pl.multiple_of(lax.rem(t - k + PARTS, PARTS) * width, width), width) for k in range(PARTS)]
     pre_gate = functools.reduce(lambda a, b: a + b, [nn(x[:, cols[k]], wg[k][...]) for k in range(PARTS)])
     pre_up = functools.reduce(lambda a, b: a + b, [nn(x[:, cols[k]], wu[k][...]) for k in range(PARTS)])
     grad_hidden = nt(c[...], wd[...])
     sig = jax.nn.sigmoid(pre_gate)
     activated = pre_gate * sig
-    hidden = (activated * pre_up).astype(BF)
     grad_gate_pre = (grad_hidden * pre_up * sig * (1.0 + pre_gate * (1.0 - sig))).astype(BF)
     grad_up_pre = (grad_hidden * activated).astype(BF)
-    for k in range(PARTS):
-        to = lax.rem(t + k, PARTS)
-        there = pl.ds(pl.multiple_of(to * width, width), width)
-        exchange[k][0:rows, :] = x[:, there]
-        exchange[k][rows : 2 * rows, :] = c[:, there]
-        exchange[k][2 * rows :, 0:ff] = hidden
-        exchange[k][2 * rows :, ff : 2 * ff] = grad_gate_pre
-        exchange[k][2 * rows :, 2 * ff : 3 * ff] = grad_up_pre
-        exchange[k][2 * rows :, 3 * ff :] = jnp.zeros((rows, width - 3 * ff), BF)
+    h_ref[:, 0:ff] = (activated * pre_up).astype(BF)
+    h_ref[:, ff : 2 * ff] = grad_gate_pre
+    h_ref[:, 2 * ff :] = grad_up_pre
     for k in range(PARTS):
         back[:, cols[k]] = nt(grad_gate_pre, wg[k][...]) + nt(grad_up_pre, wu[k][...])
-    eighth = d_model // 8
+    eighth = d // 8
     for p in range(count):
         for b in range(eighth // 128):
             for o in range(8):
@@ -167,64 +177,114 @@
 
 def expert_round(t, recv, wg, wu, wd, count):
     sources = recv.shape[0]
-    width, ff = wg[0].shape
-    d = wd.shape[1]
+    ff, d = wd.shape
     rows = sources * count
     return pl.pallas_call(
         functools.partial(expert_kernel, count),
         in_specs=[SMEM] + [VMEM] * (2 + 2 * PARTS),
-        out_specs=[VMEM] * (1 + PARTS),
-        out_shape=[jax.ShapeDtypeStruct((sources, 8, count * d // 8), BF)]
-        + [jax.ShapeDtypeStruct((3 * rows, width), BF)] * PARTS,
+        out_specs=[VMEM] * 2,
+        out_shape=[struct(sources, 8, count * d // 8), struct(rows, 3 * ff)],
         scratch_shapes=[
-            pltpu.VMEM((count * d // 4 // 128, sources * 8, 128), F32),
+            flat_scratch(recv),
             pltpu.VMEM((rows, d), BF),
             pltpu.VMEM((rows, d), BF),
             pltpu.VMEM((rows, d), F32),
             pltpu.VMEM((count * d // 8 // 128, sources * 8, 128), F32),
         ],
-        cost_estimate=cost(2 * rows * d * 5 * ff, 3 * ff * d * 2 + 5 * rows * d * 2),
+        cost_estimate=cost(2 * rows * d * 5 * ff, 3 * ff * d * 2 + 3 * rows * d * 2),
+        compiler_params=pltpu.CompilerParams(vmem_limit_bytes=28 << 20),
         name="expert_round",
     )(t, recv, *wg, *wu, wd)
 
 
-def grads_kernel(ff, t_ref, *refs):
-    n = len(refs) - (2 + PARTS) - 3
-    boxes, (gg_ref, gu_ref), downs, (x, c, h) = refs[:n], refs[n : n + 2], refs[n + 2 : n + 2 + PARTS], refs[-3:]
-    at = 0
-    for box in boxes:
-        rows = box.shape[0] // 3
-        x[at : at + rows, :] = box[0:rows, :]
-        c[at : at + rows, :] = box[rows : 2 * rows, :]
-        h[at : at + rows, :] = box[2 * rows :, 0 : 3 * ff]
-        at += rows
-    gg_ref[...] = tn(x[...], h[:, ff : 2 * ff]).astype(BF)
-    gu_ref[...] = tn(x[...], h[:, 2 * ff :]).astype(BF)
-    hidden = h[:, 0:ff]
-    down = tn(hidden, c[...]).astype(BF)
-    x[0:ff, :] = down
+def spread_kernel(kind, first, wide, t_ref, recv_ref, h_ref, *refs):
+    boxes, (flat, x) = refs[:PARTS], refs[PARTS:]
+    unpack(recv_ref, flat, [(kind, x)])
+    rows, d = x.shape
+    width = d // PARTS
+    folds = width // wide
+    part = rows // folds
+    for k in range(PARTS):
+        there = pl.ds(pl.multiple_of(lax.rem(t_ref[0] + k, PARTS) * width, width), width)
+        boxes[k][0:rows, :] = x[:, there]
+        for f in range(folds):
+            boxes[k][rows:, f * wide : (f + 1) * wide] = h_ref[f * part : (f + 1) * part, first : first + wide]
+
+
+def spread(t, recv, h, kind, first, wide):
+    rows = h.shape[0]
+    d = recv.shape[2] * 8 * recv.shape[0] // (2 * rows)
+    width = d // PARTS
+    return list(
+        pl.pallas_call(
+            functools.partial(spread_kernel, kind, first, wide),
+            in_specs=[SMEM] + [VMEM] * 2,
+            out_specs=[VMEM] * PARTS,
+            out_shape=[struct(rows + rows * wide // width, width)] * PARTS,
+            scratch_shapes=[flat_scratch(recv), pltpu.VMEM((rows, d), BF)],
+            cost_estimate=cost(rows * d, 6 * rows * d),
+            compiler_params=pltpu.CompilerParams(vmem_limit_bytes=20 << 20),
+        )(t, recv, h)
+    )
+
+
+def join(boxes, x, h):
+    rows = x.shape[0] // len(boxes)
+    wide = h.shape[1]
+    folds = x.shape[1] // wide
+    part = rows // folds
+    for i, box in enumerate(boxes):
+        x[i * rows : (i + 1) * rows, :] = box[0:rows, :]
+        for f in range(folds):
+            h[i * rows + f * part : i * rows + (f + 1) * part, :] = box[rows:, f * wide : (f + 1) * wide]
+
+
+def grads_down_kernel(t_ref, *refs):
+    boxes, downs, (c, h) = refs[:PARTS], refs[PARTS : 2 * PARTS], refs[2 * PARTS :]
+    join(boxes, c, h)
+    ff = h.shape[1]
+    c[0:ff, :] = tn(h[...], c[...]).astype(BF)
     part = ff // PARTS
     for k in range(PARTS):
-        downs[k][...] = x[pl.ds(pl.multiple_of(lax.rem(t_ref[0] + k, PARTS) * part, part), part), :]
-
-
-def grads(t, boxes, ff):
+        downs[k][...] = c[pl.ds(pl.multiple_of(lax.rem(t_ref[0] + k, PARTS) * part, part), part), :]
+
+
+def grads_up_kernel(*refs):
+    boxes, (gg_ref, gu_ref, x, h) = refs[:PARTS], refs[PARTS:]
+    join(boxes, x, h)
+    ff = gg_ref.shape[1]
+    gg_ref[...] = tn(x[...], h[:, :ff]).astype(BF)
+    gu_ref[...] = tn(x[...], h[:, ff:]).astype(BF)
+
+
+def grads_down(t, boxes, rows, ff):
     width = boxes[0].shape[1]
-    rows = sum(b.shape[0] for b in boxes) // 3
-    return pl.pallas_call(
-        functools.partial(grads_kernel, ff),
-        in_specs=[SMEM] + [VMEM] * len(boxes),
-        out_specs=[VMEM] * (2 + PARTS),
-        out_shape=[jax.ShapeDtypeStruct((width, ff), BF)] * 2
-        + [jax.ShapeDtypeStruct((ff // PARTS, width), BF)] * PARTS,
-        scratch_shapes=[
-            pltpu.VMEM((rows, width), BF),
-            pltpu.VMEM((rows, width), BF),
-            pltpu.VMEM((rows, 3 * ff), BF),
-        ],
-        cost_estimate=cost(2 * rows * width * 3 * ff, 3 * rows * width * 2 + 3 * width * ff * 2),
-        name="grads",
+    rows *= PARTS
+    return pl.pallas_call(
+        grads_down_kernel,
+        in_specs=[SMEM] + [VMEM] * PARTS,
+        out_specs=[VMEM] * PARTS,
+        out_shape=[struct(ff // PARTS, width)] * PARTS,
+        scratch_shapes=[pltpu.VMEM((rows, width), BF), pltpu.VMEM((rows, ff), BF)],
+        cost_estimate=cost(2 * rows * width * ff, 2 * rows * width * 2),
+        compiler_params=pltpu.CompilerParams(vmem_limit_bytes=12 << 20),
+        name="grads_down",
     )(t, *boxes)
+
+
+def grads_up(boxes, rows, ff):
+    width = boxes[0].shape[1]
+    rows *= PARTS
+    return pl.pallas_call(
+        grads_up_kernel,
+        in_specs=[VMEM] * PARTS,
+        out_specs=[VMEM] * 2,
+        out_shape=[struct(width, ff)] * 2,
+        scratch_shapes=[pltpu.VMEM((rows, width), BF), pltpu.VMEM((rows, 2 * ff), BF)],
+        cost_estimate=cost(4 * rows * width * ff, 3 * rows * width * 2),
+        compiler_params=pltpu.CompilerParams(vmem_limit_bytes=14 << 20),
+        name="grads_up",
+    )(*boxes)
 
 
 def combine_kernel(split, ids_ref, *refs):
@@ -269,6 +329,7 @@
         scratch_shapes=[pltpu.VMEM((c * d // 8 // 128, r.shape[0] * 8, 128), F32) for c, r in zip(split, rets)]
         + [pltpu.VMEM((slots * experts, d), BF)],
         cost_estimate=cost(2 * n_tok * slots * experts * d, 4 * n_tok * d * 2),
+        compiler_params=pltpu.CompilerParams(vmem_limit_bytes=14 << 20),
         name="combine",
     )(ids, *rets)
 
@@ -289,6 +350,7 @@
         out_specs=VMEM,
         out_shape=jax.ShapeDtypeStruct((rows, width * len(pieces)), BF),
         cost_estimate=cost(rows * width, 4 * rows * width * 4),
+        compiler_params=pltpu.CompilerParams(vmem_limit_bytes=6 << 20),
         name="place",
     )(t, *pieces)
 
@@ -297,7 +359,7 @@
     n_tok, d = tokens.shape
     experts = lax.axis_size("expert")
     slots = 2 * n_tok // experts
-    split = SPLIT if sum(SPLIT) == slots else (slots,)
+    split = (slots,)
     t = lax.axis_index("tensor").astype(jnp.int32).reshape(1)
     ff = w_gate.shape[2]
 
@@ -313,13 +375,17 @@
         recvs.append(lax.all_to_all(send, "expert", 0, 0, tiled=True))
     wg, wu, wd = everyone(w_gate[0]), everyone(w_up[0]), everyone(w_down[0])
     wd = stack_down(t, wd)
-    boxes, rets = [], []
-    for recv, count in zip(recvs, split):
-        msg, *box = expert_round(t, recv, wg, wu, wd, count)
-        rets.append(lax.all_to_all(msg, "expert", 0, 0, tiled=True))
-        boxes += [box[0]] + [shift(box[k], k) for k in range(1, PARTS)]
-    grad_gate, grad_up, *down = grads(t, boxes, ff)
-    grad_down = place(t, [down[0]] + [shift(down[k], k) for k in range(1, PARTS)])
+    (recv,), (count,) = recvs, split
+    msg, h = expert_round(t, recv, wg, wu, wd, count)
+    rets = [lax.all_to_all(msg, "expert", 0, 0, tiled=True)]
+    boxes_c = spread(t, recv, h, 1, 0, ff)
+    boxes_c = boxes_c[:1] + [shift(boxes_c[k], k) for k in range(1, PARTS)]
+    boxes_x = spread(t, recv, h, 0, ff, 2 * ff)
+    boxes_x = boxes_x[:1] + [shift(boxes_x[k], k) for k in range(1, PARTS)]
+    down = grads_down(t, boxes_c, h.shape[0], ff)
+    down = list(down[:1]) + [shift(down[k], k) for k in range(1, PARTS)]
+    grad_gate, grad_up = grads_up(boxes_x, h.shape[0], ff)
+    grad_down = place(t, down)
     input_grad = combine(expert_ids, rets, split, d)
     return input_grad, grad_gate[None], grad_up[None], grad_down[None]
 

time: 208 us -> 205 us (0.986)
  Pallas kernels: 27.3 us -> 19.1 us
  local copies, waits for them, and re-layouts: 5.43 us -> 13.4 us
    ppermute x15 -> x18, waiting for transfers between devices: 95.3 us -> 83.7 us  [shift(): lax.ppermute(x, 'tensor', [(s, (s + k) % PARTS) for s in range(PARTS)])]
    all_to_all x1, waiting for transfers between devices: 0.01 us -> 11 us  [local(): rets = [lax.all_to_all(msg, 'expert', 0, 0, tiled=True)]]
    unnamed x33 -> x35, local copies, waits for them, and re-layouts: 5.43 us -> 13.4 us
    pallas_call x1, Pallas kernels: 10.5 us -> 6.59 us  [expert_round(): pl.pallas_call(functools.partial(expert_kernel, count), in_specs=[SMEM] +...]
    pallas_call x1, Pallas kernels: 3 us -> 0.14 us  [stack_down(): pl.pallas_call(stack_kernel, in_specs=[SMEM] + [VMEM] * PARTS, out_specs=...]
    ppermute x15 -> x18, starting transfers between devices: 20.5 us -> 18.6 us  [shift(): lax.ppermute(x, 'tensor', [(s, (s + k) % PARTS) for s in range(PARTS)])]
    pallas_call x1 -> x4, Pallas kernels: 3.73 us -> 4.69 us  [the longest x2 2.47 us: spread(): pl.pallas_call(functools.partial(spread_kernel, kind, first, wide), in_sp...]
  transfers between devices with their start and end apart: 17 -> 20, of which waited for: 13 -> 15; matrix products, arithmetic and copies ran while one was open for 0% -> 0% of each run, Pallas kernels for 4% -> 3%
where the time goes in v4:
time: 205 us; the launch traced here: 204 us
  waiting for transfers between devices  121 us (59%)
  starting transfers between devices  49.5 us (24%)
  Pallas kernels  19.1 us (9%)
  local copies, waits for them, and re-layouts  13.4 us (7%)
    ppermute x18, waiting for transfers between devices, shift(): lax.ppermute(x, 'tensor', [(s, (s + k) % PARTS) for s in range(PARTS)])  83.7 us
    all_to_all x1, waiting for transfers between devices, local(): recvs.append(lax.all_to_all(send, 'expert', 0, 0, tiled=True))  26.3 us
    all_to_all x1, starting transfers between devices, local(): recvs.append(lax.all_to_all(send, 'expert', 0, 0, tiled=True))  25.6 us
    ppermute x18, starting transfers between devices, shift(): lax.ppermute(x, 'tensor', [(s, (s + k) % PARTS) for s in range(PARTS)])  18.6 us
    unnamed x35, local copies, waits for them, and re-layouts  13.4 us
    all_to_all x1, waiting for transfers between devices, local(): rets = [lax.all_to_all(msg, 'expert', 0, 0, tiled=True)]  11 us
    pallas_call x1, Pallas kernels, expert_round(): pl.pallas_call(functools.partial(expert_kernel, count), in_specs=[SMEM] +...  6.59 us
    all_to_all x1, starting transfers between devices, local(): rets = [lax.all_to_all(msg, 'expert', 0, 0, tiled=True)]  5.25 us
  transfers between devices with their start and end apart: 20, of which 15 were waited for; matrix products, arithmetic and copies ran while one was open for 0% of the time, Pallas kernels for 3%

profile of v4, /device:TPU:33, one launch (start us, length us, event | category | flops | bytes accessed | tf_op | source)
XLA Modules:
  0.0 203.7 jit_solution(10819898470413067343)
XLA Ops:
  0.6 5.1 %dispatch.1 = bf16[32,8,4096]{2,1,0:T(8,128)(2,1)} custom-call(s32[2,64]{1,0:T(2,128)} %bitcast.22, f32[2,64]{1,0:T(2,128)} %bitcast.23, bf16[64,4096]{1,0:T(8,128)(2,1)} %refs_6_.1, bf16[64,4096]{1,0:T(8,128)(2,1)} %refs_7_.1, bf16[64,4096]{1,0:T(8,128)(2,1)} %refs_6_.1, bf16[64,4096]{1,0:T(8,128)(2,1)} %refs_7_.1, bf16[64,4096]{1,0:T(8,128)(2,1)} %refs_6_.1, ...), custom_call_target="tpu_custom_call" | custom-call | flops 1073741824 | bytes 4194304 | tf_op jit(solution)/shard_map/dispatch/pallas_call | solution.py:86
  5.7 25.6 %all-to-all-start = ((bf16[32,8,4096]{2,1,0:T(8,128)(2,1)}), bf16[32,8,4096]{2,1,0:T(8,128)(2,1)S(1)}, u32[]{:S(2)}, u32[]{:S(2)}) async-start(bf16[32,8,4096]{2,1,0:T(8,128)(2,1)} %dispatch.1), calls=%async_computation | async-start | bytes 4194304 | tf_op jit(solution)/shard_map/all_to_all | solution.py:375
  31.3 1.5 collective-permute-start
  32.8 1.3 collective-permute-start.6
  34.2 1.5 collective-permute-start.7
  35.7 1.9 collective-permute-start.8
  37.9 8.1 %collective-permute-done.refs_1_ = bf16[1024,256]{1,0:T(8,128)(2,1)S(1)} collective-permute-done((bf16[1024,256]{1,0:T(8,128)(2,1)S(1)}, bf16[1024,256]{1,0:T(8,128)(2,1)S(1)}, u32[]{:S(2)}, u32[]{:S(2)}) %collective-permute-start) | collective-permute-done | bytes 524320 | tf_op jit(solution)/shard_map/ppermute | solution.py:367
  47.9 9.2 %collective-permute-done.6.refs_1_ = bf16[64,4096]{1,0:T(8,128)(2,1)S(1)} collective-permute-done((bf16[64,4096]{1,0:T(8,128)(2,1)S(1)}, bf16[64,4096]{1,0:T(8,128)(2,1)S(1)}, u32[]{:S(2)}, u32[]{:S(2)}) %collective-permute-start.6) | collective-permute-done | bytes 524320 | tf_op jit(solution)/shard_map/ppermute | solution.py:367
  57.9 11.4 %collective-permute-done.7.refs_2_ = bf16[64,4096]{1,0:T(8,128)(2,1)S(1)} collective-permute-done((bf16[64,4096]{1,0:T(8,128)(2,1)S(1)}, bf16[64,4096]{1,0:T(8,128)(2,1)S(1)}, u32[]{:S(2)}, u32[]{:S(2)}) %collective-permute-start.7) | collective-permute-done | bytes 524320 | tf_op jit(solution)/shard_map/ppermute | solution.py:367
  75.8 4.9 %collective-permute-done.1.refs_2_ = bf16[1024,256]{1,0:T(8,128)(2,1)} collective-permute-done((bf16[1024,256]{1,0:T(8,128)(2,1)S(1)}, bf16[1024,256]{1,0:T(8,128)(2,1)}, u32[]{:S(2)}, u32[]{:S(2)}) %collective-permute-start.1) | collective-permute-done | bytes 524320 | tf_op jit(solution)/shard_map/ppermute | solution.py:367
  80.7 1.5 collective-permute-done.2.refs_3_
  82.2 12.9 %collective-permute-done.3.refs_5_ = bf16[1024,256]{1,0:T(8,128)(2,1)} collective-permute-done((bf16[1024,256]{1,0:T(8,128)(2,1)}, bf16[1024,256]{1,0:T(8,128)(2,1)}, u32[]{:S(2)}, u32[]{:S(2)}) %collective-permute-start.3) | collective-permute-done | bytes 524320 | tf_op jit(solution)/shard_map/ppermute | solution.py:367
  95.1 7.0 %collective-permute-done.4.refs_6_ = bf16[1024,256]{1,0:T(8,128)(2,1)} collective-permute-done((bf16[1024,256]{1,0:T(8,128)(2,1)}, bf16[1024,256]{1,0:T(8,128)(2,1)}, u32[]{:S(2)}, u32[]{:S(2)}) %collective-permute-start.4) | collective-permute-done | bytes 524320 | tf_op jit(solution)/shard_map/ppermute | solution.py:367
  102.1 1.6 collective-permute-done.5.refs_7_
  103.6 26.3 %all-to-all-done.recv_ref = bf16[32,8,4096]{2,1,0:T(8,128)(2,1)S(1)} async-done(((bf16[32,8,4096]{2,1,0:T(8,128)(2,1)}), bf16[32,8,4096]{2,1,0:T(8,128)(2,1)S(1)}, u32[]{:S(2)}, u32[]{:S(2)}) %all-to-all-start) | async-done | bytes 2097184 | tf_op jit(solution)/shard_map/all_to_all | solution.py:375
  130.0 1.6 copy-done.1
  133.6 6.6 %expert_round.1 = (bf16[32,8,2048]{2,1,0:T(8,128)(2,1)S(1)}, bf16[128,768]{1,0:T(8,128)(2,1)S(1)}) custom-call(s32[1]{0:T(128)} %bitcast.t_ref, bf16[32,8,4096]{2,1,0:T(8,128)(2,1)S(1)} %all-to-all-done.recv_ref, bf16[1024,256]{1,0:T(8,128)(2,1)S(1)} %bitcast.16, bf16[1024,256]{1,0:T(8,128)(2,1)S(1)} %copy-done.7, ...), custom_call_target="tpu_custom_call" | custom-call | flops 1342177280 | bytes 9437184 | tf_op jit(solution)/shard_map/expert_round/pallas_call | solution.py:182
  141.2 5.3 %all-to-all-start.1 = ((bf16[32,8,2048]{2,1,0:T(8,128)(2,1)}), bf16[32,8,2048]{2,1,0:T(8,128)(2,1)S(1)}, u32[]{:S(2)}, u32[]{:S(2)}) async-start(bf16[32,8,2048]{2,1,0:T(8,128)(2,1)} %copy-done.2), calls=%async_computation.1 | async-start | bytes 2097152 | tf_op jit(solution)/shard_map/all_to_all | solution.py:380
  147.3 1.4 collective-permute-start.12
  148.7 1.7 shard_map.102
  150.4 1.3 collective-permute-start.9
  151.7 1.4 collective-permute-start.13
  153.2 2.0 %collective-permute-start.14 = (bf16[160,1024]{1,0:T(8,128)(2,1)S(1)}, bf16[160,1024]{1,0:T(8,128)(2,1)S(1)}, u32[]{:S(2)}, u32[]{:S(2)}) collective-permute-start(bf16[160,1024]{1,0:T(8,128)(2,1)S(1)} %get-tuple-element.31), channel_id=1, source_target_pairs={{0,3},{1,0},{2,1},{3,2},{4,7},{5,4},{6,5},{7,6},{8,11},{9,8},{10,9... | collective-permute-start | bytes 983048 | tf_op jit(solution)/shard_map/ppermute | solution.py:367
  155.4 2.1 %collective-permute-done.12.refs_1_ = bf16[160,1024]{1,0:T(8,128)(2,1)S(1)} collective-permute-done((bf16[160,1024]{1,0:T(8,128)(2,1)S(1)}, bf16[160,1024]{1,0:T(8,128)(2,1)S(1)}, u32[]{:S(2)}, u32[]{:S(2)}) %collective-permute-start.12) | collective-permute-done | bytes 327712 | tf_op jit(solution)/shard_map/ppermute | solution.py:367
  158.8 15.2 %collective-permute-done.13.refs_2_ = bf16[160,1024]{1,0:T(8,128)(2,1)S(1)} collective-permute-done((bf16[160,1024]{1,0:T(8,128)(2,1)S(1)}, bf16[160,1024]{1,0:T(8,128)(2,1)S(1)}, u32[]{:S(2)}, u32[]{:S(2)}) %collective-permute-start.13) | collective-permute-done | bytes 327712 | tf_op jit(solution)/shard_map/ppermute | solution.py:367
  175.2 2.1 %collective-permute-start.17 = (bf16[64,1024]{1,0:T(8,128)(2,1)S(1)}, bf16[64,1024]{1,0:T(8,128)(2,1)S(1)}, u32[]{:S(2)}, u32[]{:S(2)}) collective-permute-start(bf16[64,1024]{1,0:T(8,128)(2,1)S(1)} %get-tuple-element.35), channel_id=1, source_target_pairs={{0,3},{1,0},{2,1},{3,2},{4,7},{5,4},{6,5},{7,6},{8,11},{9,8},{10,9... | collective-permute-start | bytes 393224 | tf_op jit(solution)/shard_map/ppermute | solution.py:367
  177.4 5.0 %collective-permute-done.10.refs_2_ = bf16[192,1024]{1,0:T(8,128)(2,1)S(1)} collective-permute-done((bf16[192,1024]{1,0:T(8,128)(2,1)}, bf16[192,1024]{1,0:T(8,128)(2,1)S(1)}, u32[]{:S(2)}, u32[]{:S(2)}) %collective-permute-start.10) | collective-permute-done | bytes 393248 | tf_op jit(solution)/shard_map/ppermute | solution.py:367
  182.4 3.5 %collective-permute-done.11.refs_3_ = bf16[192,1024]{1,0:T(8,128)(2,1)S(1)} collective-permute-done((bf16[192,1024]{1,0:T(8,128)(2,1)}, bf16[192,1024]{1,0:T(8,128)(2,1)S(1)}, u32[]{:S(2)}, u32[]{:S(2)}) %collective-permute-start.11) | collective-permute-done | bytes 393248 | tf_op jit(solution)/shard_map/ppermute | solution.py:367
  186.9 1.7 grads_up.1
  188.6 1.5 collective-permute-done.17.refs_3_
  191.0 11.0 %all-to-all-done.1.refs_0_ = bf16[32,8,2048]{2,1,0:T(8,128)(2,1)S(1)} async-done(((bf16[32,8,2048]{2,1,0:T(8,128)(2,1)}), bf16[32,8,2048]{2,1,0:T(8,128)(2,1)S(1)}, u32[]{:S(2)}, u32[]{:S(2)}) %all-to-all-start.1) | async-done | bytes 1048608 | tf_op jit(solution)/shard_map/all_to_all | solution.py:380
  202.0 1.8 combine.1
  (52 shorter events, 18.0 us)
Async XLA Ops:
  5.7 25.6 %copy-start.4 = (bf16[1,1024,256]{2,1,0:T(8,128)(2,1)S(1)}, bf16[1,1024,256]{2,1,0:T(8,128)(2,1)}, u32[]{:S(2)}) copy-start(bf16[1,1024,256]{2,1,0:T(8,128)(2,1)} %param.11) | copy-start | bytes 1572868
  5.7 27.1 %copy-start.3 = (bf16[1,64,4096]{2,1,0:T(8,128)(2,1)S(1)}, bf16[1,64,4096]{2,1,0:T(8,128)(2,1)}, u32[]{:S(2)}) copy-start(bf16[1,64,4096]{2,1,0:T(8,128)(2,1)} %param.13) | copy-start | bytes 1572868
  5.7 124.2 %all-to-all-start = ((bf16[32,8,4096]{2,1,0:T(8,128)(2,1)}), bf16[32,8,4096]{2,1,0:T(8,128)(2,1)S(1)}, u32[]{:S(2)}, u32[]{:S(2)}) async-start(bf16[32,8,4096]{2,1,0:T(8,128)(2,1)} %dispatch.1), calls=%async_computation | async-start | bytes 4194304 | tf_op jit(solution)/shard_map/all_to_all | solution.py:375
  31.3 14.6 %collective-permute-start = (bf16[1024,256]{1,0:T(8,128)(2,1)S(1)}, bf16[1024,256]{1,0:T(8,128)(2,1)S(1)}, u32[]{:S(2)}, u32[]{:S(2)}) collective-permute-start(bf16[1024,256]{1,0:T(8,128)(2,1)S(1)} %bitcast.13), channel_id=1, source_target_pairs={{0,1},{1,2},{2,3},{3,0},{4,5},{5,6},{6,7},{7,4},{8,9},{9,10},{10,1... | collective-permute-start | bytes 1572872 | tf_op jit(solution)/shard_map/ppermute | solution.py:367
  32.8 24.3 %collective-permute-start.6 = (bf16[64,4096]{1,0:T(8,128)(2,1)S(1)}, bf16[64,4096]{1,0:T(8,128)(2,1)S(1)}, u32[]{:S(2)}, u32[]{:S(2)}) collective-permute-start(bf16[64,4096]{1,0:T(8,128)(2,1)S(1)} %bitcast.9), channel_id=1, source_target_pairs={{0,1},{1,2},{2,3},{3,0},{4,5},{5,6},{6,7},{7,4},{8,9},{9,10},{10,1... | collective-permute-start | bytes 1572872 | tf_op jit(solution)/shard_map/ppermute | solution.py:367
  34.2 35.2 %collective-permute-start.7 = (bf16[64,4096]{1,0:T(8,128)(2,1)S(1)}, bf16[64,4096]{1,0:T(8,128)(2,1)S(1)}, u32[]{:S(2)}, u32[]{:S(2)}) collective-permute-start(bf16[64,4096]{1,0:T(8,128)(2,1)S(1)} %bitcast.10), channel_id=1, source_target_pairs={{0,2},{1,3},{2,0},{3,1},{4,6},{5,7},{6,4},{7,5},{8,10},{9,11},{10,... | collective-permute-start | bytes 1572872 | tf_op jit(solution)/shard_map/ppermute | solution.py:367
  35.7 34.7 %collective-permute-start.8 = (bf16[64,4096]{1,0:T(8,128)(2,1)S(1)}, bf16[64,4096]{1,0:T(8,128)(2,1)S(1)}, u32[]{:S(2)}, u32[]{:S(2)}) collective-permute-start(bf16[64,4096]{1,0:T(8,128)(2,1)S(1)} %bitcast.11), channel_id=1, source_target_pairs={{0,3},{1,0},{2,1},{3,2},{4,7},{5,4},{6,5},{7,6},{8,11},{9,8},{10,9... | collective-permute-start | bytes 1572872 | tf_op jit(solution)/shard_map/ppermute | solution.py:367
  37.6 43.1 %collective-permute-start.1 = (bf16[1024,256]{1,0:T(8,128)(2,1)S(1)}, bf16[1024,256]{1,0:T(8,128)(2,1)}, u32[]{:S(2)}, u32[]{:S(2)}) collective-permute-start(bf16[1024,256]{1,0:T(8,128)(2,1)S(1)} %bitcast.14), channel_id=1, source_target_pairs={{0,2},{1,3},{2,0},{3,1},{4,6},{5,7},{6,4},{7,5},{8,10},{9,11},{10,... | collective-permute-start | bytes 1572872 | tf_op jit(solution)/shard_map/ppermute | solution.py:367
  46.7 35.5 %collective-permute-start.2 = (bf16[1024,256]{1,0:T(8,128)(2,1)S(1)}, bf16[1024,256]{1,0:T(8,128)(2,1)}, u32[]{:S(2)}, u32[]{:S(2)}) collective-permute-start(bf16[1024,256]{1,0:T(8,128)(2,1)S(1)} %bitcast.15), channel_id=1, source_target_pairs={{0,3},{1,0},{2,1},{3,2},{4,7},{5,4},{6,5},{7,6},{8,11},{9,8},{10,9... | collective-permute-start | bytes 1572872 | tf_op jit(solution)/shard_map/ppermute | solution.py:367
  57.9 37.1 %collective-permute-start.3 = (bf16[1024,256]{1,0:T(8,128)(2,1)}, bf16[1024,256]{1,0:T(8,128)(2,1)}, u32[]{:S(2)}, u32[]{:S(2)}) collective-permute-start(bf16[1024,256]{1,0:T(8,128)(2,1)} %bitcast.17), channel_id=1, source_target_pairs={{0,1},{1,2},{2,3},{3,0},{4,5},{5,6},{6,7},{7,4},{8,9},{9,10},{10,1... | collective-permute-start | bytes 1572872 | tf_op jit(solution)/shard_map/ppermute | solution.py:367
  70.2 31.9 %collective-permute-start.4 = (bf16[1024,256]{1,0:T(8,128)(2,1)}, bf16[1024,256]{1,0:T(8,128)(2,1)}, u32[]{:S(2)}, u32[]{:S(2)}) collective-permute-start(bf16[1024,256]{1,0:T(8,128)(2,1)} %bitcast.18), channel_id=1, source_target_pairs={{0,2},{1,3},{2,0},{3,1},{4,6},{5,7},{6,4},{7,5},{8,10},{9,11},{10,... | collective-permute-start | bytes 1572872 | tf_op jit(solution)/shard_map/ppermute | solution.py:367
  71.2 32.4 %collective-permute-start.5 = (bf16[1024,256]{1,0:T(8,128)(2,1)}, bf16[1024,256]{1,0:T(8,128)(2,1)}, u32[]{:S(2)}, u32[]{:S(2)}) collective-permute-start(bf16[1024,256]{1,0:T(8,128)(2,1)} %bitcast.19), channel_id=1, source_target_pairs={{0,3},{1,0},{2,1},{3,2},{4,7},{5,4},{6,5},{7,6},{8,11},{9,8},{10,9... | collective-permute-start | bytes 1572872 | tf_op jit(solution)/shard_map/ppermute | solution.py:367
  71.2 1.0 copy-start.9
  72.2 1.0 copy-start.11
  73.3 1.0 copy-start.13
  74.5 1.3 copy-start
  130.0 1.6 copy-start.1
  131.6 1.0 copy-start.5
  132.6 1.0 copy-start.7
  141.2 60.7 %all-to-all-start.1 = ((bf16[32,8,2048]{2,1,0:T(8,128)(2,1)}), bf16[32,8,2048]{2,1,0:T(8,128)(2,1)S(1)}, u32[]{:S(2)}, u32[]{:S(2)}) async-start(bf16[32,8,2048]{2,1,0:T(8,128)(2,1)} %copy-done.2), calls=%async_computation.1 | async-start | bytes 2097152 | tf_op jit(solution)/shard_map/all_to_all | solution.py:380
  147.3 30.0 %copy-start.16 = (s32[64,2]{0,1:T(2,128)S(1)}, s32[64,2]{0,1:T(2,128)}, u32[]{:S(2)}) copy-start(s32[64,2]{0,1:T(2,128)} %param.9) | copy-start | bytes 1540
  147.3 10.2 %collective-permute-start.12 = (bf16[160,1024]{1,0:T(8,128)(2,1)S(1)}, bf16[160,1024]{1,0:T(8,128)(2,1)S(1)}, u32[]{:S(2)}, u32[]{:S(2)}) collective-permute-start(bf16[160,1024]{1,0:T(8,128)(2,1)S(1)} %get-tuple-element.29), channel_id=1, source_target_pairs={{0,1},{1,2},{2,3},{3,0},{4,5},{5,6},{6,7},{7,4},{8,9},{9,10},{10,1... | collective-permute-start | bytes 983048 | tf_op jit(solution)/shard_map/ppermute | solution.py:367
  150.4 24.8 %copy-start.14 = (bf16[192,1024]{1,0:T(8,128)(2,1)}, bf16[192,1024]{1,0:T(8,128)(2,1)S(1)}, u32[]{:S(2)}) copy-start(bf16[192,1024]{1,0:T(8,128)(2,1)S(1)} %get-tuple-element.22.refs_0_) | copy-start | bytes 1179652
  150.4 24.8 %collective-permute-start.9 = (bf16[192,1024]{1,0:T(8,128)(2,1)S(1)}, bf16[192,1024]{1,0:T(8,128)(2,1)S(1)}, u32[]{:S(2)}, u32[]{:S(2)}) collective-permute-start(bf16[192,1024]{1,0:T(8,128)(2,1)S(1)} %get-tuple-element.23), channel_id=1, source_target_pairs={{0,1},{1,2},{2,3},{3,0},{4,5},{5,6},{6,7},{7,4},{8,9},{9,10},{10,1... | collective-permute-start | bytes 1179656 | tf_op jit(solution)/shard_map/ppermute | solution.py:367
  151.7 22.2 %collective-permute-start.13 = (bf16[160,1024]{1,0:T(8,128)(2,1)S(1)}, bf16[160,1024]{1,0:T(8,128)(2,1)S(1)}, u32[]{:S(2)}, u32[]{:S(2)}) collective-permute-start(bf16[160,1024]{1,0:T(8,128)(2,1)S(1)} %get-tuple-element.30), channel_id=1, source_target_pairs={{0,2},{1,3},{2,0},{3,1},{4,6},{5,7},{6,4},{7,5},{8,10},{9,11},{10,... | collective-permute-start | bytes 983048 | tf_op jit(solution)/shard_map/ppermute | solution.py:367
  153.2 20.8 %collective-permute-start.14 = (bf16[160,1024]{1,0:T(8,128)(2,1)S(1)}, bf16[160,1024]{1,0:T(8,128)(2,1)S(1)}, u32[]{:S(2)}, u32[]{:S(2)}) collective-permute-start(bf16[160,1024]{1,0:T(8,128)(2,1)S(1)} %get-tuple-element.31), channel_id=1, source_target_pairs={{0,3},{1,0},{2,1},{3,2},{4,7},{5,4},{6,5},{7,6},{8,11},{9,8},{10,9... | collective-permute-start | bytes 983048 | tf_op jit(solution)/shard_map/ppermute | solution.py:367
  155.2 27.2 %collective-permute-start.10 = (bf16[192,1024]{1,0:T(8,128)(2,1)}, bf16[192,1024]{1,0:T(8,128)(2,1)S(1)}, u32[]{:S(2)}, u32[]{:S(2)}) collective-permute-start(bf16[192,1024]{1,0:T(8,128)(2,1)} %get-tuple-element.24), channel_id=1, source_target_pairs={{0,2},{1,3},{2,0},{3,1},{4,6},{5,7},{6,4},{7,5},{8,10},{9,11},{10,... | collective-permute-start | bytes 1179656 | tf_op jit(solution)/shard_map/ppermute | solution.py:367
  157.5 28.4 %collective-permute-start.11 = (bf16[192,1024]{1,0:T(8,128)(2,1)}, bf16[192,1024]{1,0:T(8,128)(2,1)S(1)}, u32[]{:S(2)}, u32[]{:S(2)}) collective-permute-start(bf16[192,1024]{1,0:T(8,128)(2,1)} %get-tuple-element.25), channel_id=1, source_target_pairs={{0,3},{1,0},{2,1},{3,2},{4,7},{5,4},{6,5},{7,6},{8,11},{9,8},{10,9... | collective-permute-start | bytes 1179656 | tf_op jit(solution)/shard_map/ppermute | solution.py:367
  174.4 14.2 %collective-permute-start.15 = (bf16[64,1024]{1,0:T(8,128)(2,1)S(1)}, bf16[64,1024]{1,0:T(8,128)(2,1)S(1)}, u32[]{:S(2)}, u32[]{:S(2)}) collective-permute-start(bf16[64,1024]{1,0:T(8,128)(2,1)S(1)} %get-tuple-element.33), channel_id=1, source_target_pairs={{0,1},{1,2},{2,3},{3,0},{4,5},{5,6},{6,7},{7,4},{8,9},{9,10},{10,1... | collective-permute-start | bytes 393224 | tf_op jit(solution)/shard_map/ppermute | solution.py:367
  174.6 14.1 %collective-permute-start.16 = (bf16[64,1024]{1,0:T(8,128)(2,1)S(1)}, bf16[64,1024]{1,0:T(8,128)(2,1)S(1)}, u32[]{:S(2)}, u32[]{:S(2)}) collective-permute-start(bf16[64,1024]{1,0:T(8,128)(2,1)S(1)} %get-tuple-element.34), channel_id=1, source_target_pairs={{0,2},{1,3},{2,0},{3,1},{4,6},{5,7},{6,4},{7,5},{8,10},{9,11},{10,... | collective-permute-start | bytes 393224 | tf_op jit(solution)/shard_map/ppermute | solution.py:367
  175.2 15.0 %collective-permute-start.17 = (bf16[64,1024]{1,0:T(8,128)(2,1)S(1)}, bf16[64,1024]{1,0:T(8,128)(2,1)S(1)}, u32[]{:S(2)}, u32[]{:S(2)}) collective-permute-start(bf16[64,1024]{1,0:T(8,128)(2,1)S(1)} %get-tuple-element.35), channel_id=1, source_target_pairs={{0,3},{1,0},{2,1},{3,2},{4,7},{5,4},{6,5},{7,6},{8,11},{9,8},{10,9... | collective-permute-start | bytes 393224 | tf_op jit(solution)/shard_map/ppermute | solution.py:367
  185.9 1.0 copy-start.15
  (5 other events, 4.2 us)

commit v5 on v4

--- a/solution.py
+++ b/solution.py
@@ -12,6 +12,7 @@
 F32 = jnp.float32
 VMEM = pl.BlockSpec(memory_space=pltpu.VMEM)
 SMEM = pl.BlockSpec(memory_space=pltpu.SMEM)
+HBM = pl.BlockSpec(memory_space=pltpu.HBM)
 PARTS = 4
 STEPS = 4
 
@@ -111,45 +112,48 @@
         out_specs=VMEM,
         out_shape=jax.ShapeDtypeStruct((part * PARTS, d), BF),
         cost_estimate=cost(part * d, 4 * part * d * 4),
-        compiler_params=pltpu.CompilerParams(vmem_limit_bytes=10 << 20),
         name="stack_down",
     )(t, *pieces)
 
 
-def unpack(recv_ref, flat, kinds):
-    sources = recv_ref.shape[0]
+def unpack(block, flat, step, kinds):
+    sources = block.shape[0]
     d = kinds[0][1].shape[1]
     count = kinds[0][1].shape[0] // sources
     lanes = d // 4 // STEPS
     blocks = lanes // 128
     for b in range(flat.shape[0]):
-        flat[b] = recv_ref[:, :, b * 128 : (b + 1) * 128].astype(F32).reshape(flat.shape[1:])
-    for step in range(STEPS):
-        for p in range(count):
-            for b in range(blocks):
-                for q in range(4):
-                    col = q * (d // 4) + step * lanes + b * 128
-                    for kind, dst in kinds:
-                        v = flat[(step * count + p) * blocks + b, pl.ds(2 * q + kind, sources, stride=8), :]
-                        dst[p * sources : (p + 1) * sources, col : col + 128] = v.astype(BF)
+        flat[b] = block[:, :, b * 128 : (b + 1) * 128].astype(F32).reshape(flat.shape[1:])
+    for p in range(count):
+        for b in range(blocks):
+            for q in range(4):
+                col = q * (d // 4) + step * lanes + b * 128
+                for kind, dst in kinds:
+                    v = flat[p * blocks + b, pl.ds(2 * q + kind, sources, stride=8), :]
+                    dst[p * sources : (p + 1) * sources, col : col + 128] = v.astype(BF)
 
 
 def flat_scratch(recv):
-    return pltpu.VMEM((recv.shape[2] // 128, recv.shape[0] * 8, 128), F32)
+    return pltpu.VMEM((STEPS, recv.shape[2] // STEPS // 128, recv.shape[0] * 8, 128), F32)
 
 
 def expert_kernel(count, t_ref, recv_ref, *refs):
-    wg, wu, wd, (msg_ref, h_ref, flat, x, c, back, ret) = (
-        refs[:PARTS],
-        refs[PARTS : 2 * PARTS],
-        refs[2 * PARTS],
-        refs[2 * PARTS + 1 :],
-    )
+    weights, refs = refs[: 2 * PARTS + 1], refs[2 * PARTS + 1 :]
+    msg_ref, h_ref, flat, x, c, back, ret, msg = refs[:8]
+    held, sem_out, sem_w = refs[8 : 8 + len(weights)], refs[-2], refs[-1]
+    wg, wu, wd = held[:PARTS], held[PARTS : 2 * PARTS], held[2 * PARTS]
     t = t_ref[0]
     width, ff = wg[0].shape
     d = wd.shape[1]
     sources = recv_ref.shape[0]
-    unpack(recv_ref, flat, [(0, x), (1, c)])
+    lanes = recv_ref.shape[2] // STEPS
+    weights_in = [pltpu.make_async_copy(w, v, sem_w.at[i]) for i, (w, v) in enumerate(zip(weights, held))]
+    for copy in weights_in:
+        copy.start()
+    for i in range(STEPS):
+        unpack(recv_ref.at[:, :, pl.ds(i * lanes, lanes)], flat.at[i], i, [(0, x), (1, c)])
+    for copy in weights_in:
+        copy.wait()
     cols = [pl.ds(pl.multiple_of(lax.rem(t - k + PARTS, PARTS) * width, width), width) for k in range(PARTS)]
     pre_gate = functools.reduce(lambda a, b: a + b, [nn(x[:, cols[k]], wg[k][...]) for k in range(PARTS)])
     pre_up = functools.reduce(lambda a, b: a + b, [nn(x[:, cols[k]], wu[k][...]) for k in range(PARTS)])
@@ -158,21 +162,29 @@
     activated = pre_gate * sig
     grad_gate_pre = (grad_hidden * pre_up * sig * (1.0 + pre_gate * (1.0 - sig))).astype(BF)
     grad_up_pre = (grad_hidden * activated).astype(BF)
-    h_ref[:, 0:ff] = (activated * pre_up).astype(BF)
-    h_ref[:, ff : 2 * ff] = grad_gate_pre
-    h_ref[:, 2 * ff :] = grad_up_pre
+    hidden = (activated * pre_up).astype(BF)
     for k in range(PARTS):
         back[:, cols[k]] = nt(grad_gate_pre, wg[k][...]) + nt(grad_up_pre, wu[k][...])
     eighth = d // 8
+    blocks = eighth // 128
+    out = [
+        pltpu.make_async_copy(msg.at[p], msg_ref.at[:, :, pl.ds(p * eighth, eighth)], sem_out.at[p]) for p in range(count)
+    ]
     for p in range(count):
-        for b in range(eighth // 128):
+        for b in range(blocks):
             for o in range(8):
                 col = o * eighth + b * 128
-                ret[p * (eighth // 128) + b, pl.ds(o, sources, stride=8), :] = back[
-                    p * sources : (p + 1) * sources, col : col + 128
-                ]
-    for b in range(ret.shape[0]):
-        msg_ref[:, :, b * 128 : (b + 1) * 128] = ret[b].reshape(sources, 8, 128).astype(BF)
+                ret[p * blocks + b, pl.ds(o, sources, stride=8), :] = back[p * sources : (p + 1) * sources, col : col + 128]
+        for b in range(blocks):
+            msg[p, :, :, b * 128 : (b + 1) * 128] = ret[p * blocks + b].reshape(sources, 8, 128).astype(BF)
+        if p:
+            out[p - 1].start()
+    h_ref[:, 0:ff] = hidden
+    h_ref[:, ff : 2 * ff] = grad_gate_pre
+    h_ref[:, 2 * ff :] = grad_up_pre
+    out[-1].start()
+    for copy in out:
+        copy.wait()
 
 
 def expert_round(t, recv, wg, wu, wd, count):
@@ -181,8 +193,8 @@
     rows = sources * count
     return pl.pallas_call(
         functools.partial(expert_kernel, count),
-        in_specs=[SMEM] + [VMEM] * (2 + 2 * PARTS),
-        out_specs=[VMEM] * 2,
+        in_specs=[SMEM, VMEM] + [HBM] * (1 + 2 * PARTS),
+        out_specs=[HBM, VMEM],
         out_shape=[struct(sources, 8, count * d // 8), struct(rows, 3 * ff)],
         scratch_shapes=[
             flat_scratch(recv),
@@ -190,16 +202,21 @@
             pltpu.VMEM((rows, d), BF),
             pltpu.VMEM((rows, d), F32),
             pltpu.VMEM((count * d // 8 // 128, sources * 8, 128), F32),
-        ],
+            pltpu.VMEM((count, sources, 8, d // 8), BF),
+        ]
+        + [pltpu.VMEM(w.shape, BF) for w in (*wg, *wu, wd)]
+        + [pltpu.SemaphoreType.DMA((count,)), pltpu.SemaphoreType.DMA((2 * PARTS + 1,))],
         cost_estimate=cost(2 * rows * d * 5 * ff, 3 * ff * d * 2 + 3 * rows * d * 2),
-        compiler_params=pltpu.CompilerParams(vmem_limit_bytes=28 << 20),
+        compiler_params=pltpu.CompilerParams(vmem_limit_bytes=60 << 20),
         name="expert_round",
     )(t, recv, *wg, *wu, wd)
 
 
 def spread_kernel(kind, first, wide, t_ref, recv_ref, h_ref, *refs):
     boxes, (flat, x) = refs[:PARTS], refs[PARTS:]
-    unpack(recv_ref, flat, [(kind, x)])
+    lanes = recv_ref.shape[2] // STEPS
+    for i in range(STEPS):
+        unpack(recv_ref.at[:, :, pl.ds(i * lanes, lanes)], flat.at[i], i, [(kind, x)])
     rows, d = x.shape
     width = d // PARTS
     folds = width // wide
@@ -223,7 +240,7 @@
             out_shape=[struct(rows + rows * wide // width, width)] * PARTS,
             scratch_shapes=[flat_scratch(recv), pltpu.VMEM((rows, d), BF)],
             cost_estimate=cost(rows * d, 6 * rows * d),
-            compiler_params=pltpu.CompilerParams(vmem_limit_bytes=20 << 20),
+            compiler_params=pltpu.CompilerParams(vmem_limit_bytes=60 << 20),
         )(t, recv, h)
     )
 
@@ -267,7 +284,6 @@
         out_shape=[struct(ff // PARTS, width)] * PARTS,
         scratch_shapes=[pltpu.VMEM((rows, width), BF), pltpu.VMEM((rows, ff), BF)],
         cost_estimate=cost(2 * rows * width * ff, 2 * rows * width * 2),
-        compiler_params=pltpu.CompilerParams(vmem_limit_bytes=12 << 20),
         name="grads_down",
     )(t, *boxes)
 
@@ -282,7 +298,6 @@
         out_shape=[struct(width, ff)] * 2,
         scratch_shapes=[pltpu.VMEM((rows, width), BF), pltpu.VMEM((rows, 2 * ff), BF)],
         cost_estimate=cost(4 * rows * width * ff, 3 * rows * width * 2),
-        compiler_params=pltpu.CompilerParams(vmem_limit_bytes=14 << 20),
         name="grads_up",
     )(*boxes)
 
@@ -350,7 +365,6 @@
         out_specs=VMEM,
         out_shape=jax.ShapeDtypeStruct((rows, width * len(pieces)), BF),
         cost_estimate=cost(rows * width, 4 * rows * width * 4),
-        compiler_params=pltpu.CompilerParams(vmem_limit_bytes=6 << 20),
         name="place",
     )(t, *pieces)
 

time: 205 us -> 205 us (level)
  Pallas kernels: 19.1 us -> 34.7 us
  local copies, waits for them, and re-layouts: 13.4 us -> 4.18 us
  waiting for transfers between devices: 121 us -> 115 us
    unnamed x35 -> x41, local copies, waits for them, and re-layouts: 13.4 us -> 4.18 us
    all_to_all x1, waiting for transfers between devices: 11 us -> 4.74 us  [local(): rets = [lax.all_to_all(msg, 'expert', 0, 0, tiled=True)]]
    pallas_call x2, Pallas kernels: 2.47 us -> 6.84 us  [spread(): pl.pallas_call(functools.partial(spread_kernel, kind, first, wide), in_sp...]
    pallas_call x1, Pallas kernels: 6.59 us -> 10.4 us  [expert_round(): pl.pallas_call(functools.partial(expert_kernel, count), in_specs=[SMEM, V...]
    pallas_call x1, Pallas kernels: 0.14 us -> 2.98 us  [stack_down(): pl.pallas_call(stack_kernel, in_specs=[SMEM] + [VMEM] * PARTS, out_specs=...]
    pallas_call x1, Pallas kernels: 0.48 us -> 2.56 us  [grads_down(): pl.pallas_call(grads_down_kernel, in_specs=[SMEM] + [VMEM] * PARTS, out_s...]
  transfers between devices with their start and end apart: 20 -> 20, of which waited for: 15 -> 15; matrix products, arithmetic and copies ran while one was open for 0% -> 0% of each run, Pallas kernels for 3% -> 9%
where the time goes in v5:
time: 205 us; the launch traced here: 204 us
  waiting for transfers between devices  115 us (56%)
  starting transfers between devices  49.7 us (24%)
  Pallas kernels  34.7 us (17%)
  local copies, waits for them, and re-layouts  4.18 us (2%)
    ppermute x18, waiting for transfers between devices, shift(): lax.ppermute(x, 'tensor', [(s, (s + k) % PARTS) for s in range(PARTS)])  83.9 us
    all_to_all x1, waiting for transfers between devices, local(): recvs.append(lax.all_to_all(send, 'expert', 0, 0, tiled=True))  26.3 us
    all_to_all x1, starting transfers between devices, local(): recvs.append(lax.all_to_all(send, 'expert', 0, 0, tiled=True))  25.6 us
    ppermute x18, starting transfers between devices, shift(): lax.ppermute(x, 'tensor', [(s, (s + k) % PARTS) for s in range(PARTS)])  18.8 us
    pallas_call x1, Pallas kernels, expert_round(): pl.pallas_call(functools.partial(expert_kernel, count), in_specs=[SMEM, V...  10.4 us
    pallas_call x2, Pallas kernels, spread(): pl.pallas_call(functools.partial(spread_kernel, kind, first, wide), in_sp...  6.84 us
    all_to_all x1, starting transfers between devices, local(): rets = [lax.all_to_all(msg, 'expert', 0, 0, tiled=True)]  5.26 us
    pallas_call x1, Pallas kernels, dispatch(): pl.pallas_call(functools.partial(dispatch_kernel, split), grid=(STEPS,),...  5.12 us
  transfers between devices with their start and end apart: 20, of which 15 were waited for; matrix products, arithmetic and copies ran while one was open for 0% of the time, Pallas kernels for 9%

profile of v5, /device:TPU:33, one launch (start us, length us, event | category | flops | bytes accessed | tf_op | source)
XLA Modules:
  0.0 204.3 jit_solution(4496519445771705511)
XLA Ops:
  0.6 5.1 %dispatch.1 = bf16[32,8,4096]{2,1,0:T(8,128)(2,1)} custom-call(s32[2,64]{1,0:T(2,128)} %bitcast.22, f32[2,64]{1,0:T(2,128)} %bitcast.23, bf16[64,4096]{1,0:T(8,128)(2,1)} %refs_6_.1, bf16[64,4096]{1,0:T(8,128)(2,1)} %refs_7_.1, bf16[64,4096]{1,0:T(8,128)(2,1)} %refs_6_.1, bf16[64,4096]{1,0:T(8,128)(2,1)} %refs_7_.1, bf16[64,4096]{1,0:T(8,128)(2,1)} %refs_6_.1, ...), custom_call_target="tpu_custom_call" | custom-call | flops 1073741824 | bytes 4194304 | tf_op jit(solution)/shard_map/dispatch/pallas_call | solution.py:87
  5.8 25.6 %all-to-all-start = ((bf16[32,8,4096]{2,1,0:T(8,128)(2,1)}), bf16[32,8,4096]{2,1,0:T(8,128)(2,1)S(1)}, u32[]{:S(2)}, u32[]{:S(2)}) async-start(bf16[32,8,4096]{2,1,0:T(8,128)(2,1)} %dispatch.1), calls=%async_computation | async-start | bytes 4194304 | tf_op jit(solution)/shard_map/all_to_all | solution.py:389
  31.4 1.5 collective-permute-start
  32.9 1.3 collective-permute-start.6
  34.2 1.5 collective-permute-start.7
  35.7 1.9 collective-permute-start.8
  37.9 8.0 %collective-permute-done.refs_1_ = bf16[1024,256]{1,0:T(8,128)(2,1)S(1)} collective-permute-done((bf16[1024,256]{1,0:T(8,128)(2,1)S(1)}, bf16[1024,256]{1,0:T(8,128)(2,1)S(1)}, u32[]{:S(2)}, u32[]{:S(2)}) %collective-permute-start) | collective-permute-done | bytes 524320 | tf_op jit(solution)/shard_map/ppermute | solution.py:381
  47.2 10.0 %collective-permute-done.6.refs_1_ = bf16[64,4096]{1,0:T(8,128)(2,1)S(1)} collective-permute-done((bf16[64,4096]{1,0:T(8,128)(2,1)S(1)}, bf16[64,4096]{1,0:T(8,128)(2,1)S(1)}, u32[]{:S(2)}, u32[]{:S(2)}) %collective-permute-start.6) | collective-permute-done | bytes 524320 | tf_op jit(solution)/shard_map/ppermute | solution.py:381
  57.2 12.2 %collective-permute-done.7.refs_2_ = bf16[64,4096]{1,0:T(8,128)(2,1)S(1)} collective-permute-done((bf16[64,4096]{1,0:T(8,128)(2,1)S(1)}, bf16[64,4096]{1,0:T(8,128)(2,1)S(1)}, u32[]{:S(2)}, u32[]{:S(2)}) %collective-permute-start.7) | collective-permute-done | bytes 524320 | tf_op jit(solution)/shard_map/ppermute | solution.py:381
  70.5 3.0 %stack_down.1.refs_8_ = bf16[256,4096]{1,0:T(8,128)(2,1)} custom-call(s32[1]{0:T(128)} %bitcast.t_ref, bf16[64,4096]{1,0:T(8,128)(2,1)} %bitcast.9, bf16[64,4096]{1,0:T(8,128)(2,1)} %copy-done.4, bf16[64,4096]{1,0:T(8,128)(2,1)} %copy-done.5, bf16[64,4096]{1,0:T(8,128)(2,1)} %copy-done.6), custom_call_target="tpu_custom_call" | custom-call | flops 262144 | bytes 4194304 | tf_op jit(solution)/shard_map/stack_down/pallas_call | solution.py:109
  73.4 7.3 %collective-permute-done.1.refs_2_ = bf16[1024,256]{1,0:T(8,128)(2,1)} collective-permute-done((bf16[1024,256]{1,0:T(8,128)(2,1)S(1)}, bf16[1024,256]{1,0:T(8,128)(2,1)}, u32[]{:S(2)}, u32[]{:S(2)}) %collective-permute-start.1) | collective-permute-done | bytes 524320 | tf_op jit(solution)/shard_map/ppermute | solution.py:381
  80.7 1.5 collective-permute-done.2.refs_3_
  82.2 12.1 %collective-permute-done.3.refs_5_ = bf16[1024,256]{1,0:T(8,128)(2,1)} collective-permute-done((bf16[1024,256]{1,0:T(8,128)(2,1)}, bf16[1024,256]{1,0:T(8,128)(2,1)}, u32[]{:S(2)}, u32[]{:S(2)}) %collective-permute-start.3) | collective-permute-done | bytes 524320 | tf_op jit(solution)/shard_map/ppermute | solution.py:381
  94.4 8.5 %collective-permute-done.4.refs_6_ = bf16[1024,256]{1,0:T(8,128)(2,1)} collective-permute-done((bf16[1024,256]{1,0:T(8,128)(2,1)}, bf16[1024,256]{1,0:T(8,128)(2,1)}, u32[]{:S(2)}, u32[]{:S(2)}) %collective-permute-start.4) | collective-permute-done | bytes 524320 | tf_op jit(solution)/shard_map/ppermute | solution.py:381
  103.7 26.3 %all-to-all-done.recv_ref = bf16[32,8,4096]{2,1,0:T(8,128)(2,1)S(1)} async-done(((bf16[32,8,4096]{2,1,0:T(8,128)(2,1)}), bf16[32,8,4096]{2,1,0:T(8,128)(2,1)S(1)}, u32[]{:S(2)}, u32[]{:S(2)}) %all-to-all-start) | async-done | bytes 2097184 | tf_op jit(solution)/shard_map/all_to_all | solution.py:389
  130.0 1.3 copy-done
  131.4 10.4 %expert_round.1 = (bf16[32,8,2048]{2,1,0:T(8,128)(2,1)}, bf16[128,768]{1,0:T(8,128)(2,1)}) custom-call(s32[1]{0:T(128)} %bitcast.t_ref, bf16[32,8,4096]{2,1,0:T(8,128)(2,1)} %copy-done, bf16[1024,256]{1,0:T(8,128)(2,1)} %bitcast.13, bf16[1024,256]{1,0:T(8,128)(2,1)} %copy-done.3, bf16[1024,256]{1,0:T(8,128)(2,1)} %collective-permute-done.1.refs_2_, ...), custom_call_target="tpu_custom_call" | custom-call | flops 1342177280 | bytes 9437184 | tf_op jit(solution)/shard_map/expert_round/pallas_call | solution.py:194
  141.7 5.3 %all-to-all-start.1 = ((bf16[32,8,2048]{2,1,0:T(8,128)(2,1)}), bf16[32,8,2048]{2,1,0:T(8,128)(2,1)S(1)}, u32[]{:S(2)}, u32[]{:S(2)}) async-start(bf16[32,8,2048]{2,1,0:T(8,128)(2,1)} %get-tuple-element.20), calls=%async_computation.1 | async-start | bytes 2097152 | tf_op jit(solution)/shard_map/all_to_all | solution.py:394
  147.0 3.4 %shard_map.103 = (bf16[160,1024]{1,0:T(8,128)(2,1)}, bf16[160,1024]{1,0:T(8,128)(2,1)}, bf16[160,1024]{1,0:T(8,128)(2,1)}, bf16[160,1024]{1,0:T(8,128)(2,1)}) custom-call(s32[1]{0:T(128)} %bitcast.t_ref, bf16[32,8,4096]{2,1,0:T(8,128)(2,1)} %copy-done, bf16[128,768]{1,0:T(8,128)(2,1)} %get-tuple-element.21.h_ref), custom_call_target="tpu_custom_call" | custom-call | flops 524288 | bytes 3145728 | tf_op jit(solution)/shard_map/pallas_call | solution.py:236
  150.4 1.5 collective-permute-start.12
  151.9 3.5 %shard_map.102 = (bf16[192,1024]{1,0:T(8,128)(2,1)}, bf16[192,1024]{1,0:T(8,128)(2,1)}, bf16[192,1024]{1,0:T(8,128)(2,1)}, bf16[192,1024]{1,0:T(8,128)(2,1)}) custom-call(s32[1]{0:T(128)} %bitcast.t_ref, bf16[32,8,4096]{2,1,0:T(8,128)(2,1)} %copy-done, bf16[128,768]{1,0:T(8,128)(2,1)} %get-tuple-element.21.h_ref), custom_call_target="tpu_custom_call" | custom-call | flops 524288 | bytes 3145728 | tf_op jit(solution)/shard_map/pallas_call | solution.py:236
  156.7 1.5 collective-permute-start.13
  158.2 2.0 collective-permute-start.14
  162.1 15.2 %collective-permute-done.13.refs_2_ = bf16[160,1024]{1,0:T(8,128)(2,1)S(1)} collective-permute-done((bf16[160,1024]{1,0:T(8,128)(2,1)S(1)}, bf16[160,1024]{1,0:T(8,128)(2,1)S(1)}, u32[]{:S(2)}, u32[]{:S(2)}) %collective-permute-start.13) | collective-permute-done | bytes 327712 | tf_op jit(solution)/shard_map/ppermute | solution.py:381
  178.1 2.6 %grads_down.1 = (bf16[64,1024]{1,0:T(8,128)(2,1)}, bf16[64,1024]{1,0:T(8,128)(2,1)}, bf16[64,1024]{1,0:T(8,128)(2,1)}, bf16[64,1024]{1,0:T(8,128)(2,1)}) custom-call(s32[1]{0:T(128)} %bitcast.t_ref, bf16[160,1024]{1,0:T(8,128)(2,1)} %get-tuple-element.28.refs_0_, bf16[160,1024]{1,0:T(8,128)(2,1)} %copy-done.8, bf16[160,1024]{1,0:T(8,128)(2,1)} %copy-done.9, ...), custom_call_target="tpu_custom_call" | custom-call | flops 268435456 | bytes 2097152 | tf_op jit(solution)/shard_map/grads_down/pallas_call | solution.py:280
  180.7 1.6 collective-permute-start.16
  183.6 2.1 %collective-permute-done.10.refs_2_ = bf16[192,1024]{1,0:T(8,128)(2,1)S(1)} collective-permute-done((bf16[192,1024]{1,0:T(8,128)(2,1)}, bf16[192,1024]{1,0:T(8,128)(2,1)S(1)}, u32[]{:S(2)}, u32[]{:S(2)}) %collective-permute-start.10) | collective-permute-done | bytes 393248 | tf_op jit(solution)/shard_map/ppermute | solution.py:381
  185.7 5.1 %collective-permute-done.11.refs_3_ = bf16[192,1024]{1,0:T(8,128)(2,1)S(1)} collective-permute-done((bf16[192,1024]{1,0:T(8,128)(2,1)}, bf16[192,1024]{1,0:T(8,128)(2,1)S(1)}, u32[]{:S(2)}, u32[]{:S(2)}) %collective-permute-start.11) | collective-permute-done | bytes 393248 | tf_op jit(solution)/shard_map/ppermute | solution.py:381
  191.6 3.1 %grads_up.1 = (bf16[1024,256]{1,0:T(8,128)(2,1)}, bf16[1024,256]{1,0:T(8,128)(2,1)}) custom-call(bf16[192,1024]{1,0:T(8,128)(2,1)} %get-tuple-element.22.refs_0_, bf16[192,1024]{1,0:T(8,128)(2,1)} %copy-done.15, bf16[192,1024]{1,0:T(8,128)(2,1)} %copy-done.16, bf16[192,1024]{1,0:T(8,128)(2,1)} %copy-done.17), custom_call_target="tpu_custom_call" | custom-call | flops 536870912 | bytes 3145728 | tf_op jit(solution)/shard_map/grads_up/pallas_call | solution.py:294
  195.8 1.9 place.1
  197.8 4.7 %all-to-all-done.1.refs_0_ = bf16[32,8,2048]{2,1,0:T(8,128)(2,1)S(1)} async-done(((bf16[32,8,2048]{2,1,0:T(8,128)(2,1)}), bf16[32,8,2048]{2,1,0:T(8,128)(2,1)S(1)}, u32[]{:S(2)}, u32[]{:S(2)}) %all-to-all-start.1) | async-done | bytes 1048608 | tf_op jit(solution)/shard_map/all_to_all | solution.py:394
  202.5 1.8 combine.1
  (58 shorter events, 10.7 us)
Async XLA Ops:
  5.8 25.6 %copy-start.2 = (bf16[1,1024,256]{2,1,0:T(8,128)(2,1)S(1)}, bf16[1,1024,256]{2,1,0:T(8,128)(2,1)}, u32[]{:S(2)}) copy-start(bf16[1,1024,256]{2,1,0:T(8,128)(2,1)} %param.11) | copy-start | bytes 1572868
  5.8 27.1 %copy-start.1 = (bf16[1,64,4096]{2,1,0:T(8,128)(2,1)S(1)}, bf16[1,64,4096]{2,1,0:T(8,128)(2,1)}, u32[]{:S(2)}) copy-start(bf16[1,64,4096]{2,1,0:T(8,128)(2,1)} %param.13) | copy-start | bytes 1572868
  5.8 124.2 %all-to-all-start = ((bf16[32,8,4096]{2,1,0:T(8,128)(2,1)}), bf16[32,8,4096]{2,1,0:T(8,128)(2,1)S(1)}, u32[]{:S(2)}, u32[]{:S(2)}) async-start(bf16[32,8,4096]{2,1,0:T(8,128)(2,1)} %dispatch.1), calls=%async_computation | async-start | bytes 4194304 | tf_op jit(solution)/shard_map/all_to_all | solution.py:389
  31.4 14.6 %collective-permute-start = (bf16[1024,256]{1,0:T(8,128)(2,1)S(1)}, bf16[1024,256]{1,0:T(8,128)(2,1)S(1)}, u32[]{:S(2)}, u32[]{:S(2)}) collective-permute-start(bf16[1024,256]{1,0:T(8,128)(2,1)S(1)} %bitcast.14), channel_id=1, source_target_pairs={{0,1},{1,2},{2,3},{3,0},{4,5},{5,6},{6,7},{7,4},{8,9},{9,10},{10,1... | collective-permute-start | bytes 1572872 | tf_op jit(solution)/shard_map/ppermute | solution.py:381
  32.9 24.3 %collective-permute-start.6 = (bf16[64,4096]{1,0:T(8,128)(2,1)S(1)}, bf16[64,4096]{1,0:T(8,128)(2,1)S(1)}, u32[]{:S(2)}, u32[]{:S(2)}) collective-permute-start(bf16[64,4096]{1,0:T(8,128)(2,1)S(1)} %bitcast.10), channel_id=1, source_target_pairs={{0,1},{1,2},{2,3},{3,0},{4,5},{5,6},{6,7},{7,4},{8,9},{9,10},{10,1... | collective-permute-start | bytes 1572872 | tf_op jit(solution)/shard_map/ppermute | solution.py:381
  34.2 35.2 %collective-permute-start.7 = (bf16[64,4096]{1,0:T(8,128)(2,1)S(1)}, bf16[64,4096]{1,0:T(8,128)(2,1)S(1)}, u32[]{:S(2)}, u32[]{:S(2)}) collective-permute-start(bf16[64,4096]{1,0:T(8,128)(2,1)S(1)} %bitcast.11), channel_id=1, source_target_pairs={{0,2},{1,3},{2,0},{3,1},{4,6},{5,7},{6,4},{7,5},{8,10},{9,11},{10,... | collective-permute-start | bytes 1572872 | tf_op jit(solution)/shard_map/ppermute | solution.py:381
  35.7 33.9 %collective-permute-start.8 = (bf16[64,4096]{1,0:T(8,128)(2,1)S(1)}, bf16[64,4096]{1,0:T(8,128)(2,1)S(1)}, u32[]{:S(2)}, u32[]{:S(2)}) collective-permute-start(bf16[64,4096]{1,0:T(8,128)(2,1)S(1)} %bitcast.12), channel_id=1, source_target_pairs={{0,3},{1,0},{2,1},{3,2},{4,7},{5,4},{6,5},{7,6},{8,11},{9,8},{10,9... | collective-permute-start | bytes 1572872 | tf_op jit(solution)/shard_map/ppermute | solution.py:381
  37.7 43.1 %collective-permute-start.1 = (bf16[1024,256]{1,0:T(8,128)(2,1)S(1)}, bf16[1024,256]{1,0:T(8,128)(2,1)}, u32[]{:S(2)}, u32[]{:S(2)}) collective-permute-start(bf16[1024,256]{1,0:T(8,128)(2,1)S(1)} %bitcast.15), channel_id=1, source_target_pairs={{0,2},{1,3},{2,0},{3,1},{4,6},{5,7},{6,4},{7,5},{8,10},{9,11},{10,... | collective-permute-start | bytes 1572872 | tf_op jit(solution)/shard_map/ppermute | solution.py:381
  46.0 23.7 %copy-start.3 = (bf16[1024,256]{1,0:T(8,128)(2,1)}, bf16[1024,256]{1,0:T(8,128)(2,1)S(1)}, u32[]{:S(2)}) copy-start(bf16[1024,256]{1,0:T(8,128)(2,1)S(1)} %collective-permute-done.refs_1_) | copy-start | bytes 1572868
  46.0 36.3 %collective-permute-start.2 = (bf16[1024,256]{1,0:T(8,128)(2,1)S(1)}, bf16[1024,256]{1,0:T(8,128)(2,1)}, u32[]{:S(2)}, u32[]{:S(2)}) collective-permute-start(bf16[1024,256]{1,0:T(8,128)(2,1)S(1)} %bitcast.16), channel_id=1, source_target_pairs={{0,3},{1,0},{2,1},{3,2},{4,7},{5,4},{6,5},{7,6},{8,11},{9,8},{10,9... | collective-permute-start | bytes 1572872 | tf_op jit(solution)/shard_map/ppermute | solution.py:381
  57.2 12.8 %copy-start.4 = (bf16[64,4096]{1,0:T(8,128)(2,1)}, bf16[64,4096]{1,0:T(8,128)(2,1)S(1)}, u32[]{:S(2)}) copy-start(bf16[64,4096]{1,0:T(8,128)(2,1)S(1)} %collective-permute-done.6.refs_1_) | copy-start | bytes 1572868
  57.2 37.2 %collective-permute-start.3 = (bf16[1024,256]{1,0:T(8,128)(2,1)}, bf16[1024,256]{1,0:T(8,128)(2,1)}, u32[]{:S(2)}, u32[]{:S(2)}) collective-permute-start(bf16[1024,256]{1,0:T(8,128)(2,1)} %bitcast.17), channel_id=1, source_target_pairs={{0,1},{1,2},{2,3},{3,0},{4,5},{5,6},{6,7},{7,4},{8,9},{9,10},{10,1... | collective-permute-start | bytes 1572872 | tf_op jit(solution)/shard_map/ppermute | solution.py:381
  69.4 33.5 %collective-permute-start.4 = (bf16[1024,256]{1,0:T(8,128)(2,1)}, bf16[1024,256]{1,0:T(8,128)(2,1)}, u32[]{:S(2)}, u32[]{:S(2)}) collective-permute-start(bf16[1024,256]{1,0:T(8,128)(2,1)} %bitcast.18), channel_id=1, source_target_pairs={{0,2},{1,3},{2,0},{3,1},{4,6},{5,7},{6,4},{7,5},{8,10},{9,11},{10,... | collective-permute-start | bytes 1572872 | tf_op jit(solution)/shard_map/ppermute | solution.py:381
  69.7 34.0 %collective-permute-start.5 = (bf16[1024,256]{1,0:T(8,128)(2,1)}, bf16[1024,256]{1,0:T(8,128)(2,1)S(1)}, u32[]{:S(2)}, u32[]{:S(2)}) collective-permute-start(bf16[1024,256]{1,0:T(8,128)(2,1)} %bitcast.19), channel_id=1, source_target_pairs={{0,3},{1,0},{2,1},{3,2},{4,7},{5,4},{6,5},{7,6},{8,11},{9,8},{10,9... | collective-permute-start | bytes 1572872 | tf_op jit(solution)/shard_map/ppermute | solution.py:381
  103.7 26.3 %copy-start.7 = (bf16[1024,256]{1,0:T(8,128)(2,1)}, bf16[1024,256]{1,0:T(8,128)(2,1)S(1)}, u32[]{:S(2)}) copy-start(bf16[1024,256]{1,0:T(8,128)(2,1)S(1)} %collective-permute-done.5.refs_7_) | copy-start | bytes 1572868
  130.0 1.3 copy-start
  141.7 60.8 %all-to-all-start.1 = ((bf16[32,8,2048]{2,1,0:T(8,128)(2,1)}), bf16[32,8,2048]{2,1,0:T(8,128)(2,1)S(1)}, u32[]{:S(2)}, u32[]{:S(2)}) async-start(bf16[32,8,2048]{2,1,0:T(8,128)(2,1)} %get-tuple-element.20), calls=%async_computation.1 | async-start | bytes 2097152 | tf_op jit(solution)/shard_map/all_to_all | solution.py:394
  150.4 6.3 %copy-start.19 = (bf16[160,1024]{1,0:T(8,128)(2,1)S(1)}, bf16[160,1024]{1,0:T(8,128)(2,1)}, u32[]{:S(2)}) copy-start(bf16[160,1024]{1,0:T(8,128)(2,1)} %get-tuple-element.30) | copy-start | bytes 983044
  150.4 7.8 %copy-start.18 = (bf16[160,1024]{1,0:T(8,128)(2,1)S(1)}, bf16[160,1024]{1,0:T(8,128)(2,1)}, u32[]{:S(2)}) copy-start(bf16[160,1024]{1,0:T(8,128)(2,1)} %get-tuple-element.31) | copy-start | bytes 983044
  150.4 33.1 %copy-start.14 = (s32[64,2]{0,1:T(2,128)S(1)}, s32[64,2]{0,1:T(2,128)}, u32[]{:S(2)}) copy-start(s32[64,2]{0,1:T(2,128)} %param.9) | copy-start | bytes 1540
  150.4 10.5 %collective-permute-start.12 = (bf16[160,1024]{1,0:T(8,128)(2,1)}, bf16[160,1024]{1,0:T(8,128)(2,1)S(1)}, u32[]{:S(2)}, u32[]{:S(2)}) collective-permute-start(bf16[160,1024]{1,0:T(8,128)(2,1)} %get-tuple-element.29), channel_id=1, source_target_pairs={{0,1},{1,2},{2,3},{3,0},{4,5},{5,6},{6,7},{7,4},{8,9},{9,10},{10,1... | collective-permute-start | bytes 983048 | tf_op jit(solution)/shard_map/ppermute | solution.py:381
  155.3 27.0 %collective-permute-start.9 = (bf16[192,1024]{1,0:T(8,128)(2,1)}, bf16[192,1024]{1,0:T(8,128)(2,1)S(1)}, u32[]{:S(2)}, u32[]{:S(2)}) collective-permute-start(bf16[192,1024]{1,0:T(8,128)(2,1)} %get-tuple-element.23), channel_id=1, source_target_pairs={{0,1},{1,2},{2,3},{3,0},{4,5},{5,6},{6,7},{7,4},{8,9},{9,10},{10,1... | collective-permute-start | bytes 1179656 | tf_op jit(solution)/shard_map/ppermute | solution.py:381
  156.7 20.6 %collective-permute-start.13 = (bf16[160,1024]{1,0:T(8,128)(2,1)S(1)}, bf16[160,1024]{1,0:T(8,128)(2,1)S(1)}, u32[]{:S(2)}, u32[]{:S(2)}) collective-permute-start(bf16[160,1024]{1,0:T(8,128)(2,1)S(1)} %copy-done.19), channel_id=1, source_target_pairs={{0,2},{1,3},{2,0},{3,1},{4,6},{5,7},{6,4},{7,5},{8,10},{9,11},{10,... | collective-permute-start | bytes 983048 | tf_op jit(solution)/shard_map/ppermute | solution.py:381
  158.2 19.1 %collective-permute-start.14 = (bf16[160,1024]{1,0:T(8,128)(2,1)S(1)}, bf16[160,1024]{1,0:T(8,128)(2,1)S(1)}, u32[]{:S(2)}, u32[]{:S(2)}) collective-permute-start(bf16[160,1024]{1,0:T(8,128)(2,1)S(1)} %copy-done.18), channel_id=1, source_target_pairs={{0,3},{1,0},{2,1},{3,2},{4,7},{5,4},{6,5},{7,6},{8,11},{9,8},{10,9... | collective-permute-start | bytes 983048 | tf_op jit(solution)/shard_map/ppermute | solution.py:381
  160.1 25.6 %collective-permute-start.10 = (bf16[192,1024]{1,0:T(8,128)(2,1)}, bf16[192,1024]{1,0:T(8,128)(2,1)S(1)}, u32[]{:S(2)}, u32[]{:S(2)}) collective-permute-start(bf16[192,1024]{1,0:T(8,128)(2,1)} %get-tuple-element.24), channel_id=1, source_target_pairs={{0,2},{1,3},{2,0},{3,1},{4,6},{5,7},{6,4},{7,5},{8,10},{9,11},{10,... | collective-permute-start | bytes 1179656 | tf_op jit(solution)/shard_map/ppermute | solution.py:381
  160.9 16.4 %copy-start.8 = (bf16[160,1024]{1,0:T(8,128)(2,1)}, bf16[160,1024]{1,0:T(8,128)(2,1)S(1)}, u32[]{:S(2)}) copy-start(bf16[160,1024]{1,0:T(8,128)(2,1)S(1)} %collective-permute-done.12.refs_1_) | copy-start | bytes 983044
  160.9 29.9 %collective-permute-start.11 = (bf16[192,1024]{1,0:T(8,128)(2,1)}, bf16[192,1024]{1,0:T(8,128)(2,1)S(1)}, u32[]{:S(2)}, u32[]{:S(2)}) collective-permute-start(bf16[192,1024]{1,0:T(8,128)(2,1)} %get-tuple-element.25), channel_id=1, source_target_pairs={{0,3},{1,0},{2,1},{3,2},{4,7},{5,4},{6,5},{7,6},{8,11},{9,8},{10,9... | collective-permute-start | bytes 1179656 | tf_op jit(solution)/shard_map/ppermute | solution.py:381
  180.7 14.0 %collective-permute-start.15 = (bf16[64,1024]{1,0:T(8,128)(2,1)}, bf16[64,1024]{1,0:T(8,128)(2,1)S(1)}, u32[]{:S(2)}, u32[]{:S(2)}) collective-permute-start(bf16[64,1024]{1,0:T(8,128)(2,1)} %get-tuple-element.33), channel_id=1, source_target_pairs={{0,1},{1,2},{2,3},{3,0},{4,5},{5,6},{6,7},{7,4},{8,9},{9,10},{10,1... | collective-permute-start | bytes 393224 | tf_op jit(solution)/shard_map/ppermute | solution.py:381
  180.7 14.0 %collective-permute-start.16 = (bf16[64,1024]{1,0:T(8,128)(2,1)}, bf16[64,1024]{1,0:T(8,128)(2,1)S(1)}, u32[]{:S(2)}, u32[]{:S(2)}) collective-permute-start(bf16[64,1024]{1,0:T(8,128)(2,1)} %get-tuple-element.34), channel_id=1, source_target_pairs={{0,2},{1,3},{2,0},{3,1},{4,6},{5,7},{6,4},{7,5},{8,10},{9,11},{10,... | collective-permute-start | bytes 393224 | tf_op jit(solution)/shard_map/ppermute | solution.py:381
  182.3 8.5 %copy-start.15 = (bf16[192,1024]{1,0:T(8,128)(2,1)}, bf16[192,1024]{1,0:T(8,128)(2,1)S(1)}, u32[]{:S(2)}) copy-start(bf16[192,1024]{1,0:T(8,128)(2,1)S(1)} %collective-permute-done.9.refs_1_) | copy-start | bytes 1179652
  182.3 12.9 %collective-permute-start.17 = (bf16[64,1024]{1,0:T(8,128)(2,1)}, bf16[64,1024]{1,0:T(8,128)(2,1)S(1)}, u32[]{:S(2)}, u32[]{:S(2)}) collective-permute-start(bf16[64,1024]{1,0:T(8,128)(2,1)} %get-tuple-element.35), channel_id=1, source_target_pairs={{0,3},{1,0},{2,1},{3,2},{4,7},{5,4},{6,5},{7,6},{8,11},{9,8},{10,9... | collective-permute-start | bytes 393224 | tf_op jit(solution)/shard_map/ppermute | solution.py:381
  185.7 5.1 %copy-start.16 = (bf16[192,1024]{1,0:T(8,128)(2,1)}, bf16[192,1024]{1,0:T(8,128)(2,1)S(1)}, u32[]{:S(2)}) copy-start(bf16[192,1024]{1,0:T(8,128)(2,1)S(1)} %collective-permute-done.10.refs_2_) | copy-start | bytes 1179652
  (8 other events, 5.9 us)

commit v6 on v4

--- a/solution.py
+++ b/solution.py
@@ -12,6 +12,7 @@
 F32 = jnp.float32
 VMEM = pl.BlockSpec(memory_space=pltpu.VMEM)
 SMEM = pl.BlockSpec(memory_space=pltpu.SMEM)
+HBM = pl.BlockSpec(memory_space=pltpu.HBM)
 PARTS = 4
 STEPS = 4
 
@@ -95,93 +96,111 @@
     )(ids2, gates2, *([tokens, cotangent] * 4))
 
 
-def stack_kernel(t_ref, *refs):
-    out = refs[-1]
-    part = refs[0].shape[0]
+def stack_kernel(at_ref, *refs):
+    wg, wu, wd, out = refs[:PARTS], refs[PARTS : 2 * PARTS], refs[2 * PARTS : 3 * PARTS], refs[-1]
+    width, ff = wg[0].shape
+    part, d = wd[0].shape
     for k in range(PARTS):
-        at = pl.multiple_of(lax.rem(t_ref[0] - k + PARTS, PARTS) * part, part)
-        out[pl.ds(at, part), :] = refs[k][...]
-
-
-def stack_down(t, pieces):
-    part, d = pieces[0].shape
+        owner = lax.rem(at_ref[0] - k + PARTS, PARTS)
+        rows = pl.ds(pl.multiple_of(owner * width, width), width)
+        out[rows, 0:ff] = wg[k][...]
+        out[rows, ff:] = wu[k][...]
+        for b in range(d // (2 * ff)):
+            at = pl.multiple_of(d + b * ff + owner * part, part)
+            out[pl.ds(at, part), :] = wd[k][:, b * 2 * ff : (b + 1) * 2 * ff]
+
+
+def stack(t, wg, wu, wd):
+    _, ff = wg[0].shape
+    d = wd[0].shape[1]
     return pl.pallas_call(
         stack_kernel,
-        in_specs=[SMEM] + [VMEM] * PARTS,
+        in_specs=[SMEM] + [VMEM] * (3 * PARTS),
         out_specs=VMEM,
-        out_shape=jax.ShapeDtypeStruct((part * PARTS, d), BF),
-        cost_estimate=cost(part * d, 4 * part * d * 4),
-        compiler_params=pltpu.CompilerParams(vmem_limit_bytes=10 << 20),
-        name="stack_down",
-    )(t, *pieces)
-
-
-def unpack(recv_ref, flat, kinds):
-    sources = recv_ref.shape[0]
+        out_shape=struct(d + d // 2, 2 * ff),
+        cost_estimate=cost(3 * d * ff, 12 * d * ff),
+        name="stack",
+    )(t, *wg, *wu, *wd)
+
+
+def widen(recv_ref, flat):
+    for b in range(flat.shape[0]):
+        flat[b] = recv_ref[:, :, b * 128 : (b + 1) * 128].astype(F32).reshape(flat.shape[1:])
+
+
+def unpack(flat, sources, q, kinds):
     d = kinds[0][1].shape[1]
     count = kinds[0][1].shape[0] // sources
     lanes = d // 4 // STEPS
     blocks = lanes // 128
-    for b in range(flat.shape[0]):
-        flat[b] = recv_ref[:, :, b * 128 : (b + 1) * 128].astype(F32).reshape(flat.shape[1:])
     for step in range(STEPS):
         for p in range(count):
             for b in range(blocks):
-                for q in range(4):
-                    col = q * (d // 4) + step * lanes + b * 128
-                    for kind, dst in kinds:
-                        v = flat[(step * count + p) * blocks + b, pl.ds(2 * q + kind, sources, stride=8), :]
-                        dst[p * sources : (p + 1) * sources, col : col + 128] = v.astype(BF)
+                col = q * (d // 4) + step * lanes + b * 128
+                for kind, dst in kinds:
+                    v = flat[(step * count + p) * blocks + b, pl.ds(2 * q + kind, sources, stride=8), :]
+                    dst[p * sources : (p + 1) * sources, col : col + 128] = v.astype(BF)
 
 
 def flat_scratch(recv):
     return pltpu.VMEM((recv.shape[2] // 128, recv.shape[0] * 8, 128), F32)
 
 
-def expert_kernel(count, t_ref, recv_ref, *refs):
-    wg, wu, wd, (msg_ref, h_ref, flat, x, c, back, ret) = (
-        refs[:PARTS],
-        refs[PARTS : 2 * PARTS],
-        refs[2 * PARTS],
-        refs[2 * PARTS + 1 :],
-    )
-    t = t_ref[0]
-    width, ff = wg[0].shape
-    d = wd.shape[1]
+def expert_kernel(count, recv_ref, w_ref, msg_ref, h_ref, flat, x, c, back, ret, wgu, wd, sem_w):
     sources = recv_ref.shape[0]
-    unpack(recv_ref, flat, [(0, x), (1, c)])
-    cols = [pl.ds(pl.multiple_of(lax.rem(t - k + PARTS, PARTS) * width, width), width) for k in range(PARTS)]
-    pre_gate = functools.reduce(lambda a, b: a + b, [nn(x[:, cols[k]], wg[k][...]) for k in range(PARTS)])
-    pre_up = functools.reduce(lambda a, b: a + b, [nn(x[:, cols[k]], wu[k][...]) for k in range(PARTS)])
-    grad_hidden = nt(c[...], wd[...])
+    d = x.shape[1]
+    width = d // 4
+    ff = wgu.shape[1] // 2
+    weights_in = [
+        pltpu.make_async_copy(
+            w_ref.at[pl.ds(q * width, width), :], wgu.at[pl.ds(q * width, width), :], sem_w.at[q]
+        )
+        for q in range(4)
+    ] + [pltpu.make_async_copy(w_ref.at[pl.ds(d, d // 2), :], wd, sem_w.at[4])]
+    for copy in weights_in:
+        copy.start()
+    widen(recv_ref, flat)
+    pre = jnp.zeros((x.shape[0], 2 * ff), F32)
+    for q in range(4):
+        unpack(flat, sources, q, [(0, x), (1, c)])
+        weights_in[q].wait()
+        cols = slice(q * width, (q + 1) * width)
+        pre += nn(x[:, cols], wgu[cols, :])
+    weights_in[4].wait()
+    grad_hidden = jnp.zeros((x.shape[0], ff), F32)
+    for b in range(d // (2 * ff)):
+        grad_hidden += nt(c[:, b * 2 * ff : (b + 1) * 2 * ff], wd[b * ff : (b + 1) * ff, :])
+    pre_gate, pre_up = pre[:, :ff], pre[:, ff:]
     sig = jax.nn.sigmoid(pre_gate)
     activated = pre_gate * sig
     grad_gate_pre = (grad_hidden * pre_up * sig * (1.0 + pre_gate * (1.0 - sig))).astype(BF)
     grad_up_pre = (grad_hidden * activated).astype(BF)
-    h_ref[:, 0:ff] = (activated * pre_up).astype(BF)
-    h_ref[:, ff : 2 * ff] = grad_gate_pre
-    h_ref[:, 2 * ff :] = grad_up_pre
-    for k in range(PARTS):
-        back[:, cols[k]] = nt(grad_gate_pre, wg[k][...]) + nt(grad_up_pre, wu[k][...])
+    hidden = (activated * pre_up).astype(BF)
+    both = jnp.concatenate([grad_gate_pre, grad_up_pre], axis=1)
+    for q in range(4):
+        cols = slice(q * width, (q + 1) * width)
+        back[:, cols] = nt(both, wgu[cols, :])
     eighth = d // 8
+    blocks = eighth // 128
     for p in range(count):
-        for b in range(eighth // 128):
+        for b in range(blocks):
             for o in range(8):
                 col = o * eighth + b * 128
-                ret[p * (eighth // 128) + b, pl.ds(o, sources, stride=8), :] = back[
-                    p * sources : (p + 1) * sources, col : col + 128
-                ]
-    for b in range(ret.shape[0]):
-        msg_ref[:, :, b * 128 : (b + 1) * 128] = ret[b].reshape(sources, 8, 128).astype(BF)
-
-
-def expert_round(t, recv, wg, wu, wd, count):
+                ret[p * blocks + b, pl.ds(o, sources, stride=8), :] = back[p * sources : (p + 1) * sources, col : col + 128]
+        for b in range(blocks):
+            at = p * eighth + b * 128
+            msg_ref[:, :, at : at + 128] = ret[p * blocks + b].reshape(sources, 8, 128).astype(BF)
+    h_ref[:, 0:ff] = hidden
+    h_ref[:, ff:] = both
+
+
+def expert_round(recv, weights, ff, count):
     sources = recv.shape[0]
-    ff, d = wd.shape
+    d = recv.shape[2] * 4 // count
     rows = sources * count
     return pl.pallas_call(
         functools.partial(expert_kernel, count),
-        in_specs=[SMEM] + [VMEM] * (2 + 2 * PARTS),
+        in_specs=[VMEM, HBM],
         out_specs=[VMEM] * 2,
         out_shape=[struct(sources, 8, count * d // 8), struct(rows, 3 * ff)],
         scratch_shapes=[
@@ -190,16 +209,21 @@
             pltpu.VMEM((rows, d), BF),
             pltpu.VMEM((rows, d), F32),
             pltpu.VMEM((count * d // 8 // 128, sources * 8, 128), F32),
+            pltpu.VMEM((d, 2 * ff), BF),
+            pltpu.VMEM((d // 2, 2 * ff), BF),
+            pltpu.SemaphoreType.DMA((5,)),
         ],
         cost_estimate=cost(2 * rows * d * 5 * ff, 3 * ff * d * 2 + 3 * rows * d * 2),
-        compiler_params=pltpu.CompilerParams(vmem_limit_bytes=28 << 20),
+        compiler_params=pltpu.CompilerParams(vmem_limit_bytes=50 << 20),
         name="expert_round",
-    )(t, recv, *wg, *wu, wd)
+    )(recv, weights)
 
 
 def spread_kernel(kind, first, wide, t_ref, recv_ref, h_ref, *refs):
     boxes, (flat, x) = refs[:PARTS], refs[PARTS:]
-    unpack(recv_ref, flat, [(kind, x)])
+    widen(recv_ref, flat)
+    for q in range(4):
+        unpack(flat, recv_ref.shape[0], q, [(kind, x)])
     rows, d = x.shape
     width = d // PARTS
     folds = width // wide
@@ -223,7 +247,7 @@
             out_shape=[struct(rows + rows * wide // width, width)] * PARTS,
             scratch_shapes=[flat_scratch(recv), pltpu.VMEM((rows, d), BF)],
             cost_estimate=cost(rows * d, 6 * rows * d),
-            compiler_params=pltpu.CompilerParams(vmem_limit_bytes=20 << 20),
+            compiler_params=pltpu.CompilerParams(vmem_limit_bytes=50 << 20),
         )(t, recv, h)
     )
 
@@ -267,7 +291,6 @@
         out_shape=[struct(ff // PARTS, width)] * PARTS,
         scratch_shapes=[pltpu.VMEM((rows, width), BF), pltpu.VMEM((rows, ff), BF)],
         cost_estimate=cost(2 * rows * width * ff, 2 * rows * width * 2),
-        compiler_params=pltpu.CompilerParams(vmem_limit_bytes=12 << 20),
         name="grads_down",
     )(t, *boxes)
 
@@ -282,7 +305,6 @@
         out_shape=[struct(width, ff)] * 2,
         scratch_shapes=[pltpu.VMEM((rows, width), BF), pltpu.VMEM((rows, 2 * ff), BF)],
         cost_estimate=cost(4 * rows * width * ff, 3 * rows * width * 2),
-        compiler_params=pltpu.CompilerParams(vmem_limit_bytes=14 << 20),
         name="grads_up",
     )(*boxes)
 
@@ -350,7 +372,6 @@
         out_specs=VMEM,
         out_shape=jax.ShapeDtypeStruct((rows, width * len(pieces)), BF),
         cost_estimate=cost(rows * width, 4 * rows * width * 4),
-        compiler_params=pltpu.CompilerParams(vmem_limit_bytes=6 << 20),
         name="place",
     )(t, *pieces)
 
@@ -374,9 +395,9 @@
     for send in sends:
         recvs.append(lax.all_to_all(send, "expert", 0, 0, tiled=True))
     wg, wu, wd = everyone(w_gate[0]), everyone(w_up[0]), everyone(w_down[0])
-    wd = stack_down(t, wd)
+    weights = stack(t, wg, wu, wd)
     (recv,), (count,) = recvs, split
-    msg, h = expert_round(t, recv, wg, wu, wd, count)
+    msg, h = expert_round(recv, weights, ff, count)
     rets = [lax.all_to_all(msg, "expert", 0, 0, tiled=True)]
     boxes_c = spread(t, recv, h, 1, 0, ff)
     boxes_c = boxes_c[:1] + [shift(boxes_c[k], k) for k in range(1, PARTS)]

time: 205 us -> 200 us (0.976)
  waiting for transfers between devices: 121 us -> 109 us
  Pallas kernels: 19.1 us -> 29.4 us
  local copies, waits for them, and re-layouts: 13.4 us -> 5.66 us
  starting transfers between devices: 49.5 us -> 54.7 us
    unnamed x35 -> x41, local copies, waits for them, and re-layouts: 13.4 us -> 5.66 us
    all_to_all x1, waiting for transfers between devices: 26.3 us -> 20.1 us  [local(): recvs.append(lax.all_to_all(send, 'expert', 0, 0, tiled=True))]
    pallas_call x2, Pallas kernels: 6.73 us -> 12.1 us  [the longest x1 6.2 us: expert_round(): pl.pallas_call(functools.partial(expert_kernel, count), in_specs=[VMEM, H...]
    ppermute x18, starting transfers between devices: 18.6 us -> 23.9 us  [shift(): lax.ppermute(x, 'tensor', [(s, (s + k) % PARTS) for s in range(PARTS)])]
    ppermute x18, waiting for transfers between devices: 83.7 us -> 80.5 us  [shift(): lax.ppermute(x, 'tensor', [(s, (s + k) % PARTS) for s in range(PARTS)])]
    all_to_all x1, waiting for transfers between devices: 11 us -> 8.57 us  [local(): rets = [lax.all_to_all(msg, 'expert', 0, 0, tiled=True)]]
    pallas_call x1, Pallas kernels: 0.48 us -> 2.57 us  [grads_down(): pl.pallas_call(grads_down_kernel, in_specs=[SMEM] + [VMEM] * PARTS, out_s...]
  transfers between devices with their start and end apart: 20 -> 20, of which waited for: 15 -> 13; matrix products, arithmetic and copies ran while one was open for 0% -> 0% of each run, Pallas kernels for 3% -> 8%
where the time goes in v6:
time: 200 us
  waiting for transfers between devices  109 us (54%)
  starting transfers between devices  54.7 us (27%)
  Pallas kernels  29.4 us (15%)
  local copies, waits for them, and re-layouts  5.66 us (3%)
    ppermute x18, waiting for transfers between devices, shift(): lax.ppermute(x, 'tensor', [(s, (s + k) % PARTS) for s in range(PARTS)])  80.5 us
    all_to_all x1, starting transfers between devices, local(): recvs.append(lax.all_to_all(send, 'expert', 0, 0, tiled=True))  25.6 us
    ppermute x18, starting transfers between devices, shift(): lax.ppermute(x, 'tensor', [(s, (s + k) % PARTS) for s in range(PARTS)])  23.9 us
    all_to_all x1, waiting for transfers between devices, local(): recvs.append(lax.all_to_all(send, 'expert', 0, 0, tiled=True))  20.1 us
    all_to_all x1, waiting for transfers between devices, local(): rets = [lax.all_to_all(msg, 'expert', 0, 0, tiled=True)]  8.57 us
    pallas_call x1, Pallas kernels, expert_round(): pl.pallas_call(functools.partial(expert_kernel, count), in_specs=[VMEM, H...  6.2 us
    pallas_call x1, Pallas kernels, stack(): pl.pallas_call(stack_kernel, in_specs=[SMEM] + [VMEM] * (3 * PARTS), out_...  5.93 us
    unnamed x41, local copies, waits for them, and re-layouts  5.66 us
  transfers between devices with their start and end apart: 20, of which 13 were waited for; matrix products, arithmetic and copies ran while one was open for 0% of the time, Pallas kernels for 8%

profile of v6, /device:TPU:33, one launch (start us, length us, event | category | flops | bytes accessed | tf_op | source)
XLA Modules:
  0.0 199.8 jit_solution(11247205957076631748)
XLA Ops:
  0.6 5.2 %dispatch.1 = bf16[32,8,4096]{2,1,0:T(8,128)(2,1)} custom-call(s32[2,64]{1,0:T(2,128)} %bitcast.22, f32[2,64]{1,0:T(2,128)} %bitcast.23, bf16[64,4096]{1,0:T(8,128)(2,1)} %refs_6_.1, bf16[64,4096]{1,0:T(8,128)(2,1)} %refs_7_.1, bf16[64,4096]{1,0:T(8,128)(2,1)} %refs_6_.1, bf16[64,4096]{1,0:T(8,128)(2,1)} %refs_7_.1, bf16[64,4096]{1,0:T(8,128)(2,1)} %refs_6_.1, ...), custom_call_target="tpu_custom_call" | custom-call | flops 1073741824 | bytes 4194304 | tf_op jit(solution)/shard_map/dispatch/pallas_call | solution.py:87
  5.8 25.6 %all-to-all-start = ((bf16[32,8,4096]{2,1,0:T(8,128)(2,1)}), bf16[32,8,4096]{2,1,0:T(8,128)(2,1)S(1)}, u32[]{:S(2)}, u32[]{:S(2)}) async-start(bf16[32,8,4096]{2,1,0:T(8,128)(2,1)} %dispatch.1), calls=%async_computation | async-start | bytes 4194304 | tf_op jit(solution)/shard_map/all_to_all | solution.py:396
  31.5 1.5 collective-permute-start
  32.9 2.7 %collective-permute-start.1 = (bf16[1024,256]{1,0:T(8,128)(2,1)S(1)}, bf16[1024,256]{1,0:T(8,128)(2,1)S(1)}, u32[]{:S(2)}, u32[]{:S(2)}) collective-permute-start(bf16[1024,256]{1,0:T(8,128)(2,1)S(1)} %bitcast.11), channel_id=1, source_target_pairs={{0,2},{1,3},{2,0},{3,1},{4,6},{5,7},{6,4},{7,5},{8,10},{9,11},{10,... | collective-permute-start | bytes 1572872 | tf_op jit(solution)/shard_map/ppermute | solution.py:388
  37.9 8.2 %collective-permute-done.refs_1_ = bf16[1024,256]{1,0:T(8,128)(2,1)S(1)} collective-permute-done((bf16[1024,256]{1,0:T(8,128)(2,1)S(1)}, bf16[1024,256]{1,0:T(8,128)(2,1)S(1)}, u32[]{:S(2)}, u32[]{:S(2)}) %collective-permute-start) | collective-permute-done | bytes 524320 | tf_op jit(solution)/shard_map/ppermute | solution.py:388
  46.0 1.2 collective-permute-start.5
  47.2 11.0 %collective-permute-done.1.refs_2_ = bf16[1024,256]{1,0:T(8,128)(2,1)S(1)} collective-permute-done((bf16[1024,256]{1,0:T(8,128)(2,1)S(1)}, bf16[1024,256]{1,0:T(8,128)(2,1)S(1)}, u32[]{:S(2)}, u32[]{:S(2)}) %collective-permute-start.1) | collective-permute-done | bytes 524320 | tf_op jit(solution)/shard_map/ppermute | solution.py:388
  58.3 1.9 collective-permute-start.7
  60.2 8.3 %collective-permute-done.3.refs_5_ = bf16[1024,256]{1,0:T(8,128)(2,1)S(1)} collective-permute-done((bf16[1024,256]{1,0:T(8,128)(2,1)S(1)}, bf16[1024,256]{1,0:T(8,128)(2,1)S(1)}, u32[]{:S(2)}, u32[]{:S(2)}) %collective-permute-start.3) | collective-permute-done | bytes 524320 | tf_op jit(solution)/shard_map/ppermute | solution.py:388
  68.5 1.4 collective-permute-start.8
  69.9 11.0 %collective-permute-done.4.refs_6_ = bf16[1024,256]{1,0:T(8,128)(2,1)} collective-permute-done((bf16[1024,256]{1,0:T(8,128)(2,1)S(1)}, bf16[1024,256]{1,0:T(8,128)(2,1)}, u32[]{:S(2)}, u32[]{:S(2)}) %collective-permute-start.4) | collective-permute-done | bytes 524320 | tf_op jit(solution)/shard_map/ppermute | solution.py:388
  80.9 10.2 %collective-permute-done.6.refs_9_ = bf16[64,4096]{1,0:T(8,128)(2,1)} collective-permute-done((bf16[64,4096]{1,0:T(8,128)(2,1)}, bf16[64,4096]{1,0:T(8,128)(2,1)}, u32[]{:S(2)}, u32[]{:S(2)}) %collective-permute-start.6) | collective-permute-done | bytes 524320 | tf_op jit(solution)/shard_map/ppermute | solution.py:388
  91.1 12.2 %collective-permute-done.7.refs_10_ = bf16[64,4096]{1,0:T(8,128)(2,1)S(1)} collective-permute-done((bf16[64,4096]{1,0:T(8,128)(2,1)}, bf16[64,4096]{1,0:T(8,128)(2,1)S(1)}, u32[]{:S(2)}, u32[]{:S(2)}) %collective-permute-start.7) | collective-permute-done | bytes 524320 | tf_op jit(solution)/shard_map/ppermute | solution.py:388
  104.0 5.9 %stack.1.w_ref = bf16[6144,512]{1,0:T(8,128)(2,1)} custom-call(s32[1]{0:T(128)} %bitcast.2.at_ref.t_ref, bf16[1024,256]{1,0:T(8,128)(2,1)} %bitcast.9, bf16[1024,256]{1,0:T(8,128)(2,1)} %copy-done.5, bf16[1024,256]{1,0:T(8,128)(2,1)} %copy-done.6, bf16[1024,256]{1,0:T(8,128)(2,1)} %copy-done.7, bf16[1024,256]{1,0:T(8,128)(2,1)} %bitcast.13, ...), custom_call_target="tpu_custom_call" | custom-call | flops 3145728 | bytes 12582912 | tf_op jit(solution)/shard_map/stack/pallas_call | solution.py:116
  110.0 20.1 %all-to-all-done.recv_ref = bf16[32,8,4096]{2,1,0:T(8,128)(2,1)S(1)} async-done(((bf16[32,8,4096]{2,1,0:T(8,128)(2,1)}), bf16[32,8,4096]{2,1,0:T(8,128)(2,1)S(1)}, u32[]{:S(2)}, u32[]{:S(2)}) %all-to-all-start) | async-done | bytes 2097184 | tf_op jit(solution)/shard_map/all_to_all | solution.py:396
  130.1 6.2 %expert_round.1 = (bf16[32,8,2048]{2,1,0:T(8,128)(2,1)S(1)}, bf16[128,768]{1,0:T(8,128)(2,1)S(1)}) custom-call(bf16[32,8,4096]{2,1,0:T(8,128)(2,1)S(1)} %all-to-all-done.recv_ref, bf16[6144,512]{1,0:T(8,128)(2,1)} %stack.1.w_ref), custom_call_target="tpu_custom_call" | custom-call | flops 1342177280 | bytes 9437184 | tf_op jit(solution)/shard_map/expert_round/pallas_call | solution.py:201
  137.3 5.3 %all-to-all-start.1 = ((bf16[32,8,2048]{2,1,0:T(8,128)(2,1)}), bf16[32,8,2048]{2,1,0:T(8,128)(2,1)S(1)}, u32[]{:S(2)}, u32[]{:S(2)}) async-start(bf16[32,8,2048]{2,1,0:T(8,128)(2,1)} %copy-done), calls=%async_computation.1 | async-start | bytes 2097152 | tf_op jit(solution)/shard_map/all_to_all | solution.py:401
  144.2 1.4 collective-permute-start.12
  145.5 1.9 shard_map.102
  148.1 2.7 %collective-permute-start.10 = (bf16[192,1024]{1,0:T(8,128)(2,1)}, bf16[192,1024]{1,0:T(8,128)(2,1)S(1)}, u32[]{:S(2)}, u32[]{:S(2)}) collective-permute-start(bf16[192,1024]{1,0:T(8,128)(2,1)} %get-tuple-element.24), channel_id=1, source_target_pairs={{0,2},{1,3},{2,0},{3,1},{4,6},{5,7},{6,4},{7,5},{8,10},{9,11},{10,... | collective-permute-start | bytes 1179656 | tf_op jit(solution)/shard_map/ppermute | solution.py:388
  151.1 1.5 collective-permute-start.14
  152.7 1.5 collective-permute-start.11
  154.3 16.4 %collective-permute-done.13.refs_2_ = bf16[160,1024]{1,0:T(8,128)(2,1)S(1)} collective-permute-done((bf16[160,1024]{1,0:T(8,128)(2,1)S(1)}, bf16[160,1024]{1,0:T(8,128)(2,1)S(1)}, u32[]{:S(2)}, u32[]{:S(2)}) %collective-permute-start.13) | collective-permute-done | bytes 327712 | tf_op jit(solution)/shard_map/ppermute | solution.py:388
  170.8 2.3 %collective-permute-done.14.refs_3_ = bf16[160,1024]{1,0:T(8,128)(2,1)S(1)} collective-permute-done((bf16[160,1024]{1,0:T(8,128)(2,1)S(1)}, bf16[160,1024]{1,0:T(8,128)(2,1)S(1)}, u32[]{:S(2)}, u32[]{:S(2)}) %collective-permute-start.14) | collective-permute-done | bytes 327712 | tf_op jit(solution)/shard_map/ppermute | solution.py:388
  173.8 2.6 %grads_down.1 = (bf16[64,1024]{1,0:T(8,128)(2,1)}, bf16[64,1024]{1,0:T(8,128)(2,1)}, bf16[64,1024]{1,0:T(8,128)(2,1)}, bf16[64,1024]{1,0:T(8,128)(2,1)}) custom-call(s32[1]{0:T(128)} %bitcast.2.at_ref.t_ref, bf16[160,1024]{1,0:T(8,128)(2,1)} %copy-done.1, bf16[160,1024]{1,0:T(8,128)(2,1)} %copy-done.10, bf16[160,1024]{1,0:T(8,128)(2,1)} %copy-done.11, ...), custom_call_target="tpu_custom_call" | custom-call | flops 268435456 | bytes 2097152 | tf_op jit(solution)/shard_map/grads_down/pallas_call | solution.py:287
  176.4 3.2 %collective-permute-start.15 = (bf16[64,1024]{1,0:T(8,128)(2,1)}, bf16[64,1024]{1,0:T(8,128)(2,1)S(1)}, u32[]{:S(2)}, u32[]{:S(2)}) collective-permute-start(bf16[64,1024]{1,0:T(8,128)(2,1)} %get-tuple-element.33), channel_id=1, source_target_pairs={{0,1},{1,2},{2,3},{3,0},{4,5},{5,6},{6,7},{7,4},{8,9},{9,10},{10,1... | collective-permute-start | bytes 393224 | tf_op jit(solution)/shard_map/ppermute | solution.py:388
  179.6 1.4 collective-permute-start.16
  181.0 1.1 collective-permute-start.17
  183.0 3.1 %grads_up.1 = (bf16[1024,256]{1,0:T(8,128)(2,1)}, bf16[1024,256]{1,0:T(8,128)(2,1)}) custom-call(bf16[192,1024]{1,0:T(8,128)(2,1)} %copy-done.2, bf16[192,1024]{1,0:T(8,128)(2,1)} %copy-done.19, bf16[192,1024]{1,0:T(8,128)(2,1)} %copy-done.17, bf16[192,1024]{1,0:T(8,128)(2,1)} %copy-done.18), custom_call_target="tpu_custom_call" | custom-call | flops 536870912 | bytes 3145728 | tf_op jit(solution)/shard_map/grads_up/pallas_call | solution.py:301
  187.5 1.9 place.1
  189.5 8.6 %all-to-all-done.1.refs_0_ = bf16[32,8,2048]{2,1,0:T(8,128)(2,1)S(1)} async-done(((bf16[32,8,2048]{2,1,0:T(8,128)(2,1)}), bf16[32,8,2048]{2,1,0:T(8,128)(2,1)S(1)}, u32[]{:S(2)}, u32[]{:S(2)}) %all-to-all-start.1) | async-done | bytes 1048608 | tf_op jit(solution)/shard_map/all_to_all | solution.py:401
  198.0 1.8 combine.1
  (58 shorter events, 10.0 us)
Async XLA Ops:
  5.8 25.6 %copy-start.3 = (bf16[1,1024,256]{2,1,0:T(8,128)(2,1)S(1)}, bf16[1,1024,256]{2,1,0:T(8,128)(2,1)}, u32[]{:S(2)}) copy-start(bf16[1,1024,256]{2,1,0:T(8,128)(2,1)} %param.11) | copy-start | bytes 1572868
  5.8 30.8 %copy-start.4 = (bf16[1,1024,256]{2,1,0:T(8,128)(2,1)S(1)}, bf16[1,1024,256]{2,1,0:T(8,128)(2,1)}, u32[]{:S(2)}) copy-start(bf16[1,1024,256]{2,1,0:T(8,128)(2,1)} %param.12) | copy-start | bytes 1572868
  5.8 124.2 %all-to-all-start = ((bf16[32,8,4096]{2,1,0:T(8,128)(2,1)}), bf16[32,8,4096]{2,1,0:T(8,128)(2,1)S(1)}, u32[]{:S(2)}, u32[]{:S(2)}) async-start(bf16[32,8,4096]{2,1,0:T(8,128)(2,1)} %dispatch.1), calls=%async_computation | async-start | bytes 4194304 | tf_op jit(solution)/shard_map/all_to_all | solution.py:396
  31.5 14.6 %collective-permute-start = (bf16[1024,256]{1,0:T(8,128)(2,1)S(1)}, bf16[1024,256]{1,0:T(8,128)(2,1)S(1)}, u32[]{:S(2)}, u32[]{:S(2)}) collective-permute-start(bf16[1024,256]{1,0:T(8,128)(2,1)S(1)} %bitcast.10), channel_id=1, source_target_pairs={{0,1},{1,2},{2,3},{3,0},{4,5},{5,6},{6,7},{7,4},{8,9},{9,10},{10,1... | collective-permute-start | bytes 1572872 | tf_op jit(solution)/shard_map/ppermute | solution.py:388
  32.9 25.3 %collective-permute-start.1 = (bf16[1024,256]{1,0:T(8,128)(2,1)S(1)}, bf16[1024,256]{1,0:T(8,128)(2,1)S(1)}, u32[]{:S(2)}, u32[]{:S(2)}) collective-permute-start(bf16[1024,256]{1,0:T(8,128)(2,1)S(1)} %bitcast.11), channel_id=1, source_target_pairs={{0,2},{1,3},{2,0},{3,1},{4,6},{5,7},{6,4},{7,5},{8,10},{9,11},{10,... | collective-permute-start | bytes 1572872 | tf_op jit(solution)/shard_map/ppermute | solution.py:388
  35.6 22.7 %collective-permute-start.2 = (bf16[1024,256]{1,0:T(8,128)(2,1)S(1)}, bf16[1024,256]{1,0:T(8,128)(2,1)S(1)}, u32[]{:S(2)}, u32[]{:S(2)}) collective-permute-start(bf16[1024,256]{1,0:T(8,128)(2,1)S(1)} %bitcast.12), channel_id=1, source_target_pairs={{0,3},{1,0},{2,1},{3,2},{4,7},{5,4},{6,5},{7,6},{8,11},{9,8},{10,9... | collective-permute-start | bytes 1572872 | tf_op jit(solution)/shard_map/ppermute | solution.py:388
  36.7 31.8 %collective-permute-start.3 = (bf16[1024,256]{1,0:T(8,128)(2,1)S(1)}, bf16[1024,256]{1,0:T(8,128)(2,1)S(1)}, u32[]{:S(2)}, u32[]{:S(2)}) collective-permute-start(bf16[1024,256]{1,0:T(8,128)(2,1)S(1)} %bitcast.14), channel_id=1, source_target_pairs={{0,1},{1,2},{2,3},{3,0},{4,5},{5,6},{6,7},{7,4},{8,9},{9,10},{10,1... | collective-permute-start | bytes 1572872 | tf_op jit(solution)/shard_map/ppermute | solution.py:388
  37.1 43.7 %collective-permute-start.4 = (bf16[1024,256]{1,0:T(8,128)(2,1)S(1)}, bf16[1024,256]{1,0:T(8,128)(2,1)}, u32[]{:S(2)}, u32[]{:S(2)}) collective-permute-start(bf16[1024,256]{1,0:T(8,128)(2,1)S(1)} %bitcast.15), channel_id=1, source_target_pairs={{0,2},{1,3},{2,0},{3,1},{4,6},{5,7},{6,4},{7,5},{8,10},{9,11},{10,... | collective-permute-start | bytes 1572872 | tf_op jit(solution)/shard_map/ppermute | solution.py:388
  46.0 22.5 %copy-start.5 = (bf16[1024,256]{1,0:T(8,128)(2,1)}, bf16[1024,256]{1,0:T(8,128)(2,1)S(1)}, u32[]{:S(2)}) copy-start(bf16[1024,256]{1,0:T(8,128)(2,1)S(1)} %collective-permute-done.refs_1_) | copy-start | bytes 1572868
  46.0 34.8 %collective-permute-start.5 = (bf16[1024,256]{1,0:T(8,128)(2,1)S(1)}, bf16[1024,256]{1,0:T(8,128)(2,1)}, u32[]{:S(2)}, u32[]{:S(2)}) collective-permute-start(bf16[1024,256]{1,0:T(8,128)(2,1)S(1)} %bitcast.16), channel_id=1, source_target_pairs={{0,3},{1,0},{2,1},{3,2},{4,7},{5,4},{6,5},{7,6},{8,11},{9,8},{10,9... | collective-permute-start | bytes 1572872 | tf_op jit(solution)/shard_map/ppermute | solution.py:388
  58.2 11.6 %copy-start.6 = (bf16[1024,256]{1,0:T(8,128)(2,1)}, bf16[1024,256]{1,0:T(8,128)(2,1)S(1)}, u32[]{:S(2)}) copy-start(bf16[1024,256]{1,0:T(8,128)(2,1)S(1)} %collective-permute-done.1.refs_2_) | copy-start | bytes 1572868
  58.2 32.8 %collective-permute-start.6 = (bf16[64,4096]{1,0:T(8,128)(2,1)}, bf16[64,4096]{1,0:T(8,128)(2,1)}, u32[]{:S(2)}, u32[]{:S(2)}) collective-permute-start(bf16[64,4096]{1,0:T(8,128)(2,1)} %bitcast.17), channel_id=1, source_target_pairs={{0,1},{1,2},{2,3},{3,0},{4,5},{5,6},{6,7},{7,4},{8,9},{9,10},{10,1... | collective-permute-start | bytes 1572872 | tf_op jit(solution)/shard_map/ppermute | solution.py:388
  58.3 11.6 %copy-start.7 = (bf16[1024,256]{1,0:T(8,128)(2,1)}, bf16[1024,256]{1,0:T(8,128)(2,1)S(1)}, u32[]{:S(2)}) copy-start(bf16[1024,256]{1,0:T(8,128)(2,1)S(1)} %collective-permute-done.2.refs_3_) | copy-start | bytes 1572868
  58.3 44.9 %collective-permute-start.7 = (bf16[64,4096]{1,0:T(8,128)(2,1)}, bf16[64,4096]{1,0:T(8,128)(2,1)S(1)}, u32[]{:S(2)}, u32[]{:S(2)}) collective-permute-start(bf16[64,4096]{1,0:T(8,128)(2,1)} %bitcast.18), channel_id=1, source_target_pairs={{0,2},{1,3},{2,0},{3,1},{4,6},{5,7},{6,4},{7,5},{8,10},{9,11},{10,... | collective-permute-start | bytes 1572872 | tf_op jit(solution)/shard_map/ppermute | solution.py:388
  68.5 1.4 copy-start.8
  68.5 34.7 %collective-permute-start.8 = (bf16[64,4096]{1,0:T(8,128)(2,1)}, bf16[64,4096]{1,0:T(8,128)(2,1)}, u32[]{:S(2)}, u32[]{:S(2)}) collective-permute-start(bf16[64,4096]{1,0:T(8,128)(2,1)} %bitcast.19), channel_id=1, source_target_pairs={{0,3},{1,0},{2,1},{3,2},{4,7},{5,4},{6,5},{7,6},{8,11},{9,8},{10,9... | collective-permute-start | bytes 1572872 | tf_op jit(solution)/shard_map/ppermute | solution.py:388
  136.3 1.0 copy-start
  137.3 60.7 %all-to-all-start.1 = ((bf16[32,8,2048]{2,1,0:T(8,128)(2,1)}), bf16[32,8,2048]{2,1,0:T(8,128)(2,1)S(1)}, u32[]{:S(2)}, u32[]{:S(2)}) async-start(bf16[32,8,2048]{2,1,0:T(8,128)(2,1)} %copy-done), calls=%async_computation.1 | async-start | bytes 2097152 | tf_op jit(solution)/shard_map/all_to_all | solution.py:401
  144.2 37.9 %copy-start.16 = (s32[64,2]{0,1:T(2,128)S(1)}, s32[64,2]{0,1:T(2,128)}, u32[]{:S(2)}) copy-start(s32[64,2]{0,1:T(2,128)} %param.9) | copy-start | bytes 1540
  144.2 10.1 %collective-permute-start.12 = (bf16[160,1024]{1,0:T(8,128)(2,1)S(1)}, bf16[160,1024]{1,0:T(8,128)(2,1)S(1)}, u32[]{:S(2)}, u32[]{:S(2)}) collective-permute-start(bf16[160,1024]{1,0:T(8,128)(2,1)S(1)} %get-tuple-element.29), channel_id=1, source_target_pairs={{0,1},{1,2},{2,3},{3,0},{4,5},{5,6},{6,7},{7,4},{8,9},{9,10},{10,1... | collective-permute-start | bytes 983048 | tf_op jit(solution)/shard_map/ppermute | solution.py:388
  148.1 32.8 %collective-permute-start.10 = (bf16[192,1024]{1,0:T(8,128)(2,1)}, bf16[192,1024]{1,0:T(8,128)(2,1)S(1)}, u32[]{:S(2)}, u32[]{:S(2)}) collective-permute-start(bf16[192,1024]{1,0:T(8,128)(2,1)} %get-tuple-element.24), channel_id=1, source_target_pairs={{0,2},{1,3},{2,0},{3,1},{4,6},{5,7},{6,4},{7,5},{8,10},{9,11},{10,... | collective-permute-start | bytes 1179656 | tf_op jit(solution)/shard_map/ppermute | solution.py:388
  150.9 19.9 %collective-permute-start.13 = (bf16[160,1024]{1,0:T(8,128)(2,1)S(1)}, bf16[160,1024]{1,0:T(8,128)(2,1)S(1)}, u32[]{:S(2)}, u32[]{:S(2)}) collective-permute-start(bf16[160,1024]{1,0:T(8,128)(2,1)S(1)} %get-tuple-element.30), channel_id=1, source_target_pairs={{0,2},{1,3},{2,0},{3,1},{4,6},{5,7},{6,4},{7,5},{8,10},{9,11},{10,... | collective-permute-start | bytes 983048 | tf_op jit(solution)/shard_map/ppermute | solution.py:388
  151.1 22.0 %collective-permute-start.14 = (bf16[160,1024]{1,0:T(8,128)(2,1)S(1)}, bf16[160,1024]{1,0:T(8,128)(2,1)S(1)}, u32[]{:S(2)}, u32[]{:S(2)}) collective-permute-start(bf16[160,1024]{1,0:T(8,128)(2,1)S(1)} %get-tuple-element.31), channel_id=1, source_target_pairs={{0,3},{1,0},{2,1},{3,2},{4,7},{5,4},{6,5},{7,6},{8,11},{9,8},{10,9... | collective-permute-start | bytes 983048 | tf_op jit(solution)/shard_map/ppermute | solution.py:388
  152.7 29.5 %collective-permute-start.11 = (bf16[192,1024]{1,0:T(8,128)(2,1)}, bf16[192,1024]{1,0:T(8,128)(2,1)S(1)}, u32[]{:S(2)}, u32[]{:S(2)}) collective-permute-start(bf16[192,1024]{1,0:T(8,128)(2,1)} %get-tuple-element.25), channel_id=1, source_target_pairs={{0,3},{1,0},{2,1},{3,2},{4,7},{5,4},{6,5},{7,6},{8,11},{9,8},{10,9... | collective-permute-start | bytes 1179656 | tf_op jit(solution)/shard_map/ppermute | solution.py:388
  154.3 18.8 %copy-start.10 = (bf16[160,1024]{1,0:T(8,128)(2,1)}, bf16[160,1024]{1,0:T(8,128)(2,1)S(1)}, u32[]{:S(2)}) copy-start(bf16[160,1024]{1,0:T(8,128)(2,1)S(1)} %collective-permute-done.12.refs_1_) | copy-start | bytes 983044
  154.3 27.9 %collective-permute-start.9 = (bf16[192,1024]{1,0:T(8,128)(2,1)}, bf16[192,1024]{1,0:T(8,128)(2,1)S(1)}, u32[]{:S(2)}, u32[]{:S(2)}) collective-permute-start(bf16[192,1024]{1,0:T(8,128)(2,1)} %get-tuple-element.23), channel_id=1, source_target_pairs={{0,1},{1,2},{2,3},{3,0},{4,5},{5,6},{6,7},{7,4},{8,9},{9,10},{10,1... | collective-permute-start | bytes 1179656 | tf_op jit(solution)/shard_map/ppermute | solution.py:388
  170.8 2.3 %copy-start.11 = (bf16[160,1024]{1,0:T(8,128)(2,1)}, bf16[160,1024]{1,0:T(8,128)(2,1)S(1)}, u32[]{:S(2)}) copy-start(bf16[160,1024]{1,0:T(8,128)(2,1)S(1)} %collective-permute-done.13.refs_2_) | copy-start | bytes 983044
  176.4 9.7 %collective-permute-start.15 = (bf16[64,1024]{1,0:T(8,128)(2,1)}, bf16[64,1024]{1,0:T(8,128)(2,1)S(1)}, u32[]{:S(2)}, u32[]{:S(2)}) collective-permute-start(bf16[64,1024]{1,0:T(8,128)(2,1)} %get-tuple-element.33), channel_id=1, source_target_pairs={{0,1},{1,2},{2,3},{3,0},{4,5},{5,6},{6,7},{7,4},{8,9},{9,10},{10,1... | collective-permute-start | bytes 393224 | tf_op jit(solution)/shard_map/ppermute | solution.py:388
  179.6 7.2 %collective-permute-start.16 = (bf16[64,1024]{1,0:T(8,128)(2,1)}, bf16[64,1024]{1,0:T(8,128)(2,1)S(1)}, u32[]{:S(2)}, u32[]{:S(2)}) collective-permute-start(bf16[64,1024]{1,0:T(8,128)(2,1)} %get-tuple-element.34), channel_id=1, source_target_pairs={{0,2},{1,3},{2,0},{3,1},{4,6},{5,7},{6,4},{7,5},{8,10},{9,11},{10,... | collective-permute-start | bytes 393224 | tf_op jit(solution)/shard_map/ppermute | solution.py:388
  181.0 1.2 copy-start.17
  181.0 5.8 %collective-permute-start.17 = (bf16[64,1024]{1,0:T(8,128)(2,1)}, bf16[64,1024]{1,0:T(8,128)(2,1)S(1)}, u32[]{:S(2)}, u32[]{:S(2)}) collective-permute-start(bf16[64,1024]{1,0:T(8,128)(2,1)} %get-tuple-element.35), channel_id=1, source_target_pairs={{0,3},{1,0},{2,1},{3,2},{4,7},{5,4},{6,5},{7,6},{8,11},{9,8},{10,9... | collective-permute-start | bytes 393224 | tf_op jit(solution)/shard_map/ppermute | solution.py:388
  182.2 0.9 copy-start.19
  (8 other events, 5.8 us)

commit v7 on v6

--- a/solution.py
+++ b/solution.py
@@ -14,7 +14,7 @@
 SMEM = pl.BlockSpec(memory_space=pltpu.SMEM)
 HBM = pl.BlockSpec(memory_space=pltpu.HBM)
 PARTS = 4
-STEPS = 4
+STEPS = 2
 
 
 def cost(flops, bytes_accessed):
@@ -97,7 +97,7 @@
 
 
 def stack_kernel(at_ref, *refs):
-    wg, wu, wd, out = refs[:PARTS], refs[PARTS : 2 * PARTS], refs[2 * PARTS : 3 * PARTS], refs[-1]
+    wg, wu, wd, (out, whole) = refs[:PARTS], refs[PARTS : 2 * PARTS], refs[2 * PARTS : 3 * PARTS], refs[-2:]
     width, ff = wg[0].shape
     part, d = wd[0].shape
     for k in range(PARTS):
@@ -105,9 +105,11 @@
         rows = pl.ds(pl.multiple_of(owner * width, width), width)
         out[rows, 0:ff] = wg[k][...]
         out[rows, ff:] = wu[k][...]
-        for b in range(d // (2 * ff)):
-            at = pl.multiple_of(d + b * ff + owner * part, part)
-            out[pl.ds(at, part), :] = wd[k][:, b * 2 * ff : (b + 1) * 2 * ff]
+        whole[pl.ds(pl.multiple_of(owner * part, part), part), :] = wd[k][...]
+    for b in range(d // (2 * ff)):
+        for h in range(2):
+            col = (2 * b + h) * ff
+            out[d + b * ff : d + (b + 1) * ff, h * ff : (h + 1) * ff] = whole[:, col : col + ff].T
 
 
 def stack(t, wg, wu, wd):
@@ -118,6 +120,7 @@
         in_specs=[SMEM] + [VMEM] * (3 * PARTS),
         out_specs=VMEM,
         out_shape=struct(d + d // 2, 2 * ff),
+        scratch_shapes=[pltpu.VMEM((ff, d), BF)],
         cost_estimate=cost(3 * d * ff, 12 * d * ff),
         name="stack",
     )(t, *wg, *wu, *wd)
@@ -157,19 +160,22 @@
         )
         for q in range(4)
     ] + [pltpu.make_async_copy(w_ref.at[pl.ds(d, d // 2), :], wd, sem_w.at[4])]
-    for copy in weights_in:
+    for copy in weights_in[::-1]:
         copy.start()
     widen(recv_ref, flat)
+    for q in range(4):
+        unpack(flat, sources, q, [(1, c), (0, x)])
+    weights_in[4].wait()
+    grad_hidden = jnp.zeros((x.shape[0], ff), F32)
+    for b in range(d // (2 * ff)):
+        for h in range(2):
+            col = (2 * b + h) * ff
+            grad_hidden += nn(c[:, col : col + ff], wd[b * ff : (b + 1) * ff, h * ff : (h + 1) * ff])
     pre = jnp.zeros((x.shape[0], 2 * ff), F32)
-    for q in range(4):
-        unpack(flat, sources, q, [(0, x), (1, c)])
+    for q in range(4)[::-1]:
         weights_in[q].wait()
         cols = slice(q * width, (q + 1) * width)
         pre += nn(x[:, cols], wgu[cols, :])
-    weights_in[4].wait()
-    grad_hidden = jnp.zeros((x.shape[0], ff), F32)
-    for b in range(d // (2 * ff)):
-        grad_hidden += nt(c[:, b * 2 * ff : (b + 1) * 2 * ff], wd[b * ff : (b + 1) * ff, :])
     pre_gate, pre_up = pre[:, :ff], pre[:, ff:]
     sig = jax.nn.sigmoid(pre_gate)
     activated = pre_gate * sig
@@ -309,51 +315,56 @@
     )(*boxes)
 
 
-def combine_kernel(split, ids_ref, *refs):
-    rets, refs = refs[: len(split)], refs[len(split) :]
-    out_ref, flats, rhs = refs[0], refs[1 : 1 + len(split)], refs[1 + len(split)]
-    n_tok, d = out_ref.shape
-    slots = sum(split)
-    experts = rets[0].shape[0]
-    eighth = d // 8
-    blocks = eighth // 128
-    lane = lax.broadcasted_iota(jnp.int32, (n_tok, slots * experts), 1)
+def pick_kernel(experts, ids_ref, pick_ref):
+    n_tok, rows = pick_ref.shape
+    lane = lax.broadcasted_iota(jnp.int32, (n_tok, rows), 1)
     expert = lane % experts
     member = jnp.where((ids_ref[:, 0:1] == expert) | (ids_ref[:, 1:2] == expert), 1.0, 0.0).astype(F32)
     i = lax.broadcasted_iota(jnp.int32, (n_tok, n_tok), 0)
     j = lax.broadcasted_iota(jnp.int32, (n_tok, n_tok), 1)
     before = nn(jnp.where(j < i, 1.0, 0.0).astype(BF), member.astype(BF))
-    pick = jnp.where(before == (lane // experts).astype(F32), member, 0.0).astype(BF)
-    for ret, flat in zip(rets, flats):
-        for b in range(flat.shape[0]):
-            flat[b] = ret[:, :, b * 128 : (b + 1) * 128].astype(F32).reshape(flat.shape[1:])
+    pick_ref[...] = jnp.where(before == (lane // experts).astype(F32), member, 0.0).astype(BF)
+
+
+def pick(ids, experts, slots):
+    n_tok = ids.shape[0]
+    return pl.pallas_call(
+        functools.partial(pick_kernel, experts),
+        in_specs=[VMEM],
+        out_specs=VMEM,
+        out_shape=struct(n_tok, slots * experts),
+        cost_estimate=cost(2 * n_tok * n_tok * slots * experts, 4 * n_tok * slots * experts),
+        name="pick",
+    )(ids)
+
+
+def combine_kernel(pick_ref, ret_ref, out_ref, flat, rhs):
+    experts = ret_ref.shape[0]
+    eighth = out_ref.shape[1] // 8
+    blocks = eighth // 128
+    for b in range(flat.shape[0]):
+        flat[b] = ret_ref[:, :, b * 128 : (b + 1) * 128].astype(F32).reshape(flat.shape[1:])
     for o in range(8):
         for b in range(blocks):
             col = o * eighth + b * 128
-            p = 0
-            for flat, count in zip(flats, split):
-                for k in range(count):
-                    v = flat[k * blocks + b, pl.ds(o, experts, stride=8), :]
-                    rhs[p * experts : (p + 1) * experts, col : col + 128] = v.astype(BF)
-                    p += 1
-    out_ref[...] = nn(pick, rhs[...]).astype(BF)
-
-
-def combine(ids, rets, split, d):
-    n_tok = ids.shape[0]
-    slots = sum(split)
-    experts = rets[0].shape[0]
-    return pl.pallas_call(
-        functools.partial(combine_kernel, split),
-        in_specs=[VMEM] * (1 + len(split)),
+            for p in range(flat.shape[0] // blocks):
+                v = flat[p * blocks + b, pl.ds(o, experts, stride=8), :]
+                rhs[p * experts : (p + 1) * experts, col : col + 128] = v.astype(BF)
+    out_ref[...] = nn(pick_ref[...], rhs[...]).astype(BF)
+
+
+def combine(picks, ret, d):
+    n_tok, rows = picks.shape
+    return pl.pallas_call(
+        combine_kernel,
+        in_specs=[VMEM] * 2,
         out_specs=VMEM,
-        out_shape=jax.ShapeDtypeStruct((n_tok, d), BF),
-        scratch_shapes=[pltpu.VMEM((c * d // 8 // 128, r.shape[0] * 8, 128), F32) for c, r in zip(split, rets)]
-        + [pltpu.VMEM((slots * experts, d), BF)],
-        cost_estimate=cost(2 * n_tok * slots * experts * d, 4 * n_tok * d * 2),
+        out_shape=struct(n_tok, d),
+        scratch_shapes=[pltpu.VMEM((ret.shape[2] // 128, ret.shape[0] * 8, 128), F32), pltpu.VMEM((rows, d), BF)],
+        cost_estimate=cost(2 * n_tok * rows * d, 4 * n_tok * d * 2),
         compiler_params=pltpu.CompilerParams(vmem_limit_bytes=14 << 20),
         name="combine",
-    )(ids, *rets)
+    )(picks, ret)
 
 
 def place_kernel(t_ref, *refs):
@@ -398,7 +409,8 @@
     weights = stack(t, wg, wu, wd)
     (recv,), (count,) = recvs, split
     msg, h = expert_round(recv, weights, ff, count)
-    rets = [lax.all_to_all(msg, "expert", 0, 0, tiled=True)]
+    ret = lax.all_to_all(msg, "expert", 0, 0, tiled=True)
+    picks = pick(expert_ids, experts, slots)
     boxes_c = spread(t, recv, h, 1, 0, ff)
     boxes_c = boxes_c[:1] + [shift(boxes_c[k], k) for k in range(1, PARTS)]
     boxes_x = spread(t, recv, h, 0, ff, 2 * ff)
@@ -407,7 +419,7 @@
     down = list(down[:1]) + [shift(down[k], k) for k in range(1, PARTS)]
     grad_gate, grad_up = grads_up(boxes_x, h.shape[0], ff)
     grad_down = place(t, down)
-    input_grad = combine(expert_ids, rets, split, d)
+    input_grad = combine(picks, ret, d)
     return input_grad, grad_gate[None], grad_up[None], grad_down[None]
 
 

time: 200 us -> 199 us (level)
  waiting for transfers between devices: 109 us -> 106 us
    unnamed x41 -> x43, local copies, waits for them, and re-layouts: 5.66 us -> 6.3 us
  transfers between devices with their start and end apart: 20 -> 20, of which waited for: 13 -> 12; matrix products, arithmetic and copies ran while one was open for 0% -> 0% of each run, Pallas kernels for 8% -> 9%
where the time goes in v7:
time: 199 us; the launch traced here: 198 us
  waiting for transfers between devices  106 us (53%)
  starting transfers between devices  54.7 us (27%)
  Pallas kernels  30 us (15%)
  local copies, waits for them, and re-layouts  6.3 us (3%)
    ppermute x18, waiting for transfers between devices, shift(): lax.ppermute(x, 'tensor', [(s, (s + k) % PARTS) for s in range(PARTS)])  79.8 us
    all_to_all x1, starting transfers between devices, local(): recvs.append(lax.all_to_all(send, 'expert', 0, 0, tiled=True))  25.6 us
    ppermute x18, starting transfers between devices, shift(): lax.ppermute(x, 'tensor', [(s, (s + k) % PARTS) for s in range(PARTS)])  23.8 us
    all_to_all x1, waiting for transfers between devices, local(): recvs.append(lax.all_to_all(send, 'expert', 0, 0, tiled=True))  19.5 us
    all_to_all x1, waiting for transfers between devices, local(): ret = lax.all_to_all(msg, 'expert', 0, 0, tiled=True)  7.1 us
    pallas_call x1, Pallas kernels, stack(): pl.pallas_call(stack_kernel, in_specs=[SMEM] + [VMEM] * (3 * PARTS), out_...  6.52 us
    unnamed x43, local copies, waits for them, and re-layouts  6.3 us
    pallas_call x1, Pallas kernels, expert_round(): pl.pallas_call(functools.partial(expert_kernel, count), in_specs=[VMEM, H...  5.52 us
  transfers between devices with their start and end apart: 20, of which 12 were waited for; matrix products, arithmetic and copies ran while one was open for 0% of the time, Pallas kernels for 9%

profile of v7, /device:TPU:33, one launch (start us, length us, event | category | flops | bytes accessed | tf_op | source)
XLA Modules:
  0.0 198.3 jit_solution(15944968810632970490)
XLA Ops:
  0.6 4.4 %dispatch.1 = bf16[32,8,4096]{2,1,0:T(8,128)(2,1)} custom-call(s32[2,64]{1,0:T(2,128)} %bitcast.22, f32[2,64]{1,0:T(2,128)} %bitcast.23, bf16[64,4096]{1,0:T(8,128)(2,1)} %refs_6_.1, bf16[64,4096]{1,0:T(8,128)(2,1)} %refs_7_.1, bf16[64,4096]{1,0:T(8,128)(2,1)} %refs_6_.1, bf16[64,4096]{1,0:T(8,128)(2,1)} %refs_7_.1, bf16[64,4096]{1,0:T(8,128)(2,1)} %refs_6_.1, ...), custom_call_target="tpu_custom_call" | custom-call | flops 1073741824 | bytes 4194304 | tf_op jit(solution)/shard_map/dispatch/pallas_call | solution.py:87
  5.0 25.6 %all-to-all-start = ((bf16[32,8,4096]{2,1,0:T(8,128)(2,1)}), bf16[32,8,4096]{2,1,0:T(8,128)(2,1)S(1)}, u32[]{:S(2)}, u32[]{:S(2)}) async-start(bf16[32,8,4096]{2,1,0:T(8,128)(2,1)} %dispatch.1), calls=%async_computation | async-start | bytes 4194304 | tf_op jit(solution)/shard_map/all_to_all | solution.py:407
  30.6 1.5 collective-permute-start
  32.1 2.7 %collective-permute-start.1 = (bf16[1024,256]{1,0:T(8,128)(2,1)S(1)}, bf16[1024,256]{1,0:T(8,128)(2,1)S(1)}, u32[]{:S(2)}, u32[]{:S(2)}) collective-permute-start(bf16[1024,256]{1,0:T(8,128)(2,1)S(1)} %bitcast.11), channel_id=1, source_target_pairs={{0,2},{1,3},{2,0},{3,1},{4,6},{5,7},{6,4},{7,5},{8,10},{9,11},{10,... | collective-permute-start | bytes 1572872 | tf_op jit(solution)/shard_map/ppermute | solution.py:399
  37.0 8.2 %collective-permute-done.refs_1_ = bf16[1024,256]{1,0:T(8,128)(2,1)S(1)} collective-permute-done((bf16[1024,256]{1,0:T(8,128)(2,1)S(1)}, bf16[1024,256]{1,0:T(8,128)(2,1)S(1)}, u32[]{:S(2)}, u32[]{:S(2)}) %collective-permute-start) | collective-permute-done | bytes 524320 | tf_op jit(solution)/shard_map/ppermute | solution.py:399
  45.2 1.2 collective-permute-start.5
  46.4 11.0 %collective-permute-done.1.refs_2_ = bf16[1024,256]{1,0:T(8,128)(2,1)S(1)} collective-permute-done((bf16[1024,256]{1,0:T(8,128)(2,1)S(1)}, bf16[1024,256]{1,0:T(8,128)(2,1)S(1)}, u32[]{:S(2)}, u32[]{:S(2)}) %collective-permute-start.1) | collective-permute-done | bytes 524320 | tf_op jit(solution)/shard_map/ppermute | solution.py:399
  57.5 1.9 collective-permute-start.7
  59.4 8.3 %collective-permute-done.3.refs_5_ = bf16[1024,256]{1,0:T(8,128)(2,1)S(1)} collective-permute-done((bf16[1024,256]{1,0:T(8,128)(2,1)S(1)}, bf16[1024,256]{1,0:T(8,128)(2,1)S(1)}, u32[]{:S(2)}, u32[]{:S(2)}) %collective-permute-start.3) | collective-permute-done | bytes 524320 | tf_op jit(solution)/shard_map/ppermute | solution.py:399
  67.7 1.4 collective-permute-start.8
  69.1 11.0 %collective-permute-done.4.refs_6_ = bf16[1024,256]{1,0:T(8,128)(2,1)} collective-permute-done((bf16[1024,256]{1,0:T(8,128)(2,1)S(1)}, bf16[1024,256]{1,0:T(8,128)(2,1)}, u32[]{:S(2)}, u32[]{:S(2)}) %collective-permute-start.4) | collective-permute-done | bytes 524320 | tf_op jit(solution)/shard_map/ppermute | solution.py:399
  80.0 10.2 %collective-permute-done.6.refs_9_ = bf16[64,4096]{1,0:T(8,128)(2,1)} collective-permute-done((bf16[64,4096]{1,0:T(8,128)(2,1)}, bf16[64,4096]{1,0:T(8,128)(2,1)}, u32[]{:S(2)}, u32[]{:S(2)}) %collective-permute-start.6) | collective-permute-done | bytes 524320 | tf_op jit(solution)/shard_map/ppermute | solution.py:399
  90.2 12.2 %collective-permute-done.7.refs_10_ = bf16[64,4096]{1,0:T(8,128)(2,1)S(1)} collective-permute-done((bf16[64,4096]{1,0:T(8,128)(2,1)}, bf16[64,4096]{1,0:T(8,128)(2,1)S(1)}, u32[]{:S(2)}, u32[]{:S(2)}) %collective-permute-start.7) | collective-permute-done | bytes 524320 | tf_op jit(solution)/shard_map/ppermute | solution.py:399
  103.2 6.5 %stack.1.w_ref = bf16[6144,512]{1,0:T(8,128)(2,1)} custom-call(s32[1]{0:T(128)} %bitcast.2.at_ref.t_ref, bf16[1024,256]{1,0:T(8,128)(2,1)} %bitcast.9, bf16[1024,256]{1,0:T(8,128)(2,1)} %copy-done.6, bf16[1024,256]{1,0:T(8,128)(2,1)} %copy-done.7, bf16[1024,256]{1,0:T(8,128)(2,1)} %copy-done.8, bf16[1024,256]{1,0:T(8,128)(2,1)} %bitcast.13, ...), custom_call_target="tpu_custom_call" | custom-call | flops 3145728 | bytes 12582912 | tf_op jit(solution)/shard_map/stack/pallas_call | solution.py:118
  109.7 19.5 %all-to-all-done.recv_ref = bf16[32,8,4096]{2,1,0:T(8,128)(2,1)S(1)} async-done(((bf16[32,8,4096]{2,1,0:T(8,128)(2,1)}), bf16[32,8,4096]{2,1,0:T(8,128)(2,1)S(1)}, u32[]{:S(2)}, u32[]{:S(2)}) %all-to-all-start) | async-done | bytes 2097184 | tf_op jit(solution)/shard_map/all_to_all | solution.py:407
  129.2 5.5 %expert_round.1 = (bf16[32,8,2048]{2,1,0:T(8,128)(2,1)S(1)}, bf16[128,768]{1,0:T(8,128)(2,1)S(1)}) custom-call(bf16[32,8,4096]{2,1,0:T(8,128)(2,1)S(1)} %all-to-all-done.recv_ref, bf16[6144,512]{1,0:T(8,128)(2,1)} %stack.1.w_ref), custom_call_target="tpu_custom_call" | custom-call | flops 1342177280 | bytes 9437184 | tf_op jit(solution)/shard_map/expert_round/pallas_call | solution.py:207
  135.8 5.3 %all-to-all-start.1 = ((bf16[32,8,2048]{2,1,0:T(8,128)(2,1)}), bf16[32,8,2048]{2,1,0:T(8,128)(2,1)S(1)}, u32[]{:S(2)}, u32[]{:S(2)}) async-start(bf16[32,8,2048]{2,1,0:T(8,128)(2,1)} %copy-done), calls=%async_computation.1 | async-start | bytes 2097152 | tf_op jit(solution)/shard_map/all_to_all | solution.py:412
  142.7 1.3 collective-permute-start.12
  144.0 1.9 shard_map.102
  146.6 2.7 %collective-permute-start.10 = (bf16[192,1024]{1,0:T(8,128)(2,1)}, bf16[192,1024]{1,0:T(8,128)(2,1)S(1)}, u32[]{:S(2)}, u32[]{:S(2)}) collective-permute-start(bf16[192,1024]{1,0:T(8,128)(2,1)} %get-tuple-element.24), channel_id=1, source_target_pairs={{0,2},{1,3},{2,0},{3,1},{4,6},{5,7},{6,4},{7,5},{8,10},{9,11},{10,... | collective-permute-start | bytes 1179656 | tf_op jit(solution)/shard_map/ppermute | solution.py:399
  149.6 1.5 collective-permute-start.14
  151.2 1.5 collective-permute-start.11
  152.8 16.5 %collective-permute-done.13.refs_2_ = bf16[160,1024]{1,0:T(8,128)(2,1)S(1)} collective-permute-done((bf16[160,1024]{1,0:T(8,128)(2,1)S(1)}, bf16[160,1024]{1,0:T(8,128)(2,1)S(1)}, u32[]{:S(2)}, u32[]{:S(2)}) %collective-permute-start.13) | collective-permute-done | bytes 327712 | tf_op jit(solution)/shard_map/ppermute | solution.py:399
  169.3 2.3 %collective-permute-done.14.refs_3_ = bf16[160,1024]{1,0:T(8,128)(2,1)S(1)} collective-permute-done((bf16[160,1024]{1,0:T(8,128)(2,1)S(1)}, bf16[160,1024]{1,0:T(8,128)(2,1)S(1)}, u32[]{:S(2)}, u32[]{:S(2)}) %collective-permute-start.14) | collective-permute-done | bytes 327712 | tf_op jit(solution)/shard_map/ppermute | solution.py:399
  172.3 2.6 %grads_down.1 = (bf16[64,1024]{1,0:T(8,128)(2,1)}, bf16[64,1024]{1,0:T(8,128)(2,1)}, bf16[64,1024]{1,0:T(8,128)(2,1)}, bf16[64,1024]{1,0:T(8,128)(2,1)}) custom-call(s32[1]{0:T(128)} %bitcast.2.at_ref.t_ref, bf16[160,1024]{1,0:T(8,128)(2,1)} %copy-done.1, bf16[160,1024]{1,0:T(8,128)(2,1)} %copy-done.11, bf16[160,1024]{1,0:T(8,128)(2,1)} %copy-done.12, ...), custom_call_target="tpu_custom_call" | custom-call | flops 268435456 | bytes 2097152 | tf_op jit(solution)/shard_map/grads_down/pallas_call | solution.py:293
  174.9 3.2 %collective-permute-start.15 = (bf16[64,1024]{1,0:T(8,128)(2,1)}, bf16[64,1024]{1,0:T(8,128)(2,1)S(1)}, u32[]{:S(2)}, u32[]{:S(2)}) collective-permute-start(bf16[64,1024]{1,0:T(8,128)(2,1)} %get-tuple-element.33), channel_id=1, source_target_pairs={{0,1},{1,2},{2,3},{3,0},{4,5},{5,6},{6,7},{7,4},{8,9},{9,10},{10,1... | collective-permute-start | bytes 393224 | tf_op jit(solution)/shard_map/ppermute | solution.py:399
  178.1 1.4 collective-permute-start.16
  181.2 1.6 pick.1.pick_ref
  183.7 3.1 %grads_up.1 = (bf16[1024,256]{1,0:T(8,128)(2,1)}, bf16[1024,256]{1,0:T(8,128)(2,1)}) custom-call(bf16[192,1024]{1,0:T(8,128)(2,1)} %copy-done.3, bf16[192,1024]{1,0:T(8,128)(2,1)} %copy-done.20, bf16[192,1024]{1,0:T(8,128)(2,1)} %copy-done.18, bf16[192,1024]{1,0:T(8,128)(2,1)} %copy-done.19), custom_call_target="tpu_custom_call" | custom-call | flops 536870912 | bytes 3145728 | tf_op jit(solution)/shard_map/grads_up/pallas_call | solution.py:307
  187.5 1.9 place.1
  189.4 7.1 %all-to-all-done.1.ret_ref = bf16[32,8,2048]{2,1,0:T(8,128)(2,1)S(1)} async-done(((bf16[32,8,2048]{2,1,0:T(8,128)(2,1)}), bf16[32,8,2048]{2,1,0:T(8,128)(2,1)S(1)}, u32[]{:S(2)}, u32[]{:S(2)}) %all-to-all-start.1) | async-done | bytes 1048608 | tf_op jit(solution)/shard_map/all_to_all | solution.py:412
  196.5 1.7 combine.1
  (61 shorter events, 10.9 us)
Async XLA Ops:
  5.0 25.6 %copy-start.4 = (bf16[1,1024,256]{2,1,0:T(8,128)(2,1)S(1)}, bf16[1,1024,256]{2,1,0:T(8,128)(2,1)}, u32[]{:S(2)}) copy-start(bf16[1,1024,256]{2,1,0:T(8,128)(2,1)} %param.11) | copy-start | bytes 1572868
  5.0 30.8 %copy-start.5 = (bf16[1,1024,256]{2,1,0:T(8,128)(2,1)S(1)}, bf16[1,1024,256]{2,1,0:T(8,128)(2,1)}, u32[]{:S(2)}) copy-start(bf16[1,1024,256]{2,1,0:T(8,128)(2,1)} %param.12) | copy-start | bytes 1572868
  5.0 124.2 %all-to-all-start = ((bf16[32,8,4096]{2,1,0:T(8,128)(2,1)}), bf16[32,8,4096]{2,1,0:T(8,128)(2,1)S(1)}, u32[]{:S(2)}, u32[]{:S(2)}) async-start(bf16[32,8,4096]{2,1,0:T(8,128)(2,1)} %dispatch.1), calls=%async_computation | async-start | bytes 4194304 | tf_op jit(solution)/shard_map/all_to_all | solution.py:407
  30.6 14.6 %collective-permute-start = (bf16[1024,256]{1,0:T(8,128)(2,1)S(1)}, bf16[1024,256]{1,0:T(8,128)(2,1)S(1)}, u32[]{:S(2)}, u32[]{:S(2)}) collective-permute-start(bf16[1024,256]{1,0:T(8,128)(2,1)S(1)} %bitcast.10), channel_id=1, source_target_pairs={{0,1},{1,2},{2,3},{3,0},{4,5},{5,6},{6,7},{7,4},{8,9},{9,10},{10,1... | collective-permute-start | bytes 1572872 | tf_op jit(solution)/shard_map/ppermute | solution.py:399
  32.1 25.3 %collective-permute-start.1 = (bf16[1024,256]{1,0:T(8,128)(2,1)S(1)}, bf16[1024,256]{1,0:T(8,128)(2,1)S(1)}, u32[]{:S(2)}, u32[]{:S(2)}) collective-permute-start(bf16[1024,256]{1,0:T(8,128)(2,1)S(1)} %bitcast.11), channel_id=1, source_target_pairs={{0,2},{1,3},{2,0},{3,1},{4,6},{5,7},{6,4},{7,5},{8,10},{9,11},{10,... | collective-permute-start | bytes 1572872 | tf_op jit(solution)/shard_map/ppermute | solution.py:399
  34.8 22.7 %collective-permute-start.2 = (bf16[1024,256]{1,0:T(8,128)(2,1)S(1)}, bf16[1024,256]{1,0:T(8,128)(2,1)S(1)}, u32[]{:S(2)}, u32[]{:S(2)}) collective-permute-start(bf16[1024,256]{1,0:T(8,128)(2,1)S(1)} %bitcast.12), channel_id=1, source_target_pairs={{0,3},{1,0},{2,1},{3,2},{4,7},{5,4},{6,5},{7,6},{8,11},{9,8},{10,9... | collective-permute-start | bytes 1572872 | tf_op jit(solution)/shard_map/ppermute | solution.py:399
  35.8 31.8 %collective-permute-start.3 = (bf16[1024,256]{1,0:T(8,128)(2,1)S(1)}, bf16[1024,256]{1,0:T(8,128)(2,1)S(1)}, u32[]{:S(2)}, u32[]{:S(2)}) collective-permute-start(bf16[1024,256]{1,0:T(8,128)(2,1)S(1)} %bitcast.14), channel_id=1, source_target_pairs={{0,1},{1,2},{2,3},{3,0},{4,5},{5,6},{6,7},{7,4},{8,9},{9,10},{10,1... | collective-permute-start | bytes 1572872 | tf_op jit(solution)/shard_map/ppermute | solution.py:399
  36.3 43.7 %collective-permute-start.4 = (bf16[1024,256]{1,0:T(8,128)(2,1)S(1)}, bf16[1024,256]{1,0:T(8,128)(2,1)}, u32[]{:S(2)}, u32[]{:S(2)}) collective-permute-start(bf16[1024,256]{1,0:T(8,128)(2,1)S(1)} %bitcast.15), channel_id=1, source_target_pairs={{0,2},{1,3},{2,0},{3,1},{4,6},{5,7},{6,4},{7,5},{8,10},{9,11},{10,... | collective-permute-start | bytes 1572872 | tf_op jit(solution)/shard_map/ppermute | solution.py:399
  45.2 22.5 %copy-start.6 = (bf16[1024,256]{1,0:T(8,128)(2,1)}, bf16[1024,256]{1,0:T(8,128)(2,1)S(1)}, u32[]{:S(2)}) copy-start(bf16[1024,256]{1,0:T(8,128)(2,1)S(1)} %collective-permute-done.refs_1_) | copy-start | bytes 1572868
  45.2 34.8 %collective-permute-start.5 = (bf16[1024,256]{1,0:T(8,128)(2,1)S(1)}, bf16[1024,256]{1,0:T(8,128)(2,1)}, u32[]{:S(2)}, u32[]{:S(2)}) collective-permute-start(bf16[1024,256]{1,0:T(8,128)(2,1)S(1)} %bitcast.16), channel_id=1, source_target_pairs={{0,3},{1,0},{2,1},{3,2},{4,7},{5,4},{6,5},{7,6},{8,11},{9,8},{10,9... | collective-permute-start | bytes 1572872 | tf_op jit(solution)/shard_map/ppermute | solution.py:399
  57.4 11.6 %copy-start.7 = (bf16[1024,256]{1,0:T(8,128)(2,1)}, bf16[1024,256]{1,0:T(8,128)(2,1)S(1)}, u32[]{:S(2)}) copy-start(bf16[1024,256]{1,0:T(8,128)(2,1)S(1)} %collective-permute-done.1.refs_2_) | copy-start | bytes 1572868
  57.4 32.8 %collective-permute-start.6 = (bf16[64,4096]{1,0:T(8,128)(2,1)}, bf16[64,4096]{1,0:T(8,128)(2,1)}, u32[]{:S(2)}, u32[]{:S(2)}) collective-permute-start(bf16[64,4096]{1,0:T(8,128)(2,1)} %bitcast.17), channel_id=1, source_target_pairs={{0,1},{1,2},{2,3},{3,0},{4,5},{5,6},{6,7},{7,4},{8,9},{9,10},{10,1... | collective-permute-start | bytes 1572872 | tf_op jit(solution)/shard_map/ppermute | solution.py:399
  57.5 11.6 %copy-start.8 = (bf16[1024,256]{1,0:T(8,128)(2,1)}, bf16[1024,256]{1,0:T(8,128)(2,1)S(1)}, u32[]{:S(2)}) copy-start(bf16[1024,256]{1,0:T(8,128)(2,1)S(1)} %collective-permute-done.2.refs_3_) | copy-start | bytes 1572868
  57.5 44.9 %collective-permute-start.7 = (bf16[64,4096]{1,0:T(8,128)(2,1)}, bf16[64,4096]{1,0:T(8,128)(2,1)S(1)}, u32[]{:S(2)}, u32[]{:S(2)}) collective-permute-start(bf16[64,4096]{1,0:T(8,128)(2,1)} %bitcast.18), channel_id=1, source_target_pairs={{0,2},{1,3},{2,0},{3,1},{4,6},{5,7},{6,4},{7,5},{8,10},{9,11},{10,... | collective-permute-start | bytes 1572872 | tf_op jit(solution)/shard_map/ppermute | solution.py:399
  67.7 1.4 copy-start.9
  67.7 34.7 %collective-permute-start.8 = (bf16[64,4096]{1,0:T(8,128)(2,1)}, bf16[64,4096]{1,0:T(8,128)(2,1)}, u32[]{:S(2)}, u32[]{:S(2)}) collective-permute-start(bf16[64,4096]{1,0:T(8,128)(2,1)} %bitcast.19), channel_id=1, source_target_pairs={{0,3},{1,0},{2,1},{3,2},{4,7},{5,4},{6,5},{7,6},{8,11},{9,8},{10,9... | collective-permute-start | bytes 1572872 | tf_op jit(solution)/shard_map/ppermute | solution.py:399
  134.8 1.0 copy-start
  135.8 60.7 %all-to-all-start.1 = ((bf16[32,8,2048]{2,1,0:T(8,128)(2,1)}), bf16[32,8,2048]{2,1,0:T(8,128)(2,1)S(1)}, u32[]{:S(2)}, u32[]{:S(2)}) async-start(bf16[32,8,2048]{2,1,0:T(8,128)(2,1)} %copy-done), calls=%async_computation.1 | async-start | bytes 2097152 | tf_op jit(solution)/shard_map/all_to_all | solution.py:412
  142.7 37.8 %copy-start.17 = (s32[64,2]{0,1:T(2,128)S(1)}, s32[64,2]{0,1:T(2,128)}, u32[]{:S(2)}) copy-start(s32[64,2]{0,1:T(2,128)} %param.9) | copy-start | bytes 1540
  142.7 10.1 %collective-permute-start.12 = (bf16[160,1024]{1,0:T(8,128)(2,1)S(1)}, bf16[160,1024]{1,0:T(8,128)(2,1)S(1)}, u32[]{:S(2)}, u32[]{:S(2)}) collective-permute-start(bf16[160,1024]{1,0:T(8,128)(2,1)S(1)} %get-tuple-element.29), channel_id=1, source_target_pairs={{0,1},{1,2},{2,3},{3,0},{4,5},{5,6},{6,7},{7,4},{8,9},{9,10},{10,1... | collective-permute-start | bytes 983048 | tf_op jit(solution)/shard_map/ppermute | solution.py:399
  146.6 32.8 %collective-permute-start.10 = (bf16[192,1024]{1,0:T(8,128)(2,1)}, bf16[192,1024]{1,0:T(8,128)(2,1)S(1)}, u32[]{:S(2)}, u32[]{:S(2)}) collective-permute-start(bf16[192,1024]{1,0:T(8,128)(2,1)} %get-tuple-element.24), channel_id=1, source_target_pairs={{0,2},{1,3},{2,0},{3,1},{4,6},{5,7},{6,4},{7,5},{8,10},{9,11},{10,... | collective-permute-start | bytes 1179656 | tf_op jit(solution)/shard_map/ppermute | solution.py:399
  149.4 19.9 %collective-permute-start.13 = (bf16[160,1024]{1,0:T(8,128)(2,1)S(1)}, bf16[160,1024]{1,0:T(8,128)(2,1)S(1)}, u32[]{:S(2)}, u32[]{:S(2)}) collective-permute-start(bf16[160,1024]{1,0:T(8,128)(2,1)S(1)} %get-tuple-element.30), channel_id=1, source_target_pairs={{0,2},{1,3},{2,0},{3,1},{4,6},{5,7},{6,4},{7,5},{8,10},{9,11},{10,... | collective-permute-start | bytes 983048 | tf_op jit(solution)/shard_map/ppermute | solution.py:399
  149.6 22.0 %collective-permute-start.14 = (bf16[160,1024]{1,0:T(8,128)(2,1)S(1)}, bf16[160,1024]{1,0:T(8,128)(2,1)S(1)}, u32[]{:S(2)}, u32[]{:S(2)}) collective-permute-start(bf16[160,1024]{1,0:T(8,128)(2,1)S(1)} %get-tuple-element.31), channel_id=1, source_target_pairs={{0,3},{1,0},{2,1},{3,2},{4,7},{5,4},{6,5},{7,6},{8,11},{9,8},{10,9... | collective-permute-start | bytes 983048 | tf_op jit(solution)/shard_map/ppermute | solution.py:399
  151.2 31.6 %collective-permute-start.11 = (bf16[192,1024]{1,0:T(8,128)(2,1)}, bf16[192,1024]{1,0:T(8,128)(2,1)S(1)}, u32[]{:S(2)}, u32[]{:S(2)}) collective-permute-start(bf16[192,1024]{1,0:T(8,128)(2,1)} %get-tuple-element.25), channel_id=1, source_target_pairs={{0,3},{1,0},{2,1},{3,2},{4,7},{5,4},{6,5},{7,6},{8,11},{9,8},{10,9... | collective-permute-start | bytes 1179656 | tf_op jit(solution)/shard_map/ppermute | solution.py:399
  152.8 18.8 %copy-start.11 = (bf16[160,1024]{1,0:T(8,128)(2,1)}, bf16[160,1024]{1,0:T(8,128)(2,1)S(1)}, u32[]{:S(2)}) copy-start(bf16[160,1024]{1,0:T(8,128)(2,1)S(1)} %collective-permute-done.12.refs_1_) | copy-start | bytes 983044
  152.8 30.0 %collective-permute-start.9 = (bf16[192,1024]{1,0:T(8,128)(2,1)}, bf16[192,1024]{1,0:T(8,128)(2,1)S(1)}, u32[]{:S(2)}, u32[]{:S(2)}) collective-permute-start(bf16[192,1024]{1,0:T(8,128)(2,1)} %get-tuple-element.23), channel_id=1, source_target_pairs={{0,1},{1,2},{2,3},{3,0},{4,5},{5,6},{6,7},{7,4},{8,9},{9,10},{10,1... | collective-permute-start | bytes 1179656 | tf_op jit(solution)/shard_map/ppermute | solution.py:399
  169.3 2.3 %copy-start.12 = (bf16[160,1024]{1,0:T(8,128)(2,1)}, bf16[160,1024]{1,0:T(8,128)(2,1)S(1)}, u32[]{:S(2)}) copy-start(bf16[160,1024]{1,0:T(8,128)(2,1)S(1)} %collective-permute-done.13.refs_2_) | copy-start | bytes 983044
  174.9 11.9 %collective-permute-start.15 = (bf16[64,1024]{1,0:T(8,128)(2,1)}, bf16[64,1024]{1,0:T(8,128)(2,1)S(1)}, u32[]{:S(2)}, u32[]{:S(2)}) collective-permute-start(bf16[64,1024]{1,0:T(8,128)(2,1)} %get-tuple-element.33), channel_id=1, source_target_pairs={{0,1},{1,2},{2,3},{3,0},{4,5},{5,6},{6,7},{7,4},{8,9},{9,10},{10,1... | collective-permute-start | bytes 393224 | tf_op jit(solution)/shard_map/ppermute | solution.py:399
  178.1 8.7 %collective-permute-start.16 = (bf16[64,1024]{1,0:T(8,128)(2,1)}, bf16[64,1024]{1,0:T(8,128)(2,1)S(1)}, u32[]{:S(2)}, u32[]{:S(2)}) collective-permute-start(bf16[64,1024]{1,0:T(8,128)(2,1)} %get-tuple-element.34), channel_id=1, source_target_pairs={{0,2},{1,3},{2,0},{3,1},{4,6},{5,7},{6,4},{7,5},{8,10},{9,11},{10,... | collective-permute-start | bytes 393224 | tf_op jit(solution)/shard_map/ppermute | solution.py:399
  179.5 3.3 %copy-start.18 = (bf16[192,1024]{1,0:T(8,128)(2,1)}, bf16[192,1024]{1,0:T(8,128)(2,1)S(1)}, u32[]{:S(2)}) copy-start(bf16[192,1024]{1,0:T(8,128)(2,1)S(1)} %collective-permute-done.10.refs_2_) | copy-start | bytes 1179652
  179.5 7.3 %collective-permute-start.17 = (bf16[64,1024]{1,0:T(8,128)(2,1)}, bf16[64,1024]{1,0:T(8,128)(2,1)S(1)}, u32[]{:S(2)}, u32[]{:S(2)}) collective-permute-start(bf16[64,1024]{1,0:T(8,128)(2,1)} %get-tuple-element.35), channel_id=1, source_target_pairs={{0,3},{1,0},{2,1},{3,2},{4,7},{5,4},{6,5},{7,6},{8,11},{9,8},{10,9... | collective-permute-start | bytes 393224 | tf_op jit(solution)/shard_map/ppermute | solution.py:399
  182.8 13.7 %copy-start.2 = (bf16[64,128]{1,0:T(8,128)(2,1)S(1)}, bf16[64,128]{1,0:T(8,128)(2,1)}, u32[]{:S(2)}) copy-start(bf16[64,128]{1,0:T(8,128)(2,1)} %pick.1.pick_ref) | copy-start | bytes 49156
  (9 other events, 6.6 us)

commit v8 on v7

--- a/solution.py
+++ b/solution.py
@@ -39,7 +39,7 @@
 
 def dispatch_kernel(split, ids_ref, gate_ref, *refs):
     sources, refs = refs[:8], refs[8:]
-    outs, (pick_ref, scale_ref) = refs[: len(split)], refs[len(split) :]
+    outs, (pick_ref, scale_ref) = refs[: len(split)], refs[len(split) + 1 :]
     n_tok, lanes = sources[0].shape
     experts = outs[0].shape[0]
     rows = experts * 8
@@ -88,8 +88,8 @@
         functools.partial(dispatch_kernel, split),
         grid=(STEPS,),
         in_specs=[pl.BlockSpec((2, n_tok), lambda i: (0, 0))] * 2 + columns,
-        out_specs=[pl.BlockSpec((experts, 8, c * lanes), lambda i: (0, 0, i)) for c in split],
-        out_shape=[jax.ShapeDtypeStruct((experts, 8, c * d // 4), BF) for c in split],
+        out_specs=[pl.BlockSpec((experts, 8, c * lanes), lambda i: (0, 0, i)) for c in split] + [HBM],
+        out_shape=[struct(experts, 8, c * d // 4) for c in split] + [struct(experts, 8, slots * d // 8)],
         scratch_shapes=[pltpu.VMEM((slots, rows, 8 * n_tok), BF), pltpu.VMEM((slots, rows, 1), F32)],
         cost_estimate=cost(2 * slots * rows * 8 * n_tok * d // 4, 4 * n_tok * d * 2 + 2 * slots * experts * d * 2),
         name="dispatch",
@@ -149,7 +149,7 @@
     return pltpu.VMEM((recv.shape[2] // 128, recv.shape[0] * 8, 128), F32)
 
 
-def expert_kernel(count, recv_ref, w_ref, msg_ref, h_ref, flat, x, c, back, ret, wgu, wd, sem_w):
+def expert_kernel(count, recv_ref, w_ref, spare_ref, msg_ref, h_ref, flat, x, c, ret, msg, wgu, wd, sem_w, sem_out):
     sources = recv_ref.shape[0]
     d = x.shape[1]
     width = d // 4
@@ -183,46 +183,57 @@
     grad_up_pre = (grad_hidden * activated).astype(BF)
     hidden = (activated * pre_up).astype(BF)
     both = jnp.concatenate([grad_gate_pre, grad_up_pre], axis=1)
-    for q in range(4):
-        cols = slice(q * width, (q + 1) * width)
-        back[:, cols] = nt(both, wgu[cols, :])
     eighth = d // 8
     blocks = eighth // 128
+    for q in range(4):
+        rows = nt(both, wgu[q * width : (q + 1) * width, :])
+        for p in range(count):
+            for b in range(blocks):
+                for o in range(2):
+                    col = o * eighth + b * 128
+                    ret[p * blocks + b, pl.ds(2 * q + o, sources, stride=8), :] = rows[
+                        p * sources : (p + 1) * sources, col : col + 128
+                    ]
+    out = [
+        pltpu.make_async_copy(msg.at[p], msg_ref.at[:, :, pl.ds(p * eighth, eighth)], sem_out.at[p]) for p in range(count)
+    ]
     for p in range(count):
         for b in range(blocks):
-            for o in range(8):
-                col = o * eighth + b * 128
-                ret[p * blocks + b, pl.ds(o, sources, stride=8), :] = back[p * sources : (p + 1) * sources, col : col + 128]
-        for b in range(blocks):
-            at = p * eighth + b * 128
-            msg_ref[:, :, at : at + 128] = ret[p * blocks + b].reshape(sources, 8, 128).astype(BF)
+            msg[p, :, :, b * 128 : (b + 1) * 128] = ret[p * blocks + b].reshape(sources, 8, 128).astype(BF)
+        if p:
+            out[p - 1].start()
     h_ref[:, 0:ff] = hidden
     h_ref[:, ff:] = both
-
-
-def expert_round(recv, weights, ff, count):
+    out[-1].start()
+    for copy in out:
+        copy.wait()
+
+
+def expert_round(recv, weights, spare, ff, count):
     sources = recv.shape[0]
     d = recv.shape[2] * 4 // count
     rows = sources * count
     return pl.pallas_call(
         functools.partial(expert_kernel, count),
-        in_specs=[VMEM, HBM],
-        out_specs=[VMEM] * 2,
+        in_specs=[VMEM, HBM, HBM],
+        out_specs=[HBM, VMEM],
+        input_output_aliases={2: 0},
         out_shape=[struct(sources, 8, count * d // 8), struct(rows, 3 * ff)],
         scratch_shapes=[
             flat_scratch(recv),
             pltpu.VMEM((rows, d), BF),
             pltpu.VMEM((rows, d), BF),
-            pltpu.VMEM((rows, d), F32),
             pltpu.VMEM((count * d // 8 // 128, sources * 8, 128), F32),
+            pltpu.VMEM((count, sources, 8, d // 8), BF),
             pltpu.VMEM((d, 2 * ff), BF),
             pltpu.VMEM((d // 2, 2 * ff), BF),
             pltpu.SemaphoreType.DMA((5,)),
+            pltpu.SemaphoreType.DMA((count,)),
         ],
         cost_estimate=cost(2 * rows * d * 5 * ff, 3 * ff * d * 2 + 3 * rows * d * 2),
         compiler_params=pltpu.CompilerParams(vmem_limit_bytes=50 << 20),
         name="expert_round",
-    )(recv, weights)
+    )(recv, weights, spare)
 
 
 def spread_kernel(kind, first, wide, t_ref, recv_ref, h_ref, *refs):
@@ -401,14 +412,14 @@
     def everyone(x):
         return [x] + [shift(x, k) for k in range(1, PARTS)]
 
-    sends = dispatch(expert_ids.T, gate_wts.T, tokens, cotangent, experts, split)
+    *sends, spare = dispatch(expert_ids.T, gate_wts.T, tokens, cotangent, experts, split)
     recvs = []
     for send in sends:
         recvs.append(lax.all_to_all(send, "expert", 0, 0, tiled=True))
     wg, wu, wd = everyone(w_gate[0]), everyone(w_up[0]), everyone(w_down[0])
     weights = stack(t, wg, wu, wd)
     (recv,), (count,) = recvs, split
-    msg, h = expert_round(recv, weights, ff, count)
+    msg, h = expert_round(recv, weights, spare, ff, count)
     ret = lax.all_to_all(msg, "expert", 0, 0, tiled=True)
     picks = pick(expert_ids, experts, slots)
     boxes_c = spread(t, recv, h, 1, 0, ff)

time: 199 us -> 199 us (level)
    unnamed x43 -> x41, local copies, waits for them, and re-layouts: 6.3 us -> 4.58 us
where the time goes in v8:
time: 199 us; the launch traced here: 198 us
  waiting for transfers between devices  107 us (54%)
  starting transfers between devices  54.8 us (28%)
  Pallas kernels  31 us (16%)
  local copies, waits for them, and re-layouts  4.58 us (2%)
    ppermute x18, waiting for transfers between devices, shift(): lax.ppermute(x, 'tensor', [(s, (s + k) % PARTS) for s in range(PARTS)])  79.9 us
    all_to_all x1, starting transfers between devices, local(): recvs.append(lax.all_to_all(send, 'expert', 0, 0, tiled=True))  25.6 us
    ppermute x18, starting transfers between devices, shift(): lax.ppermute(x, 'tensor', [(s, (s + k) % PARTS) for s in range(PARTS)])  23.9 us
    all_to_all x1, waiting for transfers between devices, local(): recvs.append(lax.all_to_all(send, 'expert', 0, 0, tiled=True))  19.5 us
    all_to_all x1, waiting for transfers between devices, local(): ret = lax.all_to_all(msg, 'expert', 0, 0, tiled=True)  7.68 us
    pallas_call x1, Pallas kernels, stack(): pl.pallas_call(stack_kernel, in_specs=[SMEM] + [VMEM] * (3 * PARTS), out_...  6.52 us
    pallas_call x1, Pallas kernels, expert_round(): pl.pallas_call(functools.partial(expert_kernel, count), in_specs=[VMEM, H...  6.47 us
    all_to_all x1, starting transfers between devices, local(): ret = lax.all_to_all(msg, 'expert', 0, 0, tiled=True)  5.27 us
  transfers between devices with their start and end apart: 20, of which 12 were waited for; matrix products, arithmetic and copies ran while one was open for 0% of the time, Pallas kernels for 9%

profile of v8, /device:TPU:33, one launch (start us, length us, event | category | flops | bytes accessed | tf_op | source)
XLA Modules:
  0.0 198.2 jit_solution(14476909181537651666)
XLA Ops:
  0.6 4.4 %dispatch.1 = (bf16[32,8,4096]{2,1,0:T(8,128)(2,1)}, bf16[32,8,2048]{2,1,0:T(8,128)(2,1)}) custom-call(s32[2,64]{1,0:T(2,128)} %bitcast.22, f32[2,64]{1,0:T(2,128)} %bitcast.23, bf16[64,4096]{1,0:T(8,128)(2,1)} %refs_6_.1, bf16[64,4096]{1,0:T(8,128)(2,1)} %refs_7_.1, bf16[64,4096]{1,0:T(8,128)(2,1)} %refs_6_.1, bf16[64,4096]{1,0:T(8,128)(2,1)} %refs_7_.1, ...), custom_call_target="tpu_custom_call" | custom-call | flops 1073741824 | bytes 4194304 | tf_op jit(solution)/shard_map/dispatch/pallas_call | solution.py:87
  5.0 25.6 %all-to-all-start = ((bf16[32,8,4096]{2,1,0:T(8,128)(2,1)}), bf16[32,8,4096]{2,1,0:T(8,128)(2,1)S(1)}, u32[]{:S(2)}, u32[]{:S(2)}) async-start(bf16[32,8,4096]{2,1,0:T(8,128)(2,1)} %get-tuple-element.22), calls=%async_computation | async-start | bytes 4194304 | tf_op jit(solution)/shard_map/all_to_all | solution.py:418
  30.6 1.5 collective-permute-start
  32.1 2.7 %collective-permute-start.1 = (bf16[1024,256]{1,0:T(8,128)(2,1)S(1)}, bf16[1024,256]{1,0:T(8,128)(2,1)S(1)}, u32[]{:S(2)}, u32[]{:S(2)}) collective-permute-start(bf16[1024,256]{1,0:T(8,128)(2,1)S(1)} %bitcast.11), channel_id=1, source_target_pairs={{0,2},{1,3},{2,0},{3,1},{4,6},{5,7},{6,4},{7,5},{8,10},{9,11},{10,... | collective-permute-start | bytes 1572872 | tf_op jit(solution)/shard_map/ppermute | solution.py:410
  37.0 8.2 %collective-permute-done.refs_1_ = bf16[1024,256]{1,0:T(8,128)(2,1)S(1)} collective-permute-done((bf16[1024,256]{1,0:T(8,128)(2,1)S(1)}, bf16[1024,256]{1,0:T(8,128)(2,1)S(1)}, u32[]{:S(2)}, u32[]{:S(2)}) %collective-permute-start) | collective-permute-done | bytes 524320 | tf_op jit(solution)/shard_map/ppermute | solution.py:410
  45.2 1.2 collective-permute-start.5
  46.4 11.0 %collective-permute-done.1.refs_2_ = bf16[1024,256]{1,0:T(8,128)(2,1)S(1)} collective-permute-done((bf16[1024,256]{1,0:T(8,128)(2,1)S(1)}, bf16[1024,256]{1,0:T(8,128)(2,1)S(1)}, u32[]{:S(2)}, u32[]{:S(2)}) %collective-permute-start.1) | collective-permute-done | bytes 524320 | tf_op jit(solution)/shard_map/ppermute | solution.py:410
  57.5 1.9 collective-permute-start.7
  59.4 8.3 %collective-permute-done.3.refs_5_ = bf16[1024,256]{1,0:T(8,128)(2,1)S(1)} collective-permute-done((bf16[1024,256]{1,0:T(8,128)(2,1)S(1)}, bf16[1024,256]{1,0:T(8,128)(2,1)S(1)}, u32[]{:S(2)}, u32[]{:S(2)}) %collective-permute-start.3) | collective-permute-done | bytes 524320 | tf_op jit(solution)/shard_map/ppermute | solution.py:410
  67.7 1.4 collective-permute-start.8
  69.1 11.0 %collective-permute-done.4.refs_6_ = bf16[1024,256]{1,0:T(8,128)(2,1)} collective-permute-done((bf16[1024,256]{1,0:T(8,128)(2,1)S(1)}, bf16[1024,256]{1,0:T(8,128)(2,1)}, u32[]{:S(2)}, u32[]{:S(2)}) %collective-permute-start.4) | collective-permute-done | bytes 524320 | tf_op jit(solution)/shard_map/ppermute | solution.py:410
  80.0 10.2 %collective-permute-done.6.refs_9_ = bf16[64,4096]{1,0:T(8,128)(2,1)} collective-permute-done((bf16[64,4096]{1,0:T(8,128)(2,1)}, bf16[64,4096]{1,0:T(8,128)(2,1)}, u32[]{:S(2)}, u32[]{:S(2)}) %collective-permute-start.6) | collective-permute-done | bytes 524320 | tf_op jit(solution)/shard_map/ppermute | solution.py:410
  90.2 12.2 %collective-permute-done.7.refs_10_ = bf16[64,4096]{1,0:T(8,128)(2,1)S(1)} collective-permute-done((bf16[64,4096]{1,0:T(8,128)(2,1)}, bf16[64,4096]{1,0:T(8,128)(2,1)S(1)}, u32[]{:S(2)}, u32[]{:S(2)}) %collective-permute-start.7) | collective-permute-done | bytes 524320 | tf_op jit(solution)/shard_map/ppermute | solution.py:410
  103.2 6.5 %stack.1.w_ref = bf16[6144,512]{1,0:T(8,128)(2,1)} custom-call(s32[1]{0:T(128)} %bitcast.2.at_ref.t_ref, bf16[1024,256]{1,0:T(8,128)(2,1)} %bitcast.9, bf16[1024,256]{1,0:T(8,128)(2,1)} %copy-done.5, bf16[1024,256]{1,0:T(8,128)(2,1)} %copy-done.6, bf16[1024,256]{1,0:T(8,128)(2,1)} %copy-done.7, bf16[1024,256]{1,0:T(8,128)(2,1)} %bitcast.13, ...), custom_call_target="tpu_custom_call" | custom-call | flops 3145728 | bytes 12582912 | tf_op jit(solution)/shard_map/stack/pallas_call | solution.py:118
  109.7 19.5 %all-to-all-done.recv_ref = bf16[32,8,4096]{2,1,0:T(8,128)(2,1)S(1)} async-done(((bf16[32,8,4096]{2,1,0:T(8,128)(2,1)}), bf16[32,8,4096]{2,1,0:T(8,128)(2,1)S(1)}, u32[]{:S(2)}, u32[]{:S(2)}) %all-to-all-start) | async-done | bytes 2097184 | tf_op jit(solution)/shard_map/all_to_all | solution.py:418
  129.2 6.5 %expert_round.1 = (bf16[32,8,2048]{2,1,0:T(8,128)(2,1)}, bf16[128,768]{1,0:T(8,128)(2,1)S(1)}) custom-call(bf16[32,8,4096]{2,1,0:T(8,128)(2,1)S(1)} %all-to-all-done.recv_ref, bf16[6144,512]{1,0:T(8,128)(2,1)} %stack.1.w_ref, bf16[32,8,2048]{2,1,0:T(8,128)(2,1)} %get-tuple-element.23.spare_ref), custom_call_target="tpu_custom_call", output_to_operand_aliasing={{0}: (2, {})} | custom-call | flops 1342177280 | bytes 9437184 | tf_op jit(solution)/shard_map/expert_round/pallas_call | solution.py:216
  135.7 5.3 %all-to-all-start.1 = ((bf16[32,8,2048]{2,1,0:T(8,128)(2,1)}), bf16[32,8,2048]{2,1,0:T(8,128)(2,1)S(1)}, u32[]{:S(2)}, u32[]{:S(2)}) async-start(bf16[32,8,2048]{2,1,0:T(8,128)(2,1)} %get-tuple-element.24), calls=%async_computation.1 | async-start | bytes 2097152 | tf_op jit(solution)/shard_map/all_to_all | solution.py:423
  141.9 1.5 collective-permute-start.12
  143.4 1.9 shard_map.102
  146.0 2.7 %collective-permute-start.10 = (bf16[192,1024]{1,0:T(8,128)(2,1)}, bf16[192,1024]{1,0:T(8,128)(2,1)S(1)}, u32[]{:S(2)}, u32[]{:S(2)}) collective-permute-start(bf16[192,1024]{1,0:T(8,128)(2,1)} %get-tuple-element.28), channel_id=1, source_target_pairs={{0,2},{1,3},{2,0},{3,1},{4,6},{5,7},{6,4},{7,5},{8,10},{9,11},{10,... | collective-permute-start | bytes 1179656 | tf_op jit(solution)/shard_map/ppermute | solution.py:410
  149.0 1.6 collective-permute-start.14
  150.5 1.4 collective-permute-start.11
  152.2 16.4 %collective-permute-done.13.refs_2_ = bf16[160,1024]{1,0:T(8,128)(2,1)S(1)} collective-permute-done((bf16[160,1024]{1,0:T(8,128)(2,1)S(1)}, bf16[160,1024]{1,0:T(8,128)(2,1)S(1)}, u32[]{:S(2)}, u32[]{:S(2)}) %collective-permute-start.13) | collective-permute-done | bytes 327712 | tf_op jit(solution)/shard_map/ppermute | solution.py:410
  168.6 2.3 %collective-permute-done.14.refs_3_ = bf16[160,1024]{1,0:T(8,128)(2,1)S(1)} collective-permute-done((bf16[160,1024]{1,0:T(8,128)(2,1)S(1)}, bf16[160,1024]{1,0:T(8,128)(2,1)S(1)}, u32[]{:S(2)}, u32[]{:S(2)}) %collective-permute-start.14) | collective-permute-done | bytes 327712 | tf_op jit(solution)/shard_map/ppermute | solution.py:410
  171.7 2.6 %grads_down.1 = (bf16[64,1024]{1,0:T(8,128)(2,1)}, bf16[64,1024]{1,0:T(8,128)(2,1)}, bf16[64,1024]{1,0:T(8,128)(2,1)}, bf16[64,1024]{1,0:T(8,128)(2,1)}) custom-call(s32[1]{0:T(128)} %bitcast.2.at_ref.t_ref, bf16[160,1024]{1,0:T(8,128)(2,1)} %copy-done, bf16[160,1024]{1,0:T(8,128)(2,1)} %copy-done.10, bf16[160,1024]{1,0:T(8,128)(2,1)} %copy-done.11, ...), custom_call_target="tpu_custom_call" | custom-call | flops 268435456 | bytes 2097152 | tf_op jit(solution)/shard_map/grads_down/pallas_call | solution.py:304
  174.3 3.2 %collective-permute-start.15 = (bf16[64,1024]{1,0:T(8,128)(2,1)}, bf16[64,1024]{1,0:T(8,128)(2,1)S(1)}, u32[]{:S(2)}, u32[]{:S(2)}) collective-permute-start(bf16[64,1024]{1,0:T(8,128)(2,1)} %get-tuple-element.37), channel_id=1, source_target_pairs={{0,1},{1,2},{2,3},{3,0},{4,5},{5,6},{6,7},{7,4},{8,9},{9,10},{10,1... | collective-permute-start | bytes 393224 | tf_op jit(solution)/shard_map/ppermute | solution.py:410
  177.4 1.4 collective-permute-start.16
  180.6 1.6 pick.1.pick_ref
  183.0 3.1 %grads_up.1 = (bf16[1024,256]{1,0:T(8,128)(2,1)}, bf16[1024,256]{1,0:T(8,128)(2,1)}) custom-call(bf16[192,1024]{1,0:T(8,128)(2,1)} %copy-done.2, bf16[192,1024]{1,0:T(8,128)(2,1)} %copy-done.19, bf16[192,1024]{1,0:T(8,128)(2,1)} %copy-done.17, bf16[192,1024]{1,0:T(8,128)(2,1)} %copy-done.18), custom_call_target="tpu_custom_call" | custom-call | flops 536870912 | bytes 3145728 | tf_op jit(solution)/shard_map/grads_up/pallas_call | solution.py:318
  186.9 1.9 place.1
  188.8 7.7 %all-to-all-done.1.ret_ref = bf16[32,8,2048]{2,1,0:T(8,128)(2,1)S(1)} async-done(((bf16[32,8,2048]{2,1,0:T(8,128)(2,1)}), bf16[32,8,2048]{2,1,0:T(8,128)(2,1)S(1)}, u32[]{:S(2)}, u32[]{:S(2)}) %all-to-all-start.1) | async-done | bytes 1048608 | tf_op jit(solution)/shard_map/all_to_all | solution.py:423
  196.5 1.7 combine.1
  (59 shorter events, 9.2 us)
Async XLA Ops:
  5.0 25.6 %copy-start.3 = (bf16[1,1024,256]{2,1,0:T(8,128)(2,1)S(1)}, bf16[1,1024,256]{2,1,0:T(8,128)(2,1)}, u32[]{:S(2)}) copy-start(bf16[1,1024,256]{2,1,0:T(8,128)(2,1)} %param.11) | copy-start | bytes 1572868
  5.0 30.8 %copy-start.4 = (bf16[1,1024,256]{2,1,0:T(8,128)(2,1)S(1)}, bf16[1,1024,256]{2,1,0:T(8,128)(2,1)}, u32[]{:S(2)}) copy-start(bf16[1,1024,256]{2,1,0:T(8,128)(2,1)} %param.12) | copy-start | bytes 1572868
  5.0 124.2 %all-to-all-start = ((bf16[32,8,4096]{2,1,0:T(8,128)(2,1)}), bf16[32,8,4096]{2,1,0:T(8,128)(2,1)S(1)}, u32[]{:S(2)}, u32[]{:S(2)}) async-start(bf16[32,8,4096]{2,1,0:T(8,128)(2,1)} %get-tuple-element.22), calls=%async_computation | async-start | bytes 4194304 | tf_op jit(solution)/shard_map/all_to_all | solution.py:418
  30.6 14.6 %collective-permute-start = (bf16[1024,256]{1,0:T(8,128)(2,1)S(1)}, bf16[1024,256]{1,0:T(8,128)(2,1)S(1)}, u32[]{:S(2)}, u32[]{:S(2)}) collective-permute-start(bf16[1024,256]{1,0:T(8,128)(2,1)S(1)} %bitcast.10), channel_id=1, source_target_pairs={{0,1},{1,2},{2,3},{3,0},{4,5},{5,6},{6,7},{7,4},{8,9},{9,10},{10,1... | collective-permute-start | bytes 1572872 | tf_op jit(solution)/shard_map/ppermute | solution.py:410
  32.1 25.3 %collective-permute-start.1 = (bf16[1024,256]{1,0:T(8,128)(2,1)S(1)}, bf16[1024,256]{1,0:T(8,128)(2,1)S(1)}, u32[]{:S(2)}, u32[]{:S(2)}) collective-permute-start(bf16[1024,256]{1,0:T(8,128)(2,1)S(1)} %bitcast.11), channel_id=1, source_target_pairs={{0,2},{1,3},{2,0},{3,1},{4,6},{5,7},{6,4},{7,5},{8,10},{9,11},{10,... | collective-permute-start | bytes 1572872 | tf_op jit(solution)/shard_map/ppermute | solution.py:410
  34.8 22.7 %collective-permute-start.2 = (bf16[1024,256]{1,0:T(8,128)(2,1)S(1)}, bf16[1024,256]{1,0:T(8,128)(2,1)S(1)}, u32[]{:S(2)}, u32[]{:S(2)}) collective-permute-start(bf16[1024,256]{1,0:T(8,128)(2,1)S(1)} %bitcast.12), channel_id=1, source_target_pairs={{0,3},{1,0},{2,1},{3,2},{4,7},{5,4},{6,5},{7,6},{8,11},{9,8},{10,9... | collective-permute-start | bytes 1572872 | tf_op jit(solution)/shard_map/ppermute | solution.py:410
  35.8 31.8 %collective-permute-start.3 = (bf16[1024,256]{1,0:T(8,128)(2,1)S(1)}, bf16[1024,256]{1,0:T(8,128)(2,1)S(1)}, u32[]{:S(2)}, u32[]{:S(2)}) collective-permute-start(bf16[1024,256]{1,0:T(8,128)(2,1)S(1)} %bitcast.14), channel_id=1, source_target_pairs={{0,1},{1,2},{2,3},{3,0},{4,5},{5,6},{6,7},{7,4},{8,9},{9,10},{10,1... | collective-permute-start | bytes 1572872 | tf_op jit(solution)/shard_map/ppermute | solution.py:410
  36.3 43.7 %collective-permute-start.4 = (bf16[1024,256]{1,0:T(8,128)(2,1)S(1)}, bf16[1024,256]{1,0:T(8,128)(2,1)}, u32[]{:S(2)}, u32[]{:S(2)}) collective-permute-start(bf16[1024,256]{1,0:T(8,128)(2,1)S(1)} %bitcast.15), channel_id=1, source_target_pairs={{0,2},{1,3},{2,0},{3,1},{4,6},{5,7},{6,4},{7,5},{8,10},{9,11},{10,... | collective-permute-start | bytes 1572872 | tf_op jit(solution)/shard_map/ppermute | solution.py:410
  45.2 22.5 %copy-start.5 = (bf16[1024,256]{1,0:T(8,128)(2,1)}, bf16[1024,256]{1,0:T(8,128)(2,1)S(1)}, u32[]{:S(2)}) copy-start(bf16[1024,256]{1,0:T(8,128)(2,1)S(1)} %collective-permute-done.refs_1_) | copy-start | bytes 1572868
  45.2 34.8 %collective-permute-start.5 = (bf16[1024,256]{1,0:T(8,128)(2,1)S(1)}, bf16[1024,256]{1,0:T(8,128)(2,1)}, u32[]{:S(2)}, u32[]{:S(2)}) collective-permute-start(bf16[1024,256]{1,0:T(8,128)(2,1)S(1)} %bitcast.16), channel_id=1, source_target_pairs={{0,3},{1,0},{2,1},{3,2},{4,7},{5,4},{6,5},{7,6},{8,11},{9,8},{10,9... | collective-permute-start | bytes 1572872 | tf_op jit(solution)/shard_map/ppermute | solution.py:410
  57.4 11.6 %copy-start.6 = (bf16[1024,256]{1,0:T(8,128)(2,1)}, bf16[1024,256]{1,0:T(8,128)(2,1)S(1)}, u32[]{:S(2)}) copy-start(bf16[1024,256]{1,0:T(8,128)(2,1)S(1)} %collective-permute-done.1.refs_2_) | copy-start | bytes 1572868
  57.4 32.8 %collective-permute-start.6 = (bf16[64,4096]{1,0:T(8,128)(2,1)}, bf16[64,4096]{1,0:T(8,128)(2,1)}, u32[]{:S(2)}, u32[]{:S(2)}) collective-permute-start(bf16[64,4096]{1,0:T(8,128)(2,1)} %bitcast.17), channel_id=1, source_target_pairs={{0,1},{1,2},{2,3},{3,0},{4,5},{5,6},{6,7},{7,4},{8,9},{9,10},{10,1... | collective-permute-start | bytes 1572872 | tf_op jit(solution)/shard_map/ppermute | solution.py:410
  57.5 11.6 %copy-start.7 = (bf16[1024,256]{1,0:T(8,128)(2,1)}, bf16[1024,256]{1,0:T(8,128)(2,1)S(1)}, u32[]{:S(2)}) copy-start(bf16[1024,256]{1,0:T(8,128)(2,1)S(1)} %collective-permute-done.2.refs_3_) | copy-start | bytes 1572868
  57.5 44.9 %collective-permute-start.7 = (bf16[64,4096]{1,0:T(8,128)(2,1)}, bf16[64,4096]{1,0:T(8,128)(2,1)S(1)}, u32[]{:S(2)}, u32[]{:S(2)}) collective-permute-start(bf16[64,4096]{1,0:T(8,128)(2,1)} %bitcast.18), channel_id=1, source_target_pairs={{0,2},{1,3},{2,0},{3,1},{4,6},{5,7},{6,4},{7,5},{8,10},{9,11},{10,... | collective-permute-start | bytes 1572872 | tf_op jit(solution)/shard_map/ppermute | solution.py:410
  67.7 1.4 copy-start.8
  67.7 34.7 %collective-permute-start.8 = (bf16[64,4096]{1,0:T(8,128)(2,1)}, bf16[64,4096]{1,0:T(8,128)(2,1)}, u32[]{:S(2)}, u32[]{:S(2)}) collective-permute-start(bf16[64,4096]{1,0:T(8,128)(2,1)} %bitcast.19), channel_id=1, source_target_pairs={{0,3},{1,0},{2,1},{3,2},{4,7},{5,4},{6,5},{7,6},{8,11},{9,8},{10,9... | collective-permute-start | bytes 1572872 | tf_op jit(solution)/shard_map/ppermute | solution.py:410
  135.7 60.8 %all-to-all-start.1 = ((bf16[32,8,2048]{2,1,0:T(8,128)(2,1)}), bf16[32,8,2048]{2,1,0:T(8,128)(2,1)S(1)}, u32[]{:S(2)}, u32[]{:S(2)}) async-start(bf16[32,8,2048]{2,1,0:T(8,128)(2,1)} %get-tuple-element.24), calls=%async_computation.1 | async-start | bytes 2097152 | tf_op jit(solution)/shard_map/all_to_all | solution.py:423
  141.9 3.4 %copy-start = (bf16[160,1024]{1,0:T(8,128)(2,1)}, bf16[160,1024]{1,0:T(8,128)(2,1)S(1)}, u32[]{:S(2)}) copy-start(bf16[160,1024]{1,0:T(8,128)(2,1)S(1)} %get-tuple-element.32.refs_0_) | copy-start | bytes 983044
  141.9 38.0 %copy-start.16 = (s32[64,2]{0,1:T(2,128)S(1)}, s32[64,2]{0,1:T(2,128)}, u32[]{:S(2)}) copy-start(s32[64,2]{0,1:T(2,128)} %param.9) | copy-start | bytes 1540
  141.9 10.3 %collective-permute-start.12 = (bf16[160,1024]{1,0:T(8,128)(2,1)S(1)}, bf16[160,1024]{1,0:T(8,128)(2,1)S(1)}, u32[]{:S(2)}, u32[]{:S(2)}) collective-permute-start(bf16[160,1024]{1,0:T(8,128)(2,1)S(1)} %get-tuple-element.33), channel_id=1, source_target_pairs={{0,1},{1,2},{2,3},{3,0},{4,5},{5,6},{6,7},{7,4},{8,9},{9,10},{10,1... | collective-permute-start | bytes 983048 | tf_op jit(solution)/shard_map/ppermute | solution.py:410
  146.0 32.9 %collective-permute-start.10 = (bf16[192,1024]{1,0:T(8,128)(2,1)}, bf16[192,1024]{1,0:T(8,128)(2,1)S(1)}, u32[]{:S(2)}, u32[]{:S(2)}) collective-permute-start(bf16[192,1024]{1,0:T(8,128)(2,1)} %get-tuple-element.28), channel_id=1, source_target_pairs={{0,2},{1,3},{2,0},{3,1},{4,6},{5,7},{6,4},{7,5},{8,10},{9,11},{10,... | collective-permute-start | bytes 1179656 | tf_op jit(solution)/shard_map/ppermute | solution.py:410
  148.7 19.9 %collective-permute-start.13 = (bf16[160,1024]{1,0:T(8,128)(2,1)S(1)}, bf16[160,1024]{1,0:T(8,128)(2,1)S(1)}, u32[]{:S(2)}, u32[]{:S(2)}) collective-permute-start(bf16[160,1024]{1,0:T(8,128)(2,1)S(1)} %get-tuple-element.34), channel_id=1, source_target_pairs={{0,2},{1,3},{2,0},{3,1},{4,6},{5,7},{6,4},{7,5},{8,10},{9,11},{10,... | collective-permute-start | bytes 983048 | tf_op jit(solution)/shard_map/ppermute | solution.py:410
  149.0 22.0 %collective-permute-start.14 = (bf16[160,1024]{1,0:T(8,128)(2,1)S(1)}, bf16[160,1024]{1,0:T(8,128)(2,1)S(1)}, u32[]{:S(2)}, u32[]{:S(2)}) collective-permute-start(bf16[160,1024]{1,0:T(8,128)(2,1)S(1)} %get-tuple-element.35), channel_id=1, source_target_pairs={{0,3},{1,0},{2,1},{3,2},{4,7},{5,4},{6,5},{7,6},{8,11},{9,8},{10,9... | collective-permute-start | bytes 983048 | tf_op jit(solution)/shard_map/ppermute | solution.py:410
  150.5 31.6 %collective-permute-start.11 = (bf16[192,1024]{1,0:T(8,128)(2,1)}, bf16[192,1024]{1,0:T(8,128)(2,1)S(1)}, u32[]{:S(2)}, u32[]{:S(2)}) collective-permute-start(bf16[192,1024]{1,0:T(8,128)(2,1)} %get-tuple-element.29), channel_id=1, source_target_pairs={{0,3},{1,0},{2,1},{3,2},{4,7},{5,4},{6,5},{7,6},{8,11},{9,8},{10,9... | collective-permute-start | bytes 1179656 | tf_op jit(solution)/shard_map/ppermute | solution.py:410
  152.2 18.8 %copy-start.10 = (bf16[160,1024]{1,0:T(8,128)(2,1)}, bf16[160,1024]{1,0:T(8,128)(2,1)S(1)}, u32[]{:S(2)}) copy-start(bf16[160,1024]{1,0:T(8,128)(2,1)S(1)} %collective-permute-done.12.refs_1_) | copy-start | bytes 983044
  152.2 30.0 %collective-permute-start.9 = (bf16[192,1024]{1,0:T(8,128)(2,1)}, bf16[192,1024]{1,0:T(8,128)(2,1)S(1)}, u32[]{:S(2)}, u32[]{:S(2)}) collective-permute-start(bf16[192,1024]{1,0:T(8,128)(2,1)} %get-tuple-element.27), channel_id=1, source_target_pairs={{0,1},{1,2},{2,3},{3,0},{4,5},{5,6},{6,7},{7,4},{8,9},{9,10},{10,1... | collective-permute-start | bytes 1179656 | tf_op jit(solution)/shard_map/ppermute | solution.py:410
  168.6 2.4 %copy-start.11 = (bf16[160,1024]{1,0:T(8,128)(2,1)}, bf16[160,1024]{1,0:T(8,128)(2,1)S(1)}, u32[]{:S(2)}) copy-start(bf16[160,1024]{1,0:T(8,128)(2,1)S(1)} %collective-permute-done.13.refs_2_) | copy-start | bytes 983044
  174.3 11.9 %collective-permute-start.15 = (bf16[64,1024]{1,0:T(8,128)(2,1)}, bf16[64,1024]{1,0:T(8,128)(2,1)S(1)}, u32[]{:S(2)}, u32[]{:S(2)}) collective-permute-start(bf16[64,1024]{1,0:T(8,128)(2,1)} %get-tuple-element.37), channel_id=1, source_target_pairs={{0,1},{1,2},{2,3},{3,0},{4,5},{5,6},{6,7},{7,4},{8,9},{9,10},{10,1... | collective-permute-start | bytes 393224 | tf_op jit(solution)/shard_map/ppermute | solution.py:410
  177.4 8.7 %collective-permute-start.16 = (bf16[64,1024]{1,0:T(8,128)(2,1)}, bf16[64,1024]{1,0:T(8,128)(2,1)S(1)}, u32[]{:S(2)}, u32[]{:S(2)}) collective-permute-start(bf16[64,1024]{1,0:T(8,128)(2,1)} %get-tuple-element.38), channel_id=1, source_target_pairs={{0,2},{1,3},{2,0},{3,1},{4,6},{5,7},{6,4},{7,5},{8,10},{9,11},{10,... | collective-permute-start | bytes 393224 | tf_op jit(solution)/shard_map/ppermute | solution.py:410
  178.9 3.3 %copy-start.17 = (bf16[192,1024]{1,0:T(8,128)(2,1)}, bf16[192,1024]{1,0:T(8,128)(2,1)S(1)}, u32[]{:S(2)}) copy-start(bf16[192,1024]{1,0:T(8,128)(2,1)S(1)} %collective-permute-done.10.refs_2_) | copy-start | bytes 1179652
  178.9 7.3 %collective-permute-start.17 = (bf16[64,1024]{1,0:T(8,128)(2,1)}, bf16[64,1024]{1,0:T(8,128)(2,1)S(1)}, u32[]{:S(2)}, u32[]{:S(2)}) collective-permute-start(bf16[64,1024]{1,0:T(8,128)(2,1)} %get-tuple-element.39), channel_id=1, source_target_pairs={{0,3},{1,0},{2,1},{3,2},{4,7},{5,4},{6,5},{7,6},{8,11},{9,8},{10,9... | collective-permute-start | bytes 393224 | tf_op jit(solution)/shard_map/ppermute | solution.py:410
  182.2 14.3 %copy-start.1 = (bf16[64,128]{1,0:T(8,128)(2,1)S(1)}, bf16[64,128]{1,0:T(8,128)(2,1)}, u32[]{:S(2)}) copy-start(bf16[64,128]{1,0:T(8,128)(2,1)} %pick.1.pick_ref) | copy-start | bytes 49156
  (8 other events, 6.0 us)
